TPU v7x, 32 devices: a whole 2x2x4 slice. The times are simulated.
32 devices in a mesh: grp: 2 (over y), row: 16 (over z, x, core).
Axes of the slice: x: 2, y: 2, z: 4, core: 2. Of those that a mesh axis runs over, the one named last changes fastest.
Arguments:
- diag_blocks: float32 [8192, 512], P('row'), may hold values from -0.6 to 2.6
- lower_coupling: float32 [8192, 64], P('row'), may hold values from -0.3125 to 0.3125
- upper_coupling: float32 [8192, 64], P('row'), may hold values from -0.3125 to 0.3125
- right_sides: float32 [8192, 1024], P('row', 'grp'), parts along dimension 1, may hold values from -108 to 108
Outputs:
- solution: float32 [8192, 1024], P('row', 'grp'), parts along dimension 1
- res_norms: float32 [8, 1024], P(None, 'grp'), parts along dimension 1
There are 2 independent parts, one for each index of `grp`. A program takes and returns all parts, laid end to end along the dimension named above; an argument that names none is the same for every part. Nothing has to cross between parts.
All inputs are finite; a program needn't handle non-finite values.
Results may differ from a plain program's by a relative error of at most 0.0001.
Values sent between devices are 32-bit elements; how exact they have to be, the bound alone decides.
No kernel may reach another device: no remote copies, remote signals or barrier semaphores. Data moves between devices by JAX's collectives and lax.ppermute only.
A program may use at most 64 MiB of HBM per device.

v0:
```python
import jax
import jax.numpy as jnp
from jax import lax
from jax.sharding import PartitionSpec as P

SWEEPS = 8


def extended(shard, sides, width):
    for axis, dim in sides:
        size, length = (lax.axis_size(axis), shard.shape[dim])
        up = [(i, (i + 1) % size) for i in range(size - 1)]
        down = [(j, i) for i, j in up]
        last = lax.slice_in_dim(shard, length - width, length, axis=dim)
        first = lax.slice_in_dim(shard, 0, width, axis=dim)
        before = lax.ppermute(last, axis, up)
        after = lax.ppermute(first, axis, down)
        shard = jnp.concatenate([before, shard, after], axis=dim)
    return shard


def matmul(left, right):
    return jnp.dot(left, right, precision=lax.Precision.HIGHEST, preferred_element_type=jnp.float32)


def local(diag_blocks, lower_coupling, upper_coupling, right_sides):
    pivots = jnp.diagonal(diag_blocks)[:, None]
    width = lower_coupling.shape[1]
    solution = jnp.zeros_like(right_sides)
    partials = []
    for sweep_index in range(SWEEPS):
        padded = extended(solution, (("row", 0),), width)
        before = padded[:width]
        after = padded[padded.shape[0] - width :]
        images = (
            matmul(diag_blocks, solution)
            + matmul(lower_coupling, before)
            + matmul(upper_coupling, after)
        )
        residual = right_sides - images
        local_sums = jnp.sum(residual * residual, axis=0)
        solution = solution + residual / pivots
        partials.append(local_sums)
    res_norms = jnp.sqrt(lax.psum(jnp.stack(partials), "row"))
    return (solution, res_norms)


def solution(mesh):
    return jax.shard_map(
        local,
        mesh=mesh,
        in_specs=(P("row", None), P("row", None), P("row", None), P("row", "grp")),
        out_specs=(P("row", "grp"), P(None, "grp")),
        check_vma=False,
    )
```

profile of v0, /device:TPU:0, one launch (start us, length us, event | category | flops | bytes accessed | tf_op | source)
XLA Modules:
  0.0 163.6 jit_solution(15000186278195526279)
XLA Ops:
  0.7 1.4 collective-permute-start.1
  2.1 3.0 %collective-permute-start = (f32[64,512]{1,0:T(8,128)S(1)}, f32[64,512]{1,0:T(8,128)S(1)}, u32[]{:S(2)}, u32[]{:S(2)}) collective-permute-start(f32[64,512]{1,0:T(8,128)S(1)} %broadcast.16), channel_id=1, source_target_pairs={{0,1},{1,2},{2,3},{3,4},{4,5},{5,6},{6,7},{7,8},{8,9},{9,10},{10,1... | collective-permute-start | bytes 393224 | tf_op jit(solution)/shard_map/ppermute | solution.py:16
  5.2 8.5 %gather_fusion = f32[512]{0:T(512)S(1)} fusion(f32[512,512]{1,0:T(8,128)} %param.4, s32[512]{0:T(512)S(1)} %bitcast.87), kind=kCustom, calls=%fused_computation | custom fusion | bytes 8192 | tf_op jit(solution)/shard_map/jit(diagonal)/cond/branch_0_fun/gather | solution.py:27
  16.1 4.5 %collective-permute-start.2 = (f32[64,512]{1,0:T(8,128)S(1)}, f32[64,512]{1,0:T(8,128)S(1)}, u32[]{:S(2)}, u32[]{:S(2)}) collective-permute-start(f32[64,512]{1,0:T(8,128)S(1)} %get-tuple-element.31), channel_id=1, source_target_pairs={{0,1},{1,2},{2,3},{3,4},{4,5},{5,6},{6,7},{7,8},{8,9},{9,10},{10,1... | collective-permute-start | bytes 393224 | tf_op jit(solution)/shard_map/ppermute | solution.py:16
  20.6 1.9 %fusion.25 = f32[512,512]{0,1:T(8,128)S(1)} fusion(f32[512,512]{1,0:T(8,128)S(1)} %get-tuple-element.17, f32[512,512]{1,0:T(8,128)S(1)} %copy-done.1), kind=kOutput, calls=%fused_computation.59 | convolution fusion | flops 1610612736 | bytes 3145728 | tf_op jit(solution)/shard_map/dot_general | solution.py:23
  22.5 1.3 collective-permute-start.3
  27.0 5.7 %collective-permute-start.4 = (f32[64,512]{1,0:T(8,128)S(1)}, f32[64,512]{1,0:T(8,128)S(1)}, u32[]{:S(2)}, u32[]{:S(2)}) collective-permute-start(f32[64,512]{1,0:T(8,128)S(1)} %get-tuple-element.29), channel_id=1, source_target_pairs={{0,1},{1,2},{2,3},{3,4},{4,5},{5,6},{6,7},{7,8},{8,9},{9,10},{10,1... | collective-permute-start | bytes 393224 | tf_op jit(solution)/shard_map/ppermute | solution.py:16
  32.7 1.9 %fusion.26 = f32[512,512]{0,1:T(8,128)S(1)} fusion(f32[512,512]{1,0:T(8,128)S(1)} %get-tuple-element.15, f32[512,512]{1,0:T(8,128)S(1)} %copy-done.1), kind=kOutput, calls=%fused_computation.60 | convolution fusion | flops 1610612736 | bytes 3145728 | tf_op jit(solution)/shard_map/dot_general | solution.py:23
  34.6 1.3 collective-permute-start.5
  39.0 6.0 %collective-permute-start.6 = (f32[64,512]{1,0:T(8,128)S(1)}, f32[64,512]{1,0:T(8,128)S(1)}, u32[]{:S(2)}, u32[]{:S(2)}) collective-permute-start(f32[64,512]{1,0:T(8,128)S(1)} %get-tuple-element.27), channel_id=1, source_target_pairs={{0,1},{1,2},{2,3},{3,4},{4,5},{5,6},{6,7},{7,8},{8,9},{9,10},{10,1... | collective-permute-start | bytes 393224 | tf_op jit(solution)/shard_map/ppermute | solution.py:16
  45.1 1.9 %fusion.27 = f32[512,512]{0,1:T(8,128)S(1)} fusion(f32[512,512]{1,0:T(8,128)S(1)} %get-tuple-element.13, f32[512,512]{1,0:T(8,128)S(1)} %copy-done.1), kind=kOutput, calls=%fused_computation.61 | convolution fusion | flops 1610612736 | bytes 3145728 | tf_op jit(solution)/shard_map/dot_general | solution.py:23
  47.0 1.3 collective-permute-start.7
  51.4 5.9 %collective-permute-start.8 = (f32[64,512]{1,0:T(8,128)S(1)}, f32[64,512]{1,0:T(8,128)S(1)}, u32[]{:S(2)}, u32[]{:S(2)}) collective-permute-start(f32[64,512]{1,0:T(8,128)S(1)} %get-tuple-element.25), channel_id=1, source_target_pairs={{0,1},{1,2},{2,3},{3,4},{4,5},{5,6},{6,7},{7,8},{8,9},{9,10},{10,1... | collective-permute-start | bytes 393224 | tf_op jit(solution)/shard_map/ppermute | solution.py:16
  57.3 1.9 %fusion.28 = f32[512,512]{0,1:T(8,128)S(1)} fusion(f32[512,512]{1,0:T(8,128)S(1)} %get-tuple-element.11, f32[512,512]{1,0:T(8,128)S(1)} %copy-done.1), kind=kOutput, calls=%fused_computation.62 | convolution fusion | flops 1610612736 | bytes 3145728 | tf_op jit(solution)/shard_map/dot_general | solution.py:23
  59.2 1.3 collective-permute-start.9
  63.6 5.9 %collective-permute-start.10 = (f32[64,512]{1,0:T(8,128)S(1)}, f32[64,512]{1,0:T(8,128)S(1)}, u32[]{:S(2)}, u32[]{:S(2)}) collective-permute-start(f32[64,512]{1,0:T(8,128)S(1)} %get-tuple-element.23), channel_id=1, source_target_pairs={{0,1},{1,2},{2,3},{3,4},{4,5},{5,6},{6,7},{7,8},{8,9},{9,10},{10,1... | collective-permute-start | bytes 393224 | tf_op jit(solution)/shard_map/ppermute | solution.py:16
  69.5 1.9 %fusion.29 = f32[512,512]{0,1:T(8,128)S(1)} fusion(f32[512,512]{1,0:T(8,128)S(1)} %get-tuple-element.9, f32[512,512]{1,0:T(8,128)S(1)} %copy-done.1), kind=kOutput, calls=%fused_computation.63 | convolution fusion | flops 1610612736 | bytes 3145728 | tf_op jit(solution)/shard_map/dot_general | solution.py:23
  71.4 1.3 collective-permute-start.11
  75.9 6.1 %collective-permute-start.12 = (f32[64,512]{1,0:T(8,128)S(1)}, f32[64,512]{1,0:T(8,128)S(1)}, u32[]{:S(2)}, u32[]{:S(2)}) collective-permute-start(f32[64,512]{1,0:T(8,128)S(1)} %get-tuple-element.21), channel_id=1, source_target_pairs={{0,1},{1,2},{2,3},{3,4},{4,5},{5,6},{6,7},{7,8},{8,9},{9,10},{10,1... | collective-permute-start | bytes 393224 | tf_op jit(solution)/shard_map/ppermute | solution.py:16
  82.0 1.9 %fusion.30 = f32[512,512]{0,1:T(8,128)S(1)} fusion(f32[512,512]{1,0:T(8,128)S(1)} %get-tuple-element.7, f32[512,512]{1,0:T(8,128)S(1)} %copy-done.1), kind=kOutput, calls=%fused_computation.64 | convolution fusion | flops 1610612736 | bytes 3145728 | tf_op jit(solution)/shard_map/dot_general | solution.py:23
  88.3 5.9 %collective-permute-start.14 = (f32[64,512]{1,0:T(8,128)S(1)}, f32[64,512]{1,0:T(8,128)S(1)}, u32[]{:S(2)}, u32[]{:S(2)}) collective-permute-start(f32[64,512]{1,0:T(8,128)S(1)} %get-tuple-element.19), channel_id=1, source_target_pairs={{0,1},{1,2},{2,3},{3,4},{4,5},{5,6},{6,7},{7,8},{8,9},{9,10},{10,1... | collective-permute-start | bytes 393224 | tf_op jit(solution)/shard_map/ppermute | solution.py:16
  94.2 1.9 %fusion.31 = f32[512,512]{0,1:T(8,128)S(1)} fusion(f32[512,512]{1,0:T(8,128)S(1)} %get-tuple-element.5, f32[512,512]{1,0:T(8,128)S(1)} %copy-done.1), kind=kOutput, calls=%fused_computation.65 | convolution fusion | flops 1610612736 | bytes 3145728 | tf_op jit(solution)/shard_map/dot_general | solution.py:23
  99.3 2.2 %multiply_reduce_fusion = (f32[512]{0:T(512)S(1)}, f32[512,512]{1,0:T(8,128)}) fusion(f32[512,512]{1,0:T(8,128)S(1)} %get-tuple-element.5, f32[512]{0:T(512)S(1)} %gather_fusion, f32[512,512]{1,0:T(8,128)S(1)} %copy-done.3, f32[512,512]{0,1:T(8,128)S(1)} %convolution_add_fusion.1, f32[64,512]{1,0:T(8,128)S(1)} %collective-permute-done.15, ...), kind=kOutput, calls=%fused_computation.33 | convolution fusion | flops 202898944 | bytes 4460544 | tf_op jit(solution)/shard_map/dot_general | solution.py:23
  101.5 61.5 %psum.7 = f32[8,512]{1,0:T(8,128)S(1)} all-reduce(f32[8,512]{1,0:T(8,128)S(1)} %stack.35), channel_id=1, replica_groups=mesh['grp'=2,'row'=16] {'row'}, use_global_device_ids=true, to_apply=%region_9.10 | all-reduce | flops 4096 | bytes 32768 | tf_op jit(solution)/shard_map/psum | solution.py:44
  (53 shorter events, 26.5 us)
Async XLA Ops:
  0.6 13.2 %copy-start = (f32[512,64]{0,1:T(8,128)S(1)}, f32[512,64]{0,1:T(8,128)}, u32[]{:S(2)}) copy-start(f32[512,64]{0,1:T(8,128)} %param.6) | copy-start | bytes 393220
  0.7 13.2 %collective-permute-start.1 = (f32[64,512]{1,0:T(8,128)S(1)}, f32[64,512]{1,0:T(8,128)S(1)}, u32[]{:S(2)}, u32[]{:S(2)}) collective-permute-start(f32[64,512]{1,0:T(8,128)S(1)} %broadcast.16), channel_id=1, source_target_pairs={{1,0},{2,1},{3,2},{4,3},{5,4},{6,5},{7,6},{8,7},{9,8},{10,9},{11,1... | collective-permute-start | bytes 393224 | tf_op jit(solution)/shard_map/ppermute | solution.py:17
  2.1 12.8 %collective-permute-start = (f32[64,512]{1,0:T(8,128)S(1)}, f32[64,512]{1,0:T(8,128)S(1)}, u32[]{:S(2)}, u32[]{:S(2)}) collective-permute-start(f32[64,512]{1,0:T(8,128)S(1)} %broadcast.16), channel_id=1, source_target_pairs={{0,1},{1,2},{2,3},{3,4},{4,5},{5,6},{6,7},{7,8},{8,9},{9,10},{10,1... | collective-permute-start | bytes 393224 | tf_op jit(solution)/shard_map/ppermute | solution.py:16
  5.2 8.5 %copy-start.1 = (f32[512,512]{1,0:T(8,128)S(1)}, f32[512,512]{1,0:T(8,128)}, u32[]{:S(2)}) copy-start(f32[512,512]{1,0:T(8,128)} %param.4) | copy-start | bytes 3145732
  13.6 1.2 copy-start.3
  13.8 1.1 copy-start.2
  16.1 7.7 %collective-permute-start.2 = (f32[64,512]{1,0:T(8,128)S(1)}, f32[64,512]{1,0:T(8,128)S(1)}, u32[]{:S(2)}, u32[]{:S(2)}) collective-permute-start(f32[64,512]{1,0:T(8,128)S(1)} %get-tuple-element.31), channel_id=1, source_target_pairs={{0,1},{1,2},{2,3},{3,4},{4,5},{5,6},{6,7},{7,8},{8,9},{9,10},{10,1... | collective-permute-start | bytes 393224 | tf_op jit(solution)/shard_map/ppermute | solution.py:16
  22.5 3.2 %collective-permute-start.3 = (f32[64,512]{1,0:T(8,128)S(1)}, f32[64,512]{1,0:T(8,128)S(1)}, u32[]{:S(2)}, u32[]{:S(2)}) collective-permute-start(f32[64,512]{1,0:T(8,128)S(1)} %get-tuple-element.30), channel_id=1, source_target_pairs={{1,0},{2,1},{3,2},{4,3},{5,4},{6,5},{7,6},{8,7},{9,8},{10,9},{11,1... | collective-permute-start | bytes 393224 | tf_op jit(solution)/shard_map/ppermute | solution.py:17
  27.0 8.9 %collective-permute-start.4 = (f32[64,512]{1,0:T(8,128)S(1)}, f32[64,512]{1,0:T(8,128)S(1)}, u32[]{:S(2)}, u32[]{:S(2)}) collective-permute-start(f32[64,512]{1,0:T(8,128)S(1)} %get-tuple-element.29), channel_id=1, source_target_pairs={{0,1},{1,2},{2,3},{3,4},{4,5},{5,6},{6,7},{7,8},{8,9},{9,10},{10,1... | collective-permute-start | bytes 393224 | tf_op jit(solution)/shard_map/ppermute | solution.py:16
  34.6 3.2 %collective-permute-start.5 = (f32[64,512]{1,0:T(8,128)S(1)}, f32[64,512]{1,0:T(8,128)S(1)}, u32[]{:S(2)}, u32[]{:S(2)}) collective-permute-start(f32[64,512]{1,0:T(8,128)S(1)} %get-tuple-element.28), channel_id=1, source_target_pairs={{1,0},{2,1},{3,2},{4,3},{5,4},{6,5},{7,6},{8,7},{9,8},{10,9},{11,1... | collective-permute-start | bytes 393224 | tf_op jit(solution)/shard_map/ppermute | solution.py:17
  39.0 9.2 %collective-permute-start.6 = (f32[64,512]{1,0:T(8,128)S(1)}, f32[64,512]{1,0:T(8,128)S(1)}, u32[]{:S(2)}, u32[]{:S(2)}) collective-permute-start(f32[64,512]{1,0:T(8,128)S(1)} %get-tuple-element.27), channel_id=1, source_target_pairs={{0,1},{1,2},{2,3},{3,4},{4,5},{5,6},{6,7},{7,8},{8,9},{9,10},{10,1... | collective-permute-start | bytes 393224 | tf_op jit(solution)/shard_map/ppermute | solution.py:16
  47.0 3.2 %collective-permute-start.7 = (f32[64,512]{1,0:T(8,128)S(1)}, f32[64,512]{1,0:T(8,128)S(1)}, u32[]{:S(2)}, u32[]{:S(2)}) collective-permute-start(f32[64,512]{1,0:T(8,128)S(1)} %get-tuple-element.26), channel_id=1, source_target_pairs={{1,0},{2,1},{3,2},{4,3},{5,4},{6,5},{7,6},{8,7},{9,8},{10,9},{11,1... | collective-permute-start | bytes 393224 | tf_op jit(solution)/shard_map/ppermute | solution.py:17
  51.4 9.1 %collective-permute-start.8 = (f32[64,512]{1,0:T(8,128)S(1)}, f32[64,512]{1,0:T(8,128)S(1)}, u32[]{:S(2)}, u32[]{:S(2)}) collective-permute-start(f32[64,512]{1,0:T(8,128)S(1)} %get-tuple-element.25), channel_id=1, source_target_pairs={{0,1},{1,2},{2,3},{3,4},{4,5},{5,6},{6,7},{7,8},{8,9},{9,10},{10,1... | collective-permute-start | bytes 393224 | tf_op jit(solution)/shard_map/ppermute | solution.py:16
  59.2 3.2 %collective-permute-start.9 = (f32[64,512]{1,0:T(8,128)S(1)}, f32[64,512]{1,0:T(8,128)S(1)}, u32[]{:S(2)}, u32[]{:S(2)}) collective-permute-start(f32[64,512]{1,0:T(8,128)S(1)} %get-tuple-element.24), channel_id=1, source_target_pairs={{1,0},{2,1},{3,2},{4,3},{5,4},{6,5},{7,6},{8,7},{9,8},{10,9},{11,1... | collective-permute-start | bytes 393224 | tf_op jit(solution)/shard_map/ppermute | solution.py:17
  63.6 9.1 %collective-permute-start.10 = (f32[64,512]{1,0:T(8,128)S(1)}, f32[64,512]{1,0:T(8,128)S(1)}, u32[]{:S(2)}, u32[]{:S(2)}) collective-permute-start(f32[64,512]{1,0:T(8,128)S(1)} %get-tuple-element.23), channel_id=1, source_target_pairs={{0,1},{1,2},{2,3},{3,4},{4,5},{5,6},{6,7},{7,8},{8,9},{9,10},{10,1... | collective-permute-start | bytes 393224 | tf_op jit(solution)/shard_map/ppermute | solution.py:16
  71.4 3.2 %collective-permute-start.11 = (f32[64,512]{1,0:T(8,128)S(1)}, f32[64,512]{1,0:T(8,128)S(1)}, u32[]{:S(2)}, u32[]{:S(2)}) collective-permute-start(f32[64,512]{1,0:T(8,128)S(1)} %get-tuple-element.22), channel_id=1, source_target_pairs={{1,0},{2,1},{3,2},{4,3},{5,4},{6,5},{7,6},{8,7},{9,8},{10,9},{11,1... | collective-permute-start | bytes 393224 | tf_op jit(solution)/shard_map/ppermute | solution.py:17
  75.9 9.3 %collective-permute-start.12 = (f32[64,512]{1,0:T(8,128)S(1)}, f32[64,512]{1,0:T(8,128)S(1)}, u32[]{:S(2)}, u32[]{:S(2)}) collective-permute-start(f32[64,512]{1,0:T(8,128)S(1)} %get-tuple-element.21), channel_id=1, source_target_pairs={{0,1},{1,2},{2,3},{3,4},{4,5},{5,6},{6,7},{7,8},{8,9},{9,10},{10,1... | collective-permute-start | bytes 393224 | tf_op jit(solution)/shard_map/ppermute | solution.py:16
  83.8 3.2 %collective-permute-start.13 = (f32[64,512]{1,0:T(8,128)S(1)}, f32[64,512]{1,0:T(8,128)S(1)}, u32[]{:S(2)}, u32[]{:S(2)}) collective-permute-start(f32[64,512]{1,0:T(8,128)S(1)} %get-tuple-element.20), channel_id=1, source_target_pairs={{1,0},{2,1},{3,2},{4,3},{5,4},{6,5},{7,6},{8,7},{9,8},{10,9},{11,1... | collective-permute-start | bytes 393224 | tf_op jit(solution)/shard_map/ppermute | solution.py:17
  88.3 9.1 %collective-permute-start.14 = (f32[64,512]{1,0:T(8,128)S(1)}, f32[64,512]{1,0:T(8,128)S(1)}, u32[]{:S(2)}, u32[]{:S(2)}) collective-permute-start(f32[64,512]{1,0:T(8,128)S(1)} %get-tuple-element.19), channel_id=1, source_target_pairs={{0,1},{1,2},{2,3},{3,4},{4,5},{5,6},{6,7},{7,8},{8,9},{9,10},{10,1... | collective-permute-start | bytes 393224 | tf_op jit(solution)/shard_map/ppermute | solution.py:16
  96.1 3.2 %collective-permute-start.15 = (f32[64,512]{1,0:T(8,128)S(1)}, f32[64,512]{1,0:T(8,128)S(1)}, u32[]{:S(2)}, u32[]{:S(2)}) collective-permute-start(f32[64,512]{1,0:T(8,128)S(1)} %get-tuple-element.18), channel_id=1, source_target_pairs={{1,0},{2,1},{3,2},{4,3},{5,4},{6,5},{7,6},{8,7},{9,8},{10,9},{11,1... | collective-permute-start | bytes 393224 | tf_op jit(solution)/shard_map/ppermute | solution.py:17
where the time goes:
time: 164 us
  blocking collectives  61.5 us (38%)
  starting transfers between devices  53.4 us (33%)
  matrix products  31.8 us (19%)
  local copies, waits for them, and re-layouts  9.29 us (6%)
  waiting for transfers between devices  6.33 us (4%)
    psum x1, blocking collectives, local(): res_norms = jnp.sqrt(lax.psum(jnp.stack(partials), 'row'))  61.5 us
    ppermute x8, starting transfers between devices, extended(): before = lax.ppermute(last, axis, up)  42.9 us
    dot_general x23, matrix products, matmul(): jnp.dot(left, right, precision=lax.Precision.HIGHEST, preferred_element_t...  31.8 us
    ppermute x8, starting transfers between devices, extended(): after = lax.ppermute(first, axis, down)  10.5 us
    gather x1, local copies, waits for them, and re-layouts, local(): pivots = jnp.diagonal(diag_blocks)[:, None]  8.46 us
    ppermute x8, waiting for transfers between devices, extended(): after = lax.ppermute(first, axis, down)  6.31 us
  transfers between devices with their start and end apart: 16, of which 7 were waited for; matrix products, arithmetic and copies ran while one was open for 18% of the time, Pallas kernels for 0%

commit v1 on v0

v1 whole, which is shorter than its diff:
```python
import functools

import jax
import jax.numpy as jnp
from jax import lax
from jax.experimental import pallas as pl
from jax.experimental.pallas import tpu as pltpu
from jax.sharding import PartitionSpec as P

SWEEPS = 8
F32 = jnp.float32
BF16 = jnp.bfloat16
VMEM_GRANT = 24 * 2**20
VMEM_BLOCK = pl.BlockSpec(memory_space=pltpu.VMEM)


def call(kernel, outs, *args, hbm=(), flops=0):
    args = [a if i in hbm else pltpu.with_memory_space_constraint(a, pltpu.VMEM) for i, a in enumerate(args)]
    many = isinstance(outs, (list, tuple))
    return pl.pallas_call(
        kernel,
        out_shape=outs,
        in_specs=[VMEM_BLOCK] * len(args),
        out_specs=[VMEM_BLOCK] * len(outs) if many else VMEM_BLOCK,
        compiler_params=pltpu.CompilerParams(vmem_limit_bytes=VMEM_GRANT),
        cost_estimate=pl.CostEstimate(flops=flops, transcendentals=0, bytes_accessed=0),
    )(*args)


def halves(x):
    high = x.astype(BF16)
    return high, (x - high.astype(F32)).astype(BF16)


def left_terms(x):
    high, low = halves(x)
    return jnp.concatenate([high, low, high], axis=1)


def right_terms(x):
    high, low = halves(x)
    return jnp.concatenate([high, high, low], axis=0)


def product(left, right):
    return jnp.dot(left, right, preferred_element_type=F32)


def place():
    index, size = lax.axis_index("row"), lax.axis_size("row")
    return index % 2, jnp.logical_or(index == 0, index == size - 1)


def rims(rows, width):
    odd, _ = place()
    top = rows - width
    return pl.multiple_of(odd * top, width), pl.multiple_of((1 - odd) * top, width)


def diagonal(block, offset):
    row = lax.broadcasted_iota(jnp.int32, block.shape, 0) + offset
    column = lax.broadcasted_iota(jnp.int32, block.shape, 1)
    return jnp.sum(jnp.where(row == column, block, 0.0), axis=1, keepdims=True)


def facing(outer):
    _, end = place()
    return jnp.where(end, jnp.zeros_like(outer), outer)


def opening(diag, sides, width):
    odd, _ = place()
    top = diag.shape[0] - width
    first = sides[:width] / diagonal(diag[:width, :width], 0)
    last = sides[top:] / diagonal(diag[top:, top:], 0)
    return facing(jnp.where(odd == 1, last, first)), jnp.where(odd == 1, first, last)


def setup_kernel(diag, lower, upper, sides, diag_out, coupling_out, pivot_out, x_out, v_out, sums_out):
    odd, _ = place()
    block, side = diag[...], sides[...]
    pivots = diagonal(block, 0)
    pivot_out[...] = jnp.broadcast_to(pivots, pivot_out.shape)
    x = side / pivots
    x_out[...] = x
    sums_out[0:1, :] = jnp.sum(side * side, axis=0, keepdims=True)
    low, up = lower[...], upper[...]
    outer = jnp.where(odd == 1, up, low)
    inner = jnp.where(odd == 1, low, up)
    coupling_out[...] = left_terms(jnp.concatenate([outer, inner], axis=1))
    left = left_terms(block)
    diag_out[...] = left
    v_out[...] = side - product(left, right_terms(x))


def halo_terms(outer, inner):
    return right_terms(jnp.concatenate([outer[...], inner[...]], axis=0))


def wide(pivots, columns):
    return jnp.concatenate([pivots] * (columns // pivots.shape[1]), axis=1)


def rim_kernel(outer, inner, x, v, coupling, pivots, outer_out, inner_out, *, width):
    rows, columns = x.shape
    far, near = rims(rows, width)
    pick = lambda ref: jnp.concatenate([ref[pl.ds(far, width), :], ref[pl.ds(near, width), :]], axis=0)
    residual = pick(v) - product(pick(coupling), halo_terms(outer, inner))
    new = pick(x) + residual / wide(pick(pivots), columns)
    outer_out[...] = facing(new[:width])
    inner_out[...] = new[width:]


def sweep_kernel(outer, inner, x, v, side, diag, coupling, pivots, sums, x_out, v_out, sums_out, *, sweep):
    columns = x.shape[1]
    sums_out[...] = sums[...]
    residual = v[...] - product(coupling[...], halo_terms(outer, inner))
    sums_out[sweep : sweep + 1, :] = jnp.sum(residual * residual, axis=0, keepdims=True)
    new = x[...] + residual / wide(pivots[...], columns)
    x_out[...] = new
    v_out[...] = side[...] - product(diag[...], right_terms(new))


def last_kernel(outer, inner, v, coupling, sums, r_out, sums_out, *, sweep):
    sums_out[...] = sums[...]
    residual = v[...] - product(coupling[...], halo_terms(outer, inner))
    sums_out[sweep : sweep + 1, :] = jnp.sum(residual * residual, axis=0, keepdims=True)
    r_out[...] = residual


def close_kernel(r, x, pivots, x_out):
    x_out[...] = x[...] + r[...] / wide(pivots[...], x.shape[1])


def pairings():
    size, groups = lax.axis_size("row"), lax.axis_size("grp")
    within = [(i, i ^ 1) for i in range(size)]
    between = []
    for g in range(groups):
        for i in range(size):
            j = i + 1 if i % 2 else i - 1
            if 0 <= j < size:
                target = g * size + j
            elif groups % 2 == 0:
                target = (g ^ 1) * size + i
            else:
                target = g * size + size - 1 - i
            between.append((g * size + i, target))
    return within, between


def exchange(outer, inner):
    within, between = pairings()
    return lax.ppermute(outer, ("grp", "row"), between), lax.ppermute(inner, "row", within)


def row_sum(x):
    size = lax.axis_size("row")
    assert size & (size - 1) == 0
    step = 1
    while step < size:
        flip = step if step == 1 else step + 1
        x = x + lax.ppermute(x, "row", [(i, i ^ flip) for i in range(size)])
        step *= 2
    return x


def local(diag_blocks, lower_coupling, upper_coupling, right_sides):
    rows, columns = right_sides.shape
    width = lower_coupling.shape[1]
    rim = pltpu.VMEM((width, columns), F32)
    panel = pltpu.VMEM((rows, columns), F32)
    sums_shape = pltpu.VMEM((SWEEPS, columns), F32)
    lanes = 128
    outer, inner = opening(diag_blocks, right_sides, width)
    outer, inner = exchange(outer, inner)
    diag, coupling, pivots, x, v, sums = call(
        setup_kernel,
        [
            pltpu.VMEM((rows, 3 * rows), BF16),
            pltpu.VMEM((rows, 6 * width), BF16),
            pltpu.VMEM((rows, lanes), F32),
            panel,
            panel,
            sums_shape,
        ],
        diag_blocks, lower_coupling, upper_coupling, right_sides,
        hbm=(0, 1, 2, 3),
        flops=6 * rows * rows * columns,
    )
    for sweep in range(1, SWEEPS - 1):
        sent = call(
            functools.partial(rim_kernel, width=width),
            [rim, rim],
            outer, inner, x, v, coupling, pivots,
            flops=24 * width * width * columns,
        )
        x, v, sums = call(
            functools.partial(sweep_kernel, sweep=sweep),
            [panel, panel, sums_shape],
            outer, inner, x, v, right_sides, diag, coupling, pivots, sums,
            hbm=(4,),
            flops=6 * rows * (rows + 2 * width) * columns,
        )
        outer, inner = exchange(*sent)
    r, sums = call(
        functools.partial(last_kernel, sweep=SWEEPS - 1),
        [panel, sums_shape],
        outer, inner, v, coupling, sums,
        flops=12 * rows * width * columns,
    )
    solution = call(close_kernel, jax.ShapeDtypeStruct((rows, columns), F32), r, x, pivots, flops=10 * rows * columns)
    return solution, jnp.sqrt(row_sum(sums))


def solution(mesh):
    return jax.shard_map(
        local,
        mesh=mesh,
        in_specs=(P("row", None), P("row", None), P("row", None), P("row", "grp")),
        out_specs=(P("row", "grp"), P(None, "grp")),
        check_vma=False,
    )
```

time: 164 us -> 59.9 us (0.37)
  blocking collectives: 61.5 us -> 0 us
  matrix products: 31.8 us -> 0 us
  starting transfers between devices: 53.4 us -> 31.5 us
  Pallas kernels: 0 us -> 12.4 us
  local copies, waits for them, and re-layouts: 9.29 us -> 4.51 us
  other arithmetic: 0.16 us -> 2.65 us
    psum x1 -> x0, blocking collectives: 61.5 us -> none  [local(): res_norms = jnp.sqrt(lax.psum(jnp.stack(partials), 'row'))]
    dot_general x23 -> x0, matrix products: 31.8 us -> none  [matmul(): jnp.dot(left, right, precision=lax.Precision.HIGHEST, preferred_element_t...]
    ppermute x16 -> x18, starting transfers between devices: 53.4 us -> 31.5 us  [the longest x7 12.5 us: exchange(): lax.ppermute(outer, ('grp', 'row'), between)]
    pallas_call x0 -> x15, Pallas kernels: none -> 12.4 us  [call(): pl.pallas_call(kernel, out_shape=outs, in_specs=[VMEM_BLOCK] * len(args),...]
    gather x1 -> x0, local copies, waits for them, and re-layouts: 8.46 us -> none  [local(): pivots = jnp.diagonal(diag_blocks)[:, None]]
    unnamed x8, local copies, waits for them, and re-layouts: 0.03 us -> 4.51 us
    ppermute x16 -> x18, waiting for transfers between devices: 6.33 us -> 7.65 us  [the longest x4 4.39 us: row_sum(): x = x + lax.ppermute(x, 'row', [(i, i ^ flip) for i in range(size)])]
  transfers between devices with their start and end apart: 16 -> 18, of which waited for: 7 -> 7; matrix products, arithmetic and copies ran while one was open for 18% -> 3% of each run, Pallas kernels for 0% -> 18%
where the time goes in v1:
time: 59.9 us; the launch traced here: 59.6 us
  starting transfers between devices  31.5 us (53%)
  Pallas kernels  12.4 us (21%)
  waiting for transfers between devices  7.65 us (13%)
  local copies, waits for them, and re-layouts  4.51 us (8%)
  other arithmetic  2.65 us (4%)
  between operations  0.89 us (1%)
    ppermute x7, starting transfers between devices, exchange(): lax.ppermute(outer, ('grp', 'row'), between)  12.5 us
    pallas_call x15, Pallas kernels, call(): pl.pallas_call(kernel, out_shape=outs, in_specs=[VMEM_BLOCK] * len(args),...  12.4 us
    ppermute x7, starting transfers between devices, exchange(): lax.ppermute(inner, 'row', within)  10.8 us
    ppermute x4, starting transfers between devices, row_sum(): x = x + lax.ppermute(x, 'row', [(i, i ^ flip) for i in range(size)])  8.07 us
    unnamed x8, local copies, waits for them, and re-layouts  4.51 us
    ppermute x4, waiting for transfers between devices, row_sum(): x = x + lax.ppermute(x, 'row', [(i, i ^ flip) for i in range(size)])  4.39 us
    ppermute x7, waiting for transfers between devices, exchange(): lax.ppermute(outer, ('grp', 'row'), between)  3.24 us
  transfers between devices with their start and end apart: 18, of which 7 were waited for; matrix products, arithmetic and copies ran while one was open for 3% of the time, Pallas kernels for 18%

profile of v1, /device:TPU:0, one launch (start us, length us, event | category | flops | bytes accessed | tf_op | source)
XLA Modules:
  0.0 59.6 jit_solution(2666672424607228633)
XLA Ops:
  2.7 3.1 %collective-permute-start = (f32[64,512]{1,0:T(8,128)S(1)}, f32[64,512]{1,0:T(8,128)S(1)}, u32[]{:S(2)}, u32[]{:S(2)}) collective-permute-start(f32[64,512]{1,0:T(8,128)S(1)} %get-tuple-element.81), channel_id=1, source_target_pairs={{0,16},{1,2},{2,1},{3,4},{4,3},{5,6},{6,5},{7,8},{8,7},{9,10},{10,... | collective-permute-start | bytes 393224 | tf_op jit(solution)/shard_map/ppermute | solution.py:154
  11.8 1.6 %collective-permute-start.2 = (f32[64,512]{1,0:T(8,128)S(1)}, f32[64,512]{1,0:T(8,128)S(1)}, u32[]{:S(2)}, u32[]{:S(2)}) collective-permute-start(f32[64,512]{1,0:T(8,128)S(1)} %get-tuple-element.44), channel_id=1, source_target_pairs={{0,16},{1,2},{2,1},{3,4},{4,3},{5,6},{6,5},{7,8},{8,7},{9,10},{10,... | collective-permute-start | bytes 393224 | tf_op jit(solution)/shard_map/ppermute | solution.py:154
  13.5 1.4 %shard_map.61 = (f32[512,512]{1,0:T(8,128)S(1)}, f32[512,512]{1,0:T(8,128)S(1)}, f32[8,512]{1,0:T(8,128)S(1)}) custom-call(f32[64,512]{1,0:T(8,128)S(1)} %collective-permute-done.outer, f32[64,512]{1,0:T(8,128)S(1)} %collective-permute-done.1.inner, f32[512,512]{1,0:T(8,128)S(1)} %get-tuple-element.40.x, f32[512,512]{1,0:T(8,128)S(1)} %get-tuple-element.41.v, ...), custom_call_target="tpu_custom_call" | custom-call | flops 1006632960 | tf_op jit(solution)/shard_map/pallas_call | solution.py:20
  14.9 1.9 %collective-permute-done.2.outer = f32[64,512]{1,0:T(8,128)S(1)} collective-permute-done((f32[64,512]{1,0:T(8,128)S(1)}, f32[64,512]{1,0:T(8,128)S(1)}, u32[]{:S(2)}, u32[]{:S(2)}) %collective-permute-start.2) | collective-permute-done | bytes 131104 | tf_op jit(solution)/shard_map/ppermute | solution.py:154
  17.1 1.6 %collective-permute-start.4 = (f32[64,512]{1,0:T(8,128)S(1)}, f32[64,512]{1,0:T(8,128)S(1)}, u32[]{:S(2)}, u32[]{:S(2)}) collective-permute-start(f32[64,512]{1,0:T(8,128)S(1)} %get-tuple-element.50), channel_id=1, source_target_pairs={{0,16},{1,2},{2,1},{3,4},{4,3},{5,6},{6,5},{7,8},{8,7},{9,10},{10,... | collective-permute-start | bytes 393224 | tf_op jit(solution)/shard_map/ppermute | solution.py:154
  19.6 1.4 %shard_map.63 = (f32[512,512]{1,0:T(8,128)S(1)}, f32[512,512]{1,0:T(8,128)S(1)}, f32[8,512]{1,0:T(8,128)S(1)}) custom-call(f32[64,512]{1,0:T(8,128)S(1)} %collective-permute-done.2.outer, f32[64,512]{1,0:T(8,128)S(1)} %collective-permute-done.3.inner, f32[512,512]{1,0:T(8,128)S(1)} %get-tuple-element.48.x, f32[512,512]{1,0:T(8,128)S(1)} %get-tuple-element.49.v, ...), custom_call_target="tpu_custom_call" | custom-call | flops 1006632960 | tf_op jit(solution)/shard_map/pallas_call | solution.py:20
  22.3 1.6 %collective-permute-start.6 = (f32[64,512]{1,0:T(8,128)S(1)}, f32[64,512]{1,0:T(8,128)S(1)}, u32[]{:S(2)}, u32[]{:S(2)}) collective-permute-start(f32[64,512]{1,0:T(8,128)S(1)} %get-tuple-element.55), channel_id=1, source_target_pairs={{0,16},{1,2},{2,1},{3,4},{4,3},{5,6},{6,5},{7,8},{8,7},{9,10},{10,... | collective-permute-start | bytes 393224 | tf_op jit(solution)/shard_map/ppermute | solution.py:154
  23.9 1.8 %collective-permute-start.7 = (f32[64,512]{1,0:T(8,128)S(1)}, f32[64,512]{1,0:T(8,128)S(1)}, u32[]{:S(2)}, u32[]{:S(2)}) collective-permute-start(f32[64,512]{1,0:T(8,128)S(1)} %get-tuple-element.56), channel_id=1, source_target_pairs={{0,1},{1,0},{2,3},{3,2},{4,5},{5,4},{6,7},{7,6},{8,9},{9,8},{10,11... | collective-permute-start | bytes 393224 | tf_op jit(solution)/shard_map/ppermute | solution.py:154
  25.7 1.4 %shard_map.65 = (f32[512,512]{1,0:T(8,128)S(1)}, f32[512,512]{1,0:T(8,128)S(1)}, f32[8,512]{1,0:T(8,128)S(1)}) custom-call(f32[64,512]{1,0:T(8,128)S(1)} %collective-permute-done.4.outer, f32[64,512]{1,0:T(8,128)S(1)} %collective-permute-done.5.inner, f32[512,512]{1,0:T(8,128)S(1)} %get-tuple-element.53.x, f32[512,512]{1,0:T(8,128)S(1)} %get-tuple-element.54.v, ...), custom_call_target="tpu_custom_call" | custom-call | flops 1006632960 | tf_op jit(solution)/shard_map/pallas_call | solution.py:20
  27.6 1.6 %collective-permute-start.8 = (f32[64,512]{1,0:T(8,128)S(1)}, f32[64,512]{1,0:T(8,128)S(1)}, u32[]{:S(2)}, u32[]{:S(2)}) collective-permute-start(f32[64,512]{1,0:T(8,128)S(1)} %get-tuple-element.60), channel_id=1, source_target_pairs={{0,16},{1,2},{2,1},{3,4},{4,3},{5,6},{6,5},{7,8},{8,7},{9,10},{10,... | collective-permute-start | bytes 393224 | tf_op jit(solution)/shard_map/ppermute | solution.py:154
  29.2 2.6 %collective-permute-start.9 = (f32[64,512]{1,0:T(8,128)S(1)}, f32[64,512]{1,0:T(8,128)S(1)}, u32[]{:S(2)}, u32[]{:S(2)}) collective-permute-start(f32[64,512]{1,0:T(8,128)S(1)} %get-tuple-element.61), channel_id=1, source_target_pairs={{0,1},{1,0},{2,3},{3,2},{4,5},{5,4},{6,7},{7,6},{8,9},{9,8},{10,11... | collective-permute-start | bytes 393224 | tf_op jit(solution)/shard_map/ppermute | solution.py:154
  31.8 1.4 %shard_map.67 = (f32[512,512]{1,0:T(8,128)S(1)}, f32[512,512]{1,0:T(8,128)S(1)}, f32[8,512]{1,0:T(8,128)S(1)}) custom-call(f32[64,512]{1,0:T(8,128)S(1)} %collective-permute-done.6.outer, f32[64,512]{1,0:T(8,128)S(1)} %collective-permute-done.7.inner, f32[512,512]{1,0:T(8,128)S(1)} %get-tuple-element.58.x, f32[512,512]{1,0:T(8,128)S(1)} %get-tuple-element.59.v, ...), custom_call_target="tpu_custom_call" | custom-call | flops 1006632960 | tf_op jit(solution)/shard_map/pallas_call | solution.py:20
  33.5 1.6 %collective-permute-start.10 = (f32[64,512]{1,0:T(8,128)S(1)}, f32[64,512]{1,0:T(8,128)S(1)}, u32[]{:S(2)}, u32[]{:S(2)}) collective-permute-start(f32[64,512]{1,0:T(8,128)S(1)} %get-tuple-element.65), channel_id=1, source_target_pairs={{0,16},{1,2},{2,1},{3,4},{4,3},{5,6},{6,5},{7,8},{8,7},{9,10},{10,... | collective-permute-start | bytes 393224 | tf_op jit(solution)/shard_map/ppermute | solution.py:154
  35.1 2.7 %collective-permute-start.11 = (f32[64,512]{1,0:T(8,128)S(1)}, f32[64,512]{1,0:T(8,128)S(1)}, u32[]{:S(2)}, u32[]{:S(2)}) collective-permute-start(f32[64,512]{1,0:T(8,128)S(1)} %get-tuple-element.66), channel_id=1, source_target_pairs={{0,1},{1,0},{2,3},{3,2},{4,5},{5,4},{6,7},{7,6},{8,9},{9,8},{10,11... | collective-permute-start | bytes 393224 | tf_op jit(solution)/shard_map/ppermute | solution.py:154
  37.8 1.4 %shard_map.69 = (f32[512,512]{1,0:T(8,128)S(1)}, f32[512,512]{1,0:T(8,128)S(1)}, f32[8,512]{1,0:T(8,128)S(1)}) custom-call(f32[64,512]{1,0:T(8,128)S(1)} %collective-permute-done.8.outer, f32[64,512]{1,0:T(8,128)S(1)} %collective-permute-done.9.inner, f32[512,512]{1,0:T(8,128)S(1)} %get-tuple-element.63.x, f32[512,512]{1,0:T(8,128)S(1)} %get-tuple-element.64.v, ...), custom_call_target="tpu_custom_call" | custom-call | flops 1006632960 | tf_op jit(solution)/shard_map/pallas_call | solution.py:20
  39.5 1.6 %collective-permute-start.12 = (f32[64,512]{1,0:T(8,128)S(1)}, f32[64,512]{1,0:T(8,128)S(1)}, u32[]{:S(2)}, u32[]{:S(2)}) collective-permute-start(f32[64,512]{1,0:T(8,128)S(1)} %get-tuple-element.70), channel_id=1, source_target_pairs={{0,16},{1,2},{2,1},{3,4},{4,3},{5,6},{6,5},{7,8},{8,7},{9,10},{10,... | collective-permute-start | bytes 393224 | tf_op jit(solution)/shard_map/ppermute | solution.py:154
  41.1 2.5 %collective-permute-start.13 = (f32[64,512]{1,0:T(8,128)S(1)}, f32[64,512]{1,0:T(8,128)S(1)}, u32[]{:S(2)}, u32[]{:S(2)}) collective-permute-start(f32[64,512]{1,0:T(8,128)S(1)} %get-tuple-element.71), channel_id=1, source_target_pairs={{0,1},{1,0},{2,3},{3,2},{4,5},{5,4},{6,7},{7,6},{8,9},{9,8},{10,11... | collective-permute-start | bytes 393224 | tf_op jit(solution)/shard_map/ppermute | solution.py:154
  43.5 1.4 %shard_map.71 = (f32[512,512]{1,0:T(8,128)S(1)}, f32[512,512]{1,0:T(8,128)S(1)}, f32[8,512]{1,0:T(8,128)S(1)}) custom-call(f32[64,512]{1,0:T(8,128)S(1)} %collective-permute-done.10.outer, f32[64,512]{1,0:T(8,128)S(1)} %collective-permute-done.11.inner, f32[512,512]{1,0:T(8,128)S(1)} %get-tuple-element.68.x, f32[512,512]{1,0:T(8,128)S(1)} %get-tuple-element.69.v, ...), custom_call_target="tpu_custom_call" | custom-call | flops 1006632960 | tf_op jit(solution)/shard_map/pallas_call | solution.py:20
  45.4 1.6 %collective-permute-start.14 = (f32[8,512]{1,0:T(8,128)S(1)}, f32[8,512]{1,0:T(8,128)S(1)}, u32[]{:S(2)}, u32[]{:S(2)}) collective-permute-start(f32[8,512]{1,0:T(8,128)S(1)} %get-tuple-element.77), channel_id=1, source_target_pairs={{0,1},{1,0},{2,3},{3,2},{4,5},{5,4},{6,7},{7,6},{8,9},{9,8},{10,11... | collective-permute-start | bytes 49160 | tf_op jit(solution)/shard_map/ppermute | solution.py:163
  47.8 2.5 %collective-permute-start.15 = (f32[8,512]{1,0:T(8,128)S(1)}, f32[8,512]{1,0:T(8,128)S(1)}, u32[]{:S(2)}, u32[]{:S(2)}) collective-permute-start(f32[8,512]{1,0:T(8,128)S(1)} %add.17), channel_id=1, source_target_pairs={{0,3},{1,2},{2,1},{3,0},{4,7},{5,6},{6,5},{7,4},{8,11},{9,10},{10,... | collective-permute-start | bytes 49160 | tf_op jit(solution)/shard_map/ppermute | solution.py:163
  50.3 1.4 %collective-permute-done.15 = f32[8,512]{1,0:T(8,128)S(1)} collective-permute-done((f32[8,512]{1,0:T(8,128)S(1)}, f32[8,512]{1,0:T(8,128)S(1)}, u32[]{:S(2)}, u32[]{:S(2)}) %collective-permute-start.15) | collective-permute-done | bytes 16416 | tf_op jit(solution)/shard_map/ppermute | solution.py:163
  51.7 1.5 %collective-permute-start.16 = (f32[8,512]{1,0:T(8,128)S(1)}, f32[8,512]{1,0:T(8,128)S(1)}, u32[]{:S(2)}, u32[]{:S(2)}) collective-permute-start(f32[8,512]{1,0:T(8,128)S(1)} %add.18), channel_id=1, source_target_pairs={{0,5},{1,4},{2,7},{3,6},{4,1},{5,0},{6,3},{7,2},{8,13},{9,12},{10,... | collective-permute-start | bytes 49160 | tf_op jit(solution)/shard_map/ppermute | solution.py:163
  53.2 1.7 %collective-permute-done.16 = f32[8,512]{1,0:T(8,128)S(1)} collective-permute-done((f32[8,512]{1,0:T(8,128)S(1)}, f32[8,512]{1,0:T(8,128)S(1)}, u32[]{:S(2)}, u32[]{:S(2)}) %collective-permute-start.16) | collective-permute-done | bytes 16416 | tf_op jit(solution)/shard_map/ppermute | solution.py:163
  54.9 2.5 %collective-permute-start.17 = (f32[8,512]{1,0:T(8,128)S(1)}, f32[8,512]{1,0:T(8,128)S(1)}, u32[]{:S(2)}, u32[]{:S(2)}) collective-permute-start(f32[8,512]{1,0:T(8,128)S(1)} %add.19), channel_id=1, source_target_pairs={{0,9},{1,8},{2,11},{3,10},{4,13},{5,12},{6,15},{7,14},{8,1},{9,0},... | collective-permute-start | bytes 49160 | tf_op jit(solution)/shard_map/ppermute | solution.py:163
  (41 shorter events, 15.1 us)
Async XLA Ops:
  2.7 8.8 %collective-permute-start = (f32[64,512]{1,0:T(8,128)S(1)}, f32[64,512]{1,0:T(8,128)S(1)}, u32[]{:S(2)}, u32[]{:S(2)}) collective-permute-start(f32[64,512]{1,0:T(8,128)S(1)} %get-tuple-element.81), channel_id=1, source_target_pairs={{0,16},{1,2},{2,1},{3,4},{4,3},{5,6},{6,5},{7,8},{8,7},{9,10},{10,... | collective-permute-start | bytes 393224 | tf_op jit(solution)/shard_map/ppermute | solution.py:154
  5.7 5.8 %collective-permute-start.1 = (f32[64,512]{1,0:T(8,128)S(1)}, f32[64,512]{1,0:T(8,128)S(1)}, u32[]{:S(2)}, u32[]{:S(2)}) collective-permute-start(f32[64,512]{1,0:T(8,128)S(1)} %get-tuple-element.80), channel_id=1, source_target_pairs={{0,1},{1,0},{2,3},{3,2},{4,5},{5,4},{6,7},{7,6},{8,9},{9,8},{10,11... | collective-permute-start | bytes 393224 | tf_op jit(solution)/shard_map/ppermute | solution.py:154
  7.9 1.2 %copy-start = (f32[512,512]{1,0:T(8,128)S(1)}, f32[512,512]{1,0:T(8,128)}, u32[]{:S(2)}) copy-start(f32[512,512]{1,0:T(8,128)} %side.11) | copy-start | bytes 3145732
  9.1 1.2 %copy-start.2 = (f32[512,512]{1,0:T(8,128)S(1)}, f32[512,512]{1,0:T(8,128)}, u32[]{:S(2)}) copy-start(f32[512,512]{1,0:T(8,128)} %diag.1) | copy-start | bytes 3145732
  11.5 2.0 %copy-start.1 = (f32[512,512]{1,0:T(8,128)S(1)}, f32[512,512]{1,0:T(8,128)}, u32[]{:S(2)}) copy-start(f32[512,512]{1,0:T(8,128)} %side.11) | copy-start | bytes 3145732
  11.8 5.0 %collective-permute-start.2 = (f32[64,512]{1,0:T(8,128)S(1)}, f32[64,512]{1,0:T(8,128)S(1)}, u32[]{:S(2)}, u32[]{:S(2)}) collective-permute-start(f32[64,512]{1,0:T(8,128)S(1)} %get-tuple-element.44), channel_id=1, source_target_pairs={{0,16},{1,2},{2,1},{3,4},{4,3},{5,6},{6,5},{7,8},{8,7},{9,10},{10,... | collective-permute-start | bytes 393224 | tf_op jit(solution)/shard_map/ppermute | solution.py:154
  13.4 3.5 %collective-permute-start.3 = (f32[64,512]{1,0:T(8,128)S(1)}, f32[64,512]{1,0:T(8,128)S(1)}, u32[]{:S(2)}, u32[]{:S(2)}) collective-permute-start(f32[64,512]{1,0:T(8,128)S(1)} %get-tuple-element.45), channel_id=1, source_target_pairs={{0,1},{1,0},{2,3},{3,2},{4,5},{5,4},{6,7},{7,6},{8,9},{9,8},{10,11... | collective-permute-start | bytes 393224 | tf_op jit(solution)/shard_map/ppermute | solution.py:154
  17.1 5.0 %collective-permute-start.4 = (f32[64,512]{1,0:T(8,128)S(1)}, f32[64,512]{1,0:T(8,128)S(1)}, u32[]{:S(2)}, u32[]{:S(2)}) collective-permute-start(f32[64,512]{1,0:T(8,128)S(1)} %get-tuple-element.50), channel_id=1, source_target_pairs={{0,16},{1,2},{2,1},{3,4},{4,3},{5,6},{6,5},{7,8},{8,7},{9,10},{10,... | collective-permute-start | bytes 393224 | tf_op jit(solution)/shard_map/ppermute | solution.py:154
  18.6 3.5 %collective-permute-start.5 = (f32[64,512]{1,0:T(8,128)S(1)}, f32[64,512]{1,0:T(8,128)S(1)}, u32[]{:S(2)}, u32[]{:S(2)}) collective-permute-start(f32[64,512]{1,0:T(8,128)S(1)} %get-tuple-element.51), channel_id=1, source_target_pairs={{0,1},{1,0},{2,3},{3,2},{4,5},{5,4},{6,7},{7,6},{8,9},{9,8},{10,11... | collective-permute-start | bytes 393224 | tf_op jit(solution)/shard_map/ppermute | solution.py:154
  22.3 5.0 %collective-permute-start.6 = (f32[64,512]{1,0:T(8,128)S(1)}, f32[64,512]{1,0:T(8,128)S(1)}, u32[]{:S(2)}, u32[]{:S(2)}) collective-permute-start(f32[64,512]{1,0:T(8,128)S(1)} %get-tuple-element.55), channel_id=1, source_target_pairs={{0,16},{1,2},{2,1},{3,4},{4,3},{5,6},{6,5},{7,8},{8,7},{9,10},{10,... | collective-permute-start | bytes 393224 | tf_op jit(solution)/shard_map/ppermute | solution.py:154
  23.9 3.5 %collective-permute-start.7 = (f32[64,512]{1,0:T(8,128)S(1)}, f32[64,512]{1,0:T(8,128)S(1)}, u32[]{:S(2)}, u32[]{:S(2)}) collective-permute-start(f32[64,512]{1,0:T(8,128)S(1)} %get-tuple-element.56), channel_id=1, source_target_pairs={{0,1},{1,0},{2,3},{3,2},{4,5},{5,4},{6,7},{7,6},{8,9},{9,8},{10,11... | collective-permute-start | bytes 393224 | tf_op jit(solution)/shard_map/ppermute | solution.py:154
  27.6 5.6 %collective-permute-start.8 = (f32[64,512]{1,0:T(8,128)S(1)}, f32[64,512]{1,0:T(8,128)S(1)}, u32[]{:S(2)}, u32[]{:S(2)}) collective-permute-start(f32[64,512]{1,0:T(8,128)S(1)} %get-tuple-element.60), channel_id=1, source_target_pairs={{0,16},{1,2},{2,1},{3,4},{4,3},{5,6},{6,5},{7,8},{8,7},{9,10},{10,... | collective-permute-start | bytes 393224 | tf_op jit(solution)/shard_map/ppermute | solution.py:154
  29.2 4.0 %collective-permute-start.9 = (f32[64,512]{1,0:T(8,128)S(1)}, f32[64,512]{1,0:T(8,128)S(1)}, u32[]{:S(2)}, u32[]{:S(2)}) collective-permute-start(f32[64,512]{1,0:T(8,128)S(1)} %get-tuple-element.61), channel_id=1, source_target_pairs={{0,1},{1,0},{2,3},{3,2},{4,5},{5,4},{6,7},{7,6},{8,9},{9,8},{10,11... | collective-permute-start | bytes 393224 | tf_op jit(solution)/shard_map/ppermute | solution.py:154
  33.5 5.7 %collective-permute-start.10 = (f32[64,512]{1,0:T(8,128)S(1)}, f32[64,512]{1,0:T(8,128)S(1)}, u32[]{:S(2)}, u32[]{:S(2)}) collective-permute-start(f32[64,512]{1,0:T(8,128)S(1)} %get-tuple-element.65), channel_id=1, source_target_pairs={{0,16},{1,2},{2,1},{3,4},{4,3},{5,6},{6,5},{7,8},{8,7},{9,10},{10,... | collective-permute-start | bytes 393224 | tf_op jit(solution)/shard_map/ppermute | solution.py:154
  35.1 4.1 %collective-permute-start.11 = (f32[64,512]{1,0:T(8,128)S(1)}, f32[64,512]{1,0:T(8,128)S(1)}, u32[]{:S(2)}, u32[]{:S(2)}) collective-permute-start(f32[64,512]{1,0:T(8,128)S(1)} %get-tuple-element.66), channel_id=1, source_target_pairs={{0,1},{1,0},{2,3},{3,2},{4,5},{5,4},{6,7},{7,6},{8,9},{9,8},{10,11... | collective-permute-start | bytes 393224 | tf_op jit(solution)/shard_map/ppermute | solution.py:154
  39.5 5.4 %collective-permute-start.12 = (f32[64,512]{1,0:T(8,128)S(1)}, f32[64,512]{1,0:T(8,128)S(1)}, u32[]{:S(2)}, u32[]{:S(2)}) collective-permute-start(f32[64,512]{1,0:T(8,128)S(1)} %get-tuple-element.70), channel_id=1, source_target_pairs={{0,16},{1,2},{2,1},{3,4},{4,3},{5,6},{6,5},{7,8},{8,7},{9,10},{10,... | collective-permute-start | bytes 393224 | tf_op jit(solution)/shard_map/ppermute | solution.py:154
  41.1 3.9 %collective-permute-start.13 = (f32[64,512]{1,0:T(8,128)S(1)}, f32[64,512]{1,0:T(8,128)S(1)}, u32[]{:S(2)}, u32[]{:S(2)}) collective-permute-start(f32[64,512]{1,0:T(8,128)S(1)} %get-tuple-element.71), channel_id=1, source_target_pairs={{0,1},{1,0},{2,3},{3,2},{4,5},{5,4},{6,7},{7,6},{8,9},{9,8},{10,11... | collective-permute-start | bytes 393224 | tf_op jit(solution)/shard_map/ppermute | solution.py:154
  45.4 2.4 %collective-permute-start.14 = (f32[8,512]{1,0:T(8,128)S(1)}, f32[8,512]{1,0:T(8,128)S(1)}, u32[]{:S(2)}, u32[]{:S(2)}) collective-permute-start(f32[8,512]{1,0:T(8,128)S(1)} %get-tuple-element.77), channel_id=1, source_target_pairs={{0,1},{1,0},{2,3},{3,2},{4,5},{5,4},{6,7},{7,6},{8,9},{9,8},{10,11... | collective-permute-start | bytes 49160 | tf_op jit(solution)/shard_map/ppermute | solution.py:163
  47.8 3.9 %collective-permute-start.15 = (f32[8,512]{1,0:T(8,128)S(1)}, f32[8,512]{1,0:T(8,128)S(1)}, u32[]{:S(2)}, u32[]{:S(2)}) collective-permute-start(f32[8,512]{1,0:T(8,128)S(1)} %add.17), channel_id=1, source_target_pairs={{0,3},{1,2},{2,1},{3,0},{4,7},{5,6},{6,5},{7,4},{8,11},{9,10},{10,... | collective-permute-start | bytes 49160 | tf_op jit(solution)/shard_map/ppermute | solution.py:163
  51.7 3.2 %collective-permute-start.16 = (f32[8,512]{1,0:T(8,128)S(1)}, f32[8,512]{1,0:T(8,128)S(1)}, u32[]{:S(2)}, u32[]{:S(2)}) collective-permute-start(f32[8,512]{1,0:T(8,128)S(1)} %add.18), channel_id=1, source_target_pairs={{0,5},{1,4},{2,7},{3,6},{4,1},{5,0},{6,3},{7,2},{8,13},{9,12},{10,... | collective-permute-start | bytes 49160 | tf_op jit(solution)/shard_map/ppermute | solution.py:163
  54.9 4.1 %collective-permute-start.17 = (f32[8,512]{1,0:T(8,128)S(1)}, f32[8,512]{1,0:T(8,128)S(1)}, u32[]{:S(2)}, u32[]{:S(2)}) collective-permute-start(f32[8,512]{1,0:T(8,128)S(1)} %add.19), channel_id=1, source_target_pairs={{0,9},{1,8},{2,11},{3,10},{4,13},{5,12},{6,15},{7,14},{8,1},{9,0},... | collective-permute-start | bytes 49160 | tf_op jit(solution)/shard_map/ppermute | solution.py:163

commit v2 on v1

v2 whole, which is shorter than its diff:
```python
import functools

import jax
import jax.numpy as jnp
from jax import lax
from jax.experimental import pallas as pl
from jax.experimental.pallas import tpu as pltpu
from jax.sharding import PartitionSpec as P


SWEEPS = 8
F32 = jnp.float32
BF16 = jnp.bfloat16
VMEM_GRANT = 24 * 2**20
HBM_BLOCK = pl.BlockSpec(memory_space=pltpu.HBM)
VMEM_BLOCK = pl.BlockSpec(memory_space=pltpu.VMEM)


def call(kernel, outs, *args, hbm=(), scratch=(), flops=0):
    args = [pltpu.with_memory_space_constraint(a, pltpu.HBM if i in hbm else pltpu.VMEM) for i, a in enumerate(args)]
    many = isinstance(outs, list)
    return pl.pallas_call(
        kernel,
        out_shape=outs,
        in_specs=[HBM_BLOCK if i in hbm else VMEM_BLOCK for i in range(len(args))],
        out_specs=[VMEM_BLOCK] * len(outs) if many else VMEM_BLOCK,
        scratch_shapes=scratch,
        compiler_params=pltpu.CompilerParams(vmem_limit_bytes=VMEM_GRANT),
        cost_estimate=pl.CostEstimate(flops=flops, transcendentals=0, bytes_accessed=0),
    )(*args)


def halves(x):
    high = x.astype(BF16)
    return high, (x - high.astype(F32)).astype(BF16)


def left_terms(x):
    high, low = halves(x)
    return jnp.concatenate([high, low, high], axis=1)


def right_terms(x):
    high, low = halves(x)
    return jnp.concatenate([high, high, low], axis=0)


def product(left, right):
    return jnp.dot(left, right, preferred_element_type=F32)


def place():
    index, size = lax.axis_index("row"), lax.axis_size("row")
    return index % 2, jnp.logical_or(index == 0, index == size - 1)


def rims(rows, width):
    odd, _ = place()
    top = rows - width
    return pl.multiple_of(odd * top, width), pl.multiple_of((1 - odd) * top, width)


def diagonal(block, offset):
    row = lax.broadcasted_iota(jnp.int32, block.shape, 0) + offset
    column = lax.broadcasted_iota(jnp.int32, block.shape, 1)
    return jnp.sum(jnp.where(row == column, block, 0.0), axis=1, keepdims=True)


def facing(outer):
    _, end = place()
    return jnp.where(end, jnp.zeros_like(outer), outer)


def copies(pairs, sems):
    moves = [pltpu.make_async_copy(source, target, sems.at[i]) for i, (source, target) in enumerate(pairs)]
    for move in moves:
        move.start()
    return moves


def open_kernel(diag, lower, upper, sides, outer_out, inner_out, corners, strips, low, up, sems):
    odd, end = place()
    rows, columns = sides.shape
    width, lanes = corners.shape[1:]
    top = rows - width
    moves = copies(
        [
            (diag.at[pl.ds(0, width), pl.ds(0, lanes)], corners.at[0]),
            (diag.at[pl.ds(top, width), pl.ds(rows - lanes, lanes)], corners.at[1]),
            (sides.at[pl.ds(0, width)], strips.at[0]),
            (sides.at[pl.ds(top, width)], strips.at[1]),
            (lower.at[:, pl.ds(0, lanes)], low),
            (upper.at[:, pl.ds(rows - lanes, lanes)], up),
        ],
        sems,
    )
    for move in moves:
        move.wait()
    head, tail = diagonal(corners[0], 0), diagonal(corners[1], lanes - width)
    first = strips[0] / head
    last = strips[1] / tail
    outer_out[:, :columns] = facing(jnp.where(odd == 1, last, first))
    coupling = facing(jnp.where(odd == 1, up[...].T[lanes - width :], low[...].T[:width]))
    pivots = jnp.where(end, 1.0, jnp.where(odd == 1, tail, head))
    outer_out[:, columns:] = jnp.concatenate([coupling, jnp.broadcast_to(pivots, coupling.shape)], axis=1)
    inner_out[...] = jnp.where(odd == 1, first, last)


def setup_kernel(diag, lower, upper, sides, diag_out, coupling_out, near_out, pivot_out, side_out, x_out, v_out, sums_out, block, low, up, sems):
    odd, _ = place()
    width, rows = low.shape
    moves = copies([(sides, side_out), (diag, block), (lower, low), (upper, up)], sems)
    moves[0].wait()
    side = side_out[...]
    sums_out[0:1, :] = jnp.sum(side * side, axis=0, keepdims=True)
    moves[1].wait()
    pivots = diagonal(block[...], 0)
    pivot_out[...] = jnp.broadcast_to(pivots, pivot_out.shape)
    x = side / pivots
    x_out[...] = x
    left = left_terms(block[...])
    diag_out[...] = left
    v_out[...] = side - product(left, right_terms(x))
    moves[2].wait()
    moves[3].wait()
    outer = jnp.where(odd == 1, up[...], low[...])
    inner = jnp.where(odd == 1, low[...], up[...])
    coupling = jnp.concatenate([outer, inner], axis=0).T
    coupling_out[...] = left_terms(coupling)
    top = rows - width
    inner = coupling[:, width:]
    near_out[...] = left_terms(jnp.where(odd == 1, inner[top:, :], inner[:width, :]))


def wide(pivots, columns):
    return jnp.concatenate([pivots] * (columns // pivots.shape[1]), axis=1)


def send_kernel(inner, x, v, near, pivots, outer_out):
    rows, columns = x.shape
    width = inner.shape[0]
    far, _ = rims(rows, width)
    pick = lambda ref: ref[pl.ds(far, width), :]
    residual = pick(v) - product(near[...], right_terms(inner[...]))
    outer_out[...] = facing(pick(x) + residual / wide(pick(pivots), columns))


def outer_halo(message, opened, mine):
    if mine is None:
        return message[:, : opened.shape[1] - 128]
    columns = message.shape[1]
    width = message.shape[0]
    extra = opened[:, columns:]
    term = product(left_terms(extra[:, :width]), right_terms(mine[...]))
    return message[...] - term / extra[:, width : width + 1]


def halo_terms(message, opened, mine, inner):
    return right_terms(jnp.concatenate([outer_halo(message, opened, mine), inner[...]], axis=0))


def keep_kernel(x, outer_out):
    far, _ = rims(x.shape[0], outer_out.shape[0])
    outer_out[...] = x[pl.ds(far, outer_out.shape[0]), :]


def rim_kernel(*refs, first):
    refs = list(refs)
    mine = None if first else refs.pop(0)
    message, opened, inner, x, v, coupling, pivots, inner_out = refs
    rows, columns = x.shape
    width = inner.shape[0]
    _, near = rims(rows, width)
    pick = lambda ref: ref[pl.ds(near, width), :]
    residual = pick(v) - product(pick(coupling), halo_terms(message, opened, mine, inner))
    inner_out[...] = pick(x) + residual / wide(pick(pivots), columns)


def sweep_kernel(*refs, sweep, first):
    refs = list(refs)
    mine = None if first else refs.pop(0)
    message, opened, inner, x, v, side, diag, coupling, pivots, sums, x_out, v_out, sums_out = refs
    _, columns = x.shape
    sums_out[...] = sums[...]
    residual = v[...] - product(coupling[...], halo_terms(message, opened, mine, inner))
    sums_out[sweep : sweep + 1, :] = jnp.sum(residual * residual, axis=0, keepdims=True)
    new = x[...] + residual / wide(pivots[...], columns)
    x_out[...] = new
    v_out[...] = side[...] - product(diag[...], right_terms(new))


def last_kernel(mine, message, opened, inner, v, coupling, sums, r_out, sums_out, *, sweep):
    sums_out[...] = sums[...]
    residual = v[...] - product(coupling[...], halo_terms(message, opened, mine, inner))
    sums_out[sweep : sweep + 1, :] = jnp.sum(residual * residual, axis=0, keepdims=True)
    r_out[...] = residual


def close_kernel(r, x, pivots, x_out):
    x_out[...] = x[...] + r[...] / wide(pivots[...], x.shape[1])


def pairings():
    size, groups = lax.axis_size("row"), lax.axis_size("grp")
    within = [(i, i ^ 1) for i in range(size)]
    between = []
    for g in range(groups):
        for i in range(size):
            j = i + 1 if i % 2 else i - 1
            if 0 <= j < size:
                target = g * size + j
            elif groups % 2 == 0:
                target = (g ^ 1) * size + i
            else:
                target = g * size + size - 1 - i
            between.append((g * size + i, target))
    return within, between


def across(outer):
    return lax.ppermute(outer, ("grp", "row"), pairings()[1])


def along(inner):
    return lax.ppermute(inner, "row", pairings()[0])


def row_sum(x):
    size = lax.axis_size("row")
    assert size & (size - 1) == 0
    step = 1
    while step < size:
        flip = step if step == 1 else step + 1
        x = x + lax.ppermute(x, "row", [(i, i ^ flip) for i in range(size)])
        step *= 2
    return x


def program(diag_blocks, lower_coupling, upper_coupling, right_sides):
    rows, columns = right_sides.shape
    width = lower_coupling.shape[1]
    rim = pltpu.VMEM((width, columns), F32)
    panel = pltpu.VMEM((rows, columns), F32)
    sums_shape = pltpu.VMEM((SWEEPS, columns), F32)
    lanes = 128
    lower, upper = lower_coupling.T, upper_coupling.T
    opened, inner = call(
        open_kernel,
        [pltpu.VMEM((width, columns + 2 * width), F32), rim],
        diag_blocks, lower, upper, right_sides,
        hbm=(0, 1, 2, 3),
        scratch=[
            pltpu.VMEM((2, width, lanes), F32),
            pltpu.VMEM((2, width, columns), F32),
            pltpu.VMEM((width, lanes), F32),
            pltpu.VMEM((width, lanes), F32),
            pltpu.SemaphoreType.DMA((6,)),
        ],
    )
    opened = message = across(opened)
    inner = along(inner)
    diag, coupling, near, pivots, side, x, v, sums = call(
        setup_kernel,
        [
            pltpu.VMEM((rows, 3 * rows), BF16),
            pltpu.VMEM((rows, 6 * width), BF16),
            pltpu.VMEM((width, 3 * width), BF16),
            pltpu.VMEM((rows, lanes), F32),
            panel,
            panel,
            panel,
            sums_shape,
        ],
        diag_blocks, lower, upper, right_sides,
        hbm=(0, 1, 2, 3),
        scratch=[
            pltpu.VMEM((rows, rows), F32),
            pltpu.VMEM((width, rows), F32),
            pltpu.VMEM((width, rows), F32),
            pltpu.SemaphoreType.DMA((4,)),
        ],
        flops=6 * rows * rows * columns,
    )
    mine = []
    for sweep in range(1, SWEEPS - 1):
        sent = call(send_kernel, rim, inner, x, v, near, pivots, flops=6 * width * width * columns)
        ahead = across(sent)
        kept = call(keep_kernel, rim, x)
        rim_values = call(
            functools.partial(rim_kernel, first=sweep == 1),
            rim,
            *mine, message, opened, inner, x, v, coupling, pivots,
            flops=18 * width * width * columns,
        )
        x, v, sums = call(
            functools.partial(sweep_kernel, sweep=sweep, first=sweep == 1),
            [panel, panel, sums_shape],
            *mine, message, opened, inner, x, v, side, diag, coupling, pivots, sums,
            flops=6 * rows * (rows + 2 * width) * columns,
        )
        mine, message, inner = [kept], ahead, along(rim_values)
    r, sums = call(
        functools.partial(last_kernel, sweep=SWEEPS - 1),
        [panel, sums_shape],
        *mine, message, opened, inner, v, coupling, sums,
        flops=12 * rows * width * columns,
    )
    solution = call(close_kernel, jax.ShapeDtypeStruct((rows, columns), F32), r, x, pivots, flops=10 * rows * columns)
    return solution, jnp.sqrt(row_sum(sums))


def solution(mesh):
    return jax.shard_map(
        program,
        mesh=mesh,
        in_specs=(P("row", None), P("row", None), P("row", None), P("row", "grp")),
        out_specs=(P("row", "grp"), P(None, "grp")),
        check_vma=False,
    )
```

time: 59.9 us -> 52.6 us (0.88)
  starting transfers between devices: 31.5 us -> 20.5 us
  Pallas kernels: 12.4 us -> 18.4 us
  local copies, waits for them, and re-layouts: 4.51 us -> 0 us
  waiting for transfers between devices: 7.65 us -> 12.1 us
  other arithmetic: 2.65 us -> 0.63 us
    ppermute x14, starting transfers between devices: 23.4 us -> 12.4 us  [the longest x7 10.6 us: across(): return lax.ppermute(outer, ('grp', 'row'), pairings()[1])]
    pallas_call x15 -> x28, Pallas kernels: 12.4 us -> 18.4 us  [call(): pl.pallas_call(kernel, out_shape=outs, in_specs=[HBM_BLOCK if i in hbm el...]
    ppermute x14, waiting for transfers between devices: 3.26 us -> 7.84 us  [the longest x7 7.82 us: across(): return lax.ppermute(outer, ('grp', 'row'), pairings()[1])]
    unnamed x8 -> x0, local copies, waits for them, and re-layouts: 4.51 us -> none
    select_n x1 -> x0, other arithmetic: 1.07 us -> none  [opening(): jnp.where(odd == 1, first, last)]
    reduce_sum x1 -> x0, other arithmetic: 0.95 us -> none  [diagonal(): return jnp.sum(jnp.where(row == column, block, 0.0), axis=1, keepdims=True)]
  transfers between devices with their start and end apart: 18 -> 18, of which waited for: 7 -> 10; matrix products, arithmetic and copies ran while one was open for 3% -> 0% of each run, Pallas kernels for 18% -> 29%
where the time goes in v2:
time: 52.6 us; the launch traced here: 52.5 us
  starting transfers between devices  20.5 us (39%)
  Pallas kernels  18.4 us (35%)
  waiting for transfers between devices  12.1 us (23%)
  between operations  0.82 us (2%)
  other arithmetic  0.63 us (1%)
    pallas_call x28, Pallas kernels, call(): pl.pallas_call(kernel, out_shape=outs, in_specs=[HBM_BLOCK if i in hbm el...  18.4 us
    ppermute x7, starting transfers between devices, across(): return lax.ppermute(outer, ('grp', 'row'), pairings()[1])  10.6 us
    ppermute x4, starting transfers between devices, row_sum(): x = x + lax.ppermute(x, 'row', [(i, i ^ flip) for i in range(size)])  8.14 us
    ppermute x7, waiting for transfers between devices, across(): return lax.ppermute(outer, ('grp', 'row'), pairings()[1])  7.82 us
    ppermute x4, waiting for transfers between devices, row_sum(): x = x + lax.ppermute(x, 'row', [(i, i ^ flip) for i in range(size)])  4.26 us
    ppermute x7, starting transfers between devices, along(): return lax.ppermute(inner, 'row', pairings()[0])  1.8 us
  transfers between devices with their start and end apart: 18, of which 10 were waited for; matrix products, arithmetic and copies ran while one was open for 0% of the time, Pallas kernels for 29%

profile of v2, /device:TPU:0, one launch (start us, length us, event | category | flops | bytes accessed | tf_op | source)
XLA Modules:
  0.0 52.5 jit_solution(15413841802312866088)
XLA Ops:
  0.6 1.2 %shard_map.59 = (f32[64,640]{1,0:T(8,128)S(1)}, f32[64,512]{1,0:T(8,128)S(1)}) custom-call(f32[512,512]{1,0:T(8,128)} %diag.3, f32[64,512]{1,0:T(8,128)} %bitcast.2, f32[64,512]{1,0:T(8,128)} %bitcast.4, f32[512,512]{1,0:T(8,128)} %sides.3), custom_call_target="tpu_custom_call" | custom-call | tf_op jit(solution)/shard_map/pallas_call | solution.py:22
  1.8 3.1 %collective-permute-start = (f32[64,640]{1,0:T(8,128)S(1)}, f32[64,640]{1,0:T(8,128)S(1)}, u32[]{:S(2)}, u32[]{:S(2)}) collective-permute-start(f32[64,640]{1,0:T(8,128)S(1)} %get-tuple-element.32), channel_id=1, source_target_pairs={{0,16},{1,2},{2,1},{3,4},{4,3},{5,6},{6,5},{7,8},{8,7},{9,10},{10,... | collective-permute-start | bytes 491528 | tf_op jit(solution)/shard_map/ppermute | solution.py:221
  5.0 2.9 %shard_map.60 = (bf16[512,1536]{1,0:T(8,128)(2,1)S(1)}, bf16[512,384]{1,0:T(8,128)(2,1)S(1)}, bf16[64,192]{1,0:T(8,128)(2,1)S(1)}, f32[512,128]{1,0:T(8,128)S(1)...) custom-call(f32[512,512]{1,0:T(8,128)} %diag.3, ...), custom_call_target="tpu_custom_call" | custom-call | flops 805306368 | tf_op jit(solution)/shard_map/pallas_call | solution.py:22
  8.1 1.6 %collective-permute-start.4 = (f32[64,512]{1,0:T(8,128)S(1)}, f32[64,512]{1,0:T(8,128)S(1)}, u32[]{:S(2)}, u32[]{:S(2)}) collective-permute-start(f32[64,512]{1,0:T(8,128)S(1)} %shard_map.66), channel_id=1, source_target_pairs={{0,16},{1,2},{2,1},{3,4},{4,3},{5,6},{6,5},{7,8},{8,7},{9,10},{10,... | collective-permute-start | bytes 393224 | tf_op jit(solution)/shard_map/ppermute | solution.py:221
  10.1 1.4 %shard_map.61 = (f32[512,512]{1,0:T(8,128)S(1)}, f32[512,512]{1,0:T(8,128)S(1)}, f32[8,512]{1,0:T(8,128)S(1)}) custom-call(f32[64,640]{1,0:T(8,128)S(1)} %collective-permute-done.refs_0_.refs_1_.refs_2_.opened, f32[64,640]{1,0:T(8,128)S(1)} %collective-permute-done.refs_0_.refs_1_.refs_2_.opened, f32[64,512]{1,0:T(8,128)S(1)} %collective-permute-done.1.refs_2_.inner, ...), custom_call_target="tpu_custom_call" | custom-call | flops 1006632960 | tf_op jit(solution)/shard_map/pallas_call | solution.py:22
  11.5 1.6 %collective-permute-done.4.refs_1_ = f32[64,512]{1,0:T(8,128)S(1)} collective-permute-done((f32[64,512]{1,0:T(8,128)S(1)}, f32[64,512]{1,0:T(8,128)S(1)}, u32[]{:S(2)}, u32[]{:S(2)}) %collective-permute-start.4) | collective-permute-done | bytes 131104 | tf_op jit(solution)/shard_map/ppermute | solution.py:221
  13.9 1.5 %collective-permute-start.3 = (f32[64,512]{1,0:T(8,128)S(1)}, f32[64,512]{1,0:T(8,128)S(1)}, u32[]{:S(2)}, u32[]{:S(2)}) collective-permute-start(f32[64,512]{1,0:T(8,128)S(1)} %shard_map.64), channel_id=1, source_target_pairs={{0,16},{1,2},{2,1},{3,4},{4,3},{5,6},{6,5},{7,8},{8,7},{9,10},{10,... | collective-permute-start | bytes 393224 | tf_op jit(solution)/shard_map/ppermute | solution.py:221
  15.4 1.6 %shard_map.68 = (f32[512,512]{1,0:T(8,128)S(1)}, f32[512,512]{1,0:T(8,128)S(1)}, f32[8,512]{1,0:T(8,128)S(1)}) custom-call(f32[64,512]{1,0:T(8,128)S(1)} %shard_map.65.refs_0_, f32[64,512]{1,0:T(8,128)S(1)} %collective-permute-done.4.refs_1_, f32[64,640]{1,0:T(8,128)S(1)} %collective-permute-done.refs_0_.refs_1_.refs_2_.opened, ...), custom_call_target="tpu_custom_call" | custom-call | flops 1006632960 | tf_op jit(solution)/shard_map/pallas_call | solution.py:22
  17.8 1.1 %collective-permute-done.3.refs_1_ = f32[64,512]{1,0:T(8,128)S(1)} collective-permute-done((f32[64,512]{1,0:T(8,128)S(1)}, f32[64,512]{1,0:T(8,128)S(1)}, u32[]{:S(2)}, u32[]{:S(2)}) %collective-permute-start.3) | collective-permute-done | bytes 131104 | tf_op jit(solution)/shard_map/ppermute | solution.py:221
  19.5 1.6 %shard_map.69 = (f32[512,512]{1,0:T(8,128)S(1)}, f32[512,512]{1,0:T(8,128)S(1)}, f32[8,512]{1,0:T(8,128)S(1)}) custom-call(f32[64,512]{1,0:T(8,128)S(1)} %shard_map.62.refs_0_, f32[64,512]{1,0:T(8,128)S(1)} %collective-permute-done.3.refs_1_, f32[64,640]{1,0:T(8,128)S(1)} %collective-permute-done.refs_0_.refs_1_.refs_2_.opened, ...), custom_call_target="tpu_custom_call" | custom-call | flops 1006632960 | tf_op jit(solution)/shard_map/pallas_call | solution.py:22
  23.2 1.6 %collective-permute-start.7 = (f32[64,512]{1,0:T(8,128)S(1)}, f32[64,512]{1,0:T(8,128)S(1)}, u32[]{:S(2)}, u32[]{:S(2)}) collective-permute-start(f32[64,512]{1,0:T(8,128)S(1)} %shard_map.72), channel_id=1, source_target_pairs={{0,16},{1,2},{2,1},{3,4},{4,3},{5,6},{6,5},{7,8},{8,7},{9,10},{10,... | collective-permute-start | bytes 393224 | tf_op jit(solution)/shard_map/ppermute | solution.py:221
  24.8 1.6 %shard_map.76 = (f32[512,512]{1,0:T(8,128)S(1)}, f32[512,512]{1,0:T(8,128)S(1)}, f32[8,512]{1,0:T(8,128)S(1)}) custom-call(f32[64,512]{1,0:T(8,128)S(1)} %shard_map.73.refs_0_, f32[64,512]{1,0:T(8,128)S(1)} %collective-permute-done.8.refs_1_, f32[64,640]{1,0:T(8,128)S(1)} %collective-permute-done.refs_0_.refs_1_.refs_2_.opened, ...), custom_call_target="tpu_custom_call" | custom-call | flops 1006632960 | tf_op jit(solution)/shard_map/pallas_call | solution.py:22
  27.2 1.1 %collective-permute-done.7.refs_1_ = f32[64,512]{1,0:T(8,128)S(1)} collective-permute-done((f32[64,512]{1,0:T(8,128)S(1)}, f32[64,512]{1,0:T(8,128)S(1)}, u32[]{:S(2)}, u32[]{:S(2)}) %collective-permute-start.7) | collective-permute-done | bytes 131104 | tf_op jit(solution)/shard_map/ppermute | solution.py:221
  28.9 1.6 %shard_map.77 = (f32[512,512]{1,0:T(8,128)S(1)}, f32[512,512]{1,0:T(8,128)S(1)}, f32[8,512]{1,0:T(8,128)S(1)}) custom-call(f32[64,512]{1,0:T(8,128)S(1)} %shard_map.70.refs_0_, f32[64,512]{1,0:T(8,128)S(1)} %collective-permute-done.7.refs_1_, f32[64,640]{1,0:T(8,128)S(1)} %collective-permute-done.refs_0_.refs_1_.refs_2_.opened, ...), custom_call_target="tpu_custom_call" | custom-call | flops 1006632960 | tf_op jit(solution)/shard_map/pallas_call | solution.py:22
  30.5 1.1 %collective-permute-done.12.refs_1_ = f32[64,512]{1,0:T(8,128)S(1)} collective-permute-done((f32[64,512]{1,0:T(8,128)S(1)}, f32[64,512]{1,0:T(8,128)S(1)}, u32[]{:S(2)}, u32[]{:S(2)}) %collective-permute-start.12) | collective-permute-done | bytes 131104 | tf_op jit(solution)/shard_map/ppermute | solution.py:221
  32.6 1.6 %collective-permute-start.11 = (f32[64,512]{1,0:T(8,128)S(1)}, f32[64,512]{1,0:T(8,128)S(1)}, u32[]{:S(2)}, u32[]{:S(2)}) collective-permute-start(f32[64,512]{1,0:T(8,128)S(1)} %shard_map.80), channel_id=1, source_target_pairs={{0,16},{1,2},{2,1},{3,4},{4,3},{5,6},{6,5},{7,8},{8,7},{9,10},{10,... | collective-permute-start | bytes 393224 | tf_op jit(solution)/shard_map/ppermute | solution.py:221
  34.3 1.6 %shard_map.84 = (f32[512,512]{1,0:T(8,128)S(1)}, f32[512,512]{1,0:T(8,128)S(1)}, f32[8,512]{1,0:T(8,128)S(1)}) custom-call(f32[64,512]{1,0:T(8,128)S(1)} %shard_map.81.refs_0_, f32[64,512]{1,0:T(8,128)S(1)} %collective-permute-done.12.refs_1_, f32[64,640]{1,0:T(8,128)S(1)} %collective-permute-done.refs_0_.refs_1_.refs_2_.opened, ...), custom_call_target="tpu_custom_call" | custom-call | flops 1006632960 | tf_op jit(solution)/shard_map/pallas_call | solution.py:22
  35.8 1.8 %collective-permute-done.11.message = f32[64,512]{1,0:T(8,128)S(1)} collective-permute-done((f32[64,512]{1,0:T(8,128)S(1)}, f32[64,512]{1,0:T(8,128)S(1)}, u32[]{:S(2)}, u32[]{:S(2)}) %collective-permute-start.11) | collective-permute-done | bytes 131104 | tf_op jit(solution)/shard_map/ppermute | solution.py:221
  40.0 3.1 %collective-permute-start.15 = (f32[8,512]{1,0:T(8,128)S(1)}, f32[8,512]{1,0:T(8,128)S(1)}, u32[]{:S(2)}, u32[]{:S(2)}) collective-permute-start(f32[8,512]{1,0:T(8,128)S(1)} %add.12), channel_id=1, source_target_pairs={{0,3},{1,2},{2,1},{3,0},{4,7},{5,6},{6,5},{7,4},{8,11},{9,10},{10,... | collective-permute-start | bytes 49160 | tf_op jit(solution)/shard_map/ppermute | solution.py:234
  43.2 1.4 %collective-permute-done.15 = f32[8,512]{1,0:T(8,128)S(1)} collective-permute-done((f32[8,512]{1,0:T(8,128)S(1)}, f32[8,512]{1,0:T(8,128)S(1)}, u32[]{:S(2)}, u32[]{:S(2)}) %collective-permute-start.15) | collective-permute-done | bytes 16416 | tf_op jit(solution)/shard_map/ppermute | solution.py:234
  44.6 1.6 %collective-permute-start.16 = (f32[8,512]{1,0:T(8,128)S(1)}, f32[8,512]{1,0:T(8,128)S(1)}, u32[]{:S(2)}, u32[]{:S(2)}) collective-permute-start(f32[8,512]{1,0:T(8,128)S(1)} %add.13), channel_id=1, source_target_pairs={{0,5},{1,4},{2,7},{3,6},{4,1},{5,0},{6,3},{7,2},{8,13},{9,12},{10,... | collective-permute-start | bytes 49160 | tf_op jit(solution)/shard_map/ppermute | solution.py:234
  46.2 1.6 %collective-permute-done.16 = f32[8,512]{1,0:T(8,128)S(1)} collective-permute-done((f32[8,512]{1,0:T(8,128)S(1)}, f32[8,512]{1,0:T(8,128)S(1)}, u32[]{:S(2)}, u32[]{:S(2)}) %collective-permute-start.16) | collective-permute-done | bytes 16416 | tf_op jit(solution)/shard_map/ppermute | solution.py:234
  47.8 2.6 %collective-permute-start.17 = (f32[8,512]{1,0:T(8,128)S(1)}, f32[8,512]{1,0:T(8,128)S(1)}, u32[]{:S(2)}, u32[]{:S(2)}) collective-permute-start(f32[8,512]{1,0:T(8,128)S(1)} %add.14), channel_id=1, source_target_pairs={{0,9},{1,8},{2,11},{3,10},{4,13},{5,12},{6,15},{7,14},{8,1},{9,0},... | collective-permute-start | bytes 49160 | tf_op jit(solution)/shard_map/ppermute | solution.py:234
  50.4 1.1 %shard_map.86 = f32[512,512]{1,0:T(8,128)} custom-call(f32[512,512]{1,0:T(8,128)S(1)} %get-tuple-element.59.r, f32[512,512]{1,0:T(8,128)S(1)} %get-tuple-element.60.x, f32[512,128]{1,0:T(8,128)S(1)} %get-tuple-element.39.refs_8_.refs_6_.pivots.refs_7_.refs_9_), custom_call_target="tpu_custom_call" | custom-call | flops 2621440 | tf_op jit(solution)/shard_map/pallas_call | solution.py:22
  (44 shorter events, 10.8 us)
Async XLA Ops:
  1.8 7.8 %collective-permute-start = (f32[64,640]{1,0:T(8,128)S(1)}, f32[64,640]{1,0:T(8,128)S(1)}, u32[]{:S(2)}, u32[]{:S(2)}) collective-permute-start(f32[64,640]{1,0:T(8,128)S(1)} %get-tuple-element.32), channel_id=1, source_target_pairs={{0,16},{1,2},{2,1},{3,4},{4,3},{5,6},{6,5},{7,8},{8,7},{9,10},{10,... | collective-permute-start | bytes 491528 | tf_op jit(solution)/shard_map/ppermute | solution.py:221
  4.9 3.0 %collective-permute-start.1 = (f32[64,512]{1,0:T(8,128)S(1)}, f32[64,512]{1,0:T(8,128)S(1)}, u32[]{:S(2)}, u32[]{:S(2)}) collective-permute-start(f32[64,512]{1,0:T(8,128)S(1)} %get-tuple-element.33), channel_id=1, source_target_pairs={{0,1},{1,0},{2,3},{3,2},{4,5},{5,4},{6,7},{7,6},{8,9},{9,8},{10,11... | collective-permute-start | bytes 393224 | tf_op jit(solution)/shard_map/ppermute | solution.py:225
  8.1 5.0 %collective-permute-start.4 = (f32[64,512]{1,0:T(8,128)S(1)}, f32[64,512]{1,0:T(8,128)S(1)}, u32[]{:S(2)}, u32[]{:S(2)}) collective-permute-start(f32[64,512]{1,0:T(8,128)S(1)} %shard_map.66), channel_id=1, source_target_pairs={{0,16},{1,2},{2,1},{3,4},{4,3},{5,6},{6,5},{7,8},{8,7},{9,10},{10,... | collective-permute-start | bytes 393224 | tf_op jit(solution)/shard_map/ppermute | solution.py:221
  9.9 3.2 %collective-permute-start.2 = (f32[64,512]{1,0:T(8,128)S(1)}, f32[64,512]{1,0:T(8,128)S(1)}, u32[]{:S(2)}, u32[]{:S(2)}) collective-permute-start(f32[64,512]{1,0:T(8,128)S(1)} %shard_map.63), channel_id=1, source_target_pairs={{0,1},{1,0},{2,3},{3,2},{4,5},{5,4},{6,7},{7,6},{8,9},{9,8},{10,11... | collective-permute-start | bytes 393224 | tf_op jit(solution)/shard_map/ppermute | solution.py:225
  13.5 3.4 %collective-permute-start.5 = (f32[64,512]{1,0:T(8,128)S(1)}, f32[64,512]{1,0:T(8,128)S(1)}, u32[]{:S(2)}, u32[]{:S(2)}) collective-permute-start(f32[64,512]{1,0:T(8,128)S(1)} %shard_map.67), channel_id=1, source_target_pairs={{0,1},{1,0},{2,3},{3,2},{4,5},{5,4},{6,7},{7,6},{8,9},{9,8},{10,11... | collective-permute-start | bytes 393224 | tf_op jit(solution)/shard_map/ppermute | solution.py:225
  13.9 5.0 %collective-permute-start.3 = (f32[64,512]{1,0:T(8,128)S(1)}, f32[64,512]{1,0:T(8,128)S(1)}, u32[]{:S(2)}, u32[]{:S(2)}) collective-permute-start(f32[64,512]{1,0:T(8,128)S(1)} %shard_map.64), channel_id=1, source_target_pairs={{0,16},{1,2},{2,1},{3,4},{4,3},{5,6},{6,5},{7,8},{8,7},{9,10},{10,... | collective-permute-start | bytes 393224 | tf_op jit(solution)/shard_map/ppermute | solution.py:221
  17.1 5.0 %collective-permute-start.8 = (f32[64,512]{1,0:T(8,128)S(1)}, f32[64,512]{1,0:T(8,128)S(1)}, u32[]{:S(2)}, u32[]{:S(2)}) collective-permute-start(f32[64,512]{1,0:T(8,128)S(1)} %shard_map.74), channel_id=1, source_target_pairs={{0,16},{1,2},{2,1},{3,4},{4,3},{5,6},{6,5},{7,8},{8,7},{9,10},{10,... | collective-permute-start | bytes 393224 | tf_op jit(solution)/shard_map/ppermute | solution.py:221
  19.3 2.9 %collective-permute-start.6 = (f32[64,512]{1,0:T(8,128)S(1)}, f32[64,512]{1,0:T(8,128)S(1)}, u32[]{:S(2)}, u32[]{:S(2)}) collective-permute-start(f32[64,512]{1,0:T(8,128)S(1)} %shard_map.71), channel_id=1, source_target_pairs={{0,1},{1,0},{2,3},{3,2},{4,5},{5,4},{6,7},{7,6},{8,9},{9,8},{10,11... | collective-permute-start | bytes 393224 | tf_op jit(solution)/shard_map/ppermute | solution.py:225
  22.6 3.8 %collective-permute-start.9 = (f32[64,512]{1,0:T(8,128)S(1)}, f32[64,512]{1,0:T(8,128)S(1)}, u32[]{:S(2)}, u32[]{:S(2)}) collective-permute-start(f32[64,512]{1,0:T(8,128)S(1)} %shard_map.75), channel_id=1, source_target_pairs={{0,1},{1,0},{2,3},{3,2},{4,5},{5,4},{6,7},{7,6},{8,9},{9,8},{10,11... | collective-permute-start | bytes 393224 | tf_op jit(solution)/shard_map/ppermute | solution.py:225
  23.2 5.0 %collective-permute-start.7 = (f32[64,512]{1,0:T(8,128)S(1)}, f32[64,512]{1,0:T(8,128)S(1)}, u32[]{:S(2)}, u32[]{:S(2)}) collective-permute-start(f32[64,512]{1,0:T(8,128)S(1)} %shard_map.72), channel_id=1, source_target_pairs={{0,16},{1,2},{2,1},{3,4},{4,3},{5,6},{6,5},{7,8},{8,7},{9,10},{10,... | collective-permute-start | bytes 393224 | tf_op jit(solution)/shard_map/ppermute | solution.py:221
  26.6 5.0 %collective-permute-start.12 = (f32[64,512]{1,0:T(8,128)S(1)}, f32[64,512]{1,0:T(8,128)S(1)}, u32[]{:S(2)}, u32[]{:S(2)}) collective-permute-start(f32[64,512]{1,0:T(8,128)S(1)} %shard_map.82), channel_id=1, source_target_pairs={{0,16},{1,2},{2,1},{3,4},{4,3},{5,6},{6,5},{7,8},{8,7},{9,10},{10,... | collective-permute-start | bytes 393224 | tf_op jit(solution)/shard_map/ppermute | solution.py:221
  28.7 3.0 %collective-permute-start.10 = (f32[64,512]{1,0:T(8,128)S(1)}, f32[64,512]{1,0:T(8,128)S(1)}, u32[]{:S(2)}, u32[]{:S(2)}) collective-permute-start(f32[64,512]{1,0:T(8,128)S(1)} %shard_map.79), channel_id=1, source_target_pairs={{0,1},{1,0},{2,3},{3,2},{4,5},{5,4},{6,7},{7,6},{8,9},{9,8},{10,11... | collective-permute-start | bytes 393224 | tf_op jit(solution)/shard_map/ppermute | solution.py:225
  32.0 3.8 %collective-permute-start.13 = (f32[64,512]{1,0:T(8,128)S(1)}, f32[64,512]{1,0:T(8,128)S(1)}, u32[]{:S(2)}, u32[]{:S(2)}) collective-permute-start(f32[64,512]{1,0:T(8,128)S(1)} %shard_map.83), channel_id=1, source_target_pairs={{0,1},{1,0},{2,3},{3,2},{4,5},{5,4},{6,7},{7,6},{8,9},{9,8},{10,11... | collective-permute-start | bytes 393224 | tf_op jit(solution)/shard_map/ppermute | solution.py:225
  32.6 5.0 %collective-permute-start.11 = (f32[64,512]{1,0:T(8,128)S(1)}, f32[64,512]{1,0:T(8,128)S(1)}, u32[]{:S(2)}, u32[]{:S(2)}) collective-permute-start(f32[64,512]{1,0:T(8,128)S(1)} %shard_map.80), channel_id=1, source_target_pairs={{0,16},{1,2},{2,1},{3,4},{4,3},{5,6},{6,5},{7,8},{8,7},{9,10},{10,... | collective-permute-start | bytes 393224 | tf_op jit(solution)/shard_map/ppermute | solution.py:221
  38.3 1.7 %collective-permute-start.14 = (f32[8,512]{1,0:T(8,128)S(1)}, f32[8,512]{1,0:T(8,128)S(1)}, u32[]{:S(2)}, u32[]{:S(2)}) collective-permute-start(f32[8,512]{1,0:T(8,128)S(1)} %get-tuple-element.61), channel_id=1, source_target_pairs={{0,1},{1,0},{2,3},{3,2},{4,5},{5,4},{6,7},{7,6},{8,9},{9,8},{10,11... | collective-permute-start | bytes 49160 | tf_op jit(solution)/shard_map/ppermute | solution.py:234
  40.0 4.6 %collective-permute-start.15 = (f32[8,512]{1,0:T(8,128)S(1)}, f32[8,512]{1,0:T(8,128)S(1)}, u32[]{:S(2)}, u32[]{:S(2)}) collective-permute-start(f32[8,512]{1,0:T(8,128)S(1)} %add.12), channel_id=1, source_target_pairs={{0,3},{1,2},{2,1},{3,0},{4,7},{5,6},{6,5},{7,4},{8,11},{9,10},{10,... | collective-permute-start | bytes 49160 | tf_op jit(solution)/shard_map/ppermute | solution.py:234
  44.6 3.2 %collective-permute-start.16 = (f32[8,512]{1,0:T(8,128)S(1)}, f32[8,512]{1,0:T(8,128)S(1)}, u32[]{:S(2)}, u32[]{:S(2)}) collective-permute-start(f32[8,512]{1,0:T(8,128)S(1)} %add.13), channel_id=1, source_target_pairs={{0,5},{1,4},{2,7},{3,6},{4,1},{5,0},{6,3},{7,2},{8,13},{9,12},{10,... | collective-permute-start | bytes 49160 | tf_op jit(solution)/shard_map/ppermute | solution.py:234
  47.8 4.1 %collective-permute-start.17 = (f32[8,512]{1,0:T(8,128)S(1)}, f32[8,512]{1,0:T(8,128)S(1)}, u32[]{:S(2)}, u32[]{:S(2)}) collective-permute-start(f32[8,512]{1,0:T(8,128)S(1)} %add.14), channel_id=1, source_target_pairs={{0,9},{1,8},{2,11},{3,10},{4,13},{5,12},{6,15},{7,14},{8,1},{9,0},... | collective-permute-start | bytes 49160 | tf_op jit(solution)/shard_map/ppermute | solution.py:234

commit v3 on v2

--- a/solution.py
+++ b/solution.py
@@ -79,7 +79,7 @@
 
 
 def open_kernel(diag, lower, upper, sides, outer_out, inner_out, corners, strips, low, up, sems):
-    odd, end = place()
+    odd, _ = place()
     rows, columns = sides.shape
     width, lanes = corners.shape[1:]
     top = rows - width
@@ -100,104 +100,113 @@
     first = strips[0] / head
     last = strips[1] / tail
     outer_out[:, :columns] = facing(jnp.where(odd == 1, last, first))
-    coupling = facing(jnp.where(odd == 1, up[...].T[lanes - width :], low[...].T[:width]))
-    pivots = jnp.where(end, 1.0, jnp.where(odd == 1, tail, head))
-    outer_out[:, columns:] = jnp.concatenate([coupling, jnp.broadcast_to(pivots, coupling.shape)], axis=1)
+    coupling = jnp.where(odd == 1, up[...].T[lanes - width :] / tail, low[...].T[:width] / head)
+    outer_out[:, columns:] = jnp.concatenate([facing(coupling), jnp.zeros_like(coupling)], axis=1)
     inner_out[...] = jnp.where(odd == 1, first, last)
 
 
-def setup_kernel(diag, lower, upper, sides, diag_out, coupling_out, near_out, pivot_out, side_out, x_out, v_out, sums_out, block, low, up, sems):
-    odd, _ = place()
-    width, rows = low.shape
+def setup_kernel(diag, lower, upper, sides, diag_out, outer_out, inner_out, scale_out, side_out, x_out, terms_out, v_out, sums_out, block, low, up, sems):
+    odd, _ = place()
+    _, rows = low.shape
     moves = copies([(sides, side_out), (diag, block), (lower, low), (upper, up)], sems)
     moves[0].wait()
     side = side_out[...]
     sums_out[0:1, :] = jnp.sum(side * side, axis=0, keepdims=True)
     moves[1].wait()
-    pivots = diagonal(block[...], 0)
-    pivot_out[...] = jnp.broadcast_to(pivots, pivot_out.shape)
-    x = side / pivots
+    scale = 1.0 / diagonal(block[...], 0)
+    scale_out[...] = jnp.broadcast_to(scale, scale_out.shape)
+    x = side * scale
     x_out[...] = x
-    left = left_terms(block[...])
-    diag_out[...] = left
-    v_out[...] = side - product(left, right_terms(x))
+    terms_out[...] = right_terms(x)
+    diag_out[...] = left_terms(block[...])
+    far, _ = spans(rows)
+    v_out[...] = applied(side_out, diag_out, terms_out, far)
     moves[2].wait()
     moves[3].wait()
-    outer = jnp.where(odd == 1, up[...], low[...])
-    inner = jnp.where(odd == 1, low[...], up[...])
-    coupling = jnp.concatenate([outer, inner], axis=0).T
-    coupling_out[...] = left_terms(coupling)
-    top = rows - width
-    inner = coupling[:, width:]
-    near_out[...] = left_terms(jnp.where(odd == 1, inner[top:, :], inner[:width, :]))
+    low, up = low[...], up[...]
+    outer_out[...] = left_terms(jnp.where(odd == 1, up, low).T)
+    inner_out[...] = left_terms(jnp.where(odd == 1, low, up).T)
+
+
+def spans(rows):
+    odd, _ = place()
+    half = rows // 2
+    return pl.multiple_of(odd * half, half), pl.multiple_of((1 - odd) * half, half)
+
+
+def applied(side, diag, terms, start):
+    some = pl.ds(start, side.shape[0] // 2)
+    return side[some, :] - product(diag[some, :], terms[...])
 
 
 def wide(pivots, columns):
     return jnp.concatenate([pivots] * (columns // pivots.shape[1]), axis=1)
 
 
-def send_kernel(inner, x, v, near, pivots, outer_out):
+def send_kernel(inner, x, v, coupling, scale, outer_out):
+    odd, _ = place()
     rows, columns = x.shape
     width = inner.shape[0]
     far, _ = rims(rows, width)
-    pick = lambda ref: ref[pl.ds(far, width), :]
-    residual = pick(v) - product(near[...], right_terms(inner[...]))
-    outer_out[...] = facing(pick(x) + residual / wide(pick(pivots), columns))
-
-
-def outer_halo(message, opened, mine):
-    if mine is None:
-        return message[:, : opened.shape[1] - 128]
-    columns = message.shape[1]
-    width = message.shape[0]
-    extra = opened[:, columns:]
-    term = product(left_terms(extra[:, :width]), right_terms(mine[...]))
-    return message[...] - term / extra[:, width : width + 1]
-
-
-def halo_terms(message, opened, mine, inner):
-    return right_terms(jnp.concatenate([outer_halo(message, opened, mine), inner[...]], axis=0))
-
-
-def keep_kernel(x, outer_out):
-    far, _ = rims(x.shape[0], outer_out.shape[0])
-    outer_out[...] = x[pl.ds(far, outer_out.shape[0]), :]
+    rim = pl.ds(far, width)
+    inside = pl.ds(pl.multiple_of(odd * (v.shape[0] - width), width), width)
+    residual = v[inside, :] - product(coupling[rim, :], right_terms(inner[...]))
+    outer_out[...] = facing(x[rim, :] + residual * wide(scale[rim, :], columns))
+
+
+def fill_kernel(inner, terms, v, side, diag, coupling, u_out):
+    far, near = spans(side.shape[0])
+    half = v.shape[0]
+    halo = right_terms(inner[...])
+    u_out[pl.ds(far, half), :] = v[...] - product(coupling[pl.ds(far, half), :], halo)
+    u_out[pl.ds(near, half), :] = applied(side, diag, terms, near) - product(coupling[pl.ds(near, half), :], halo)
+
+
+def outer_halo(message, correction):
+    if correction is None:
+        return message[:, : message.shape[1] - 128]
+    return message[...] - correction[...]
 
 
 def rim_kernel(*refs, first):
     refs = list(refs)
-    mine = None if first else refs.pop(0)
-    message, opened, inner, x, v, coupling, pivots, inner_out = refs
+    correction = None if first else refs.pop(0)
+    message, x, u, coupling, scale, halo_out, inner_out = refs
     rows, columns = x.shape
-    width = inner.shape[0]
+    width = inner_out.shape[0]
     _, near = rims(rows, width)
-    pick = lambda ref: ref[pl.ds(near, width), :]
-    residual = pick(v) - product(pick(coupling), halo_terms(message, opened, mine, inner))
-    inner_out[...] = pick(x) + residual / wide(pick(pivots), columns)
-
-
-def sweep_kernel(*refs, sweep, first):
-    refs = list(refs)
-    mine = None if first else refs.pop(0)
-    message, opened, inner, x, v, side, diag, coupling, pivots, sums, x_out, v_out, sums_out = refs
-    _, columns = x.shape
+    rim = pl.ds(near, width)
+    halo = right_terms(outer_halo(message, correction))
+    halo_out[...] = halo
+    residual = u[rim, :] - product(coupling[rim, :], halo)
+    inner_out[...] = x[rim, :] + residual * wide(scale[rim, :], columns)
+
+
+def sweep_kernel(halo, opened, x, terms, u, side, diag, coupling, scale, sums, x_out, terms_out, v_out, correction_out, sums_out, *, sweep):
+    rows, columns = x.shape
+    width = opened.shape[0]
+    far, _ = rims(rows, width)
+    mine = jnp.concatenate([terms[pl.ds(far + part * rows, width), :] for part in range(3)], axis=0)
+    correction_out[...] = product(left_terms(opened[:, columns : columns + width]), mine)
     sums_out[...] = sums[...]
-    residual = v[...] - product(coupling[...], halo_terms(message, opened, mine, inner))
+    residual = u[...] - product(coupling[...], halo[...])
     sums_out[sweep : sweep + 1, :] = jnp.sum(residual * residual, axis=0, keepdims=True)
-    new = x[...] + residual / wide(pivots[...], columns)
+    new = x[...] + residual * wide(scale[...], columns)
     x_out[...] = new
-    v_out[...] = side[...] - product(diag[...], right_terms(new))
-
-
-def last_kernel(mine, message, opened, inner, v, coupling, sums, r_out, sums_out, *, sweep):
+    terms_out[...] = right_terms(new)
+    start, _ = spans(rows)
+    v_out[...] = applied(side, diag, terms_out, start)
+
+
+def last_kernel(correction, message, u, coupling, sums, r_out, sums_out, *, sweep):
     sums_out[...] = sums[...]
-    residual = v[...] - product(coupling[...], halo_terms(message, opened, mine, inner))
+    residual = u[...] - product(coupling[...], right_terms(outer_halo(message, correction)))
     sums_out[sweep : sweep + 1, :] = jnp.sum(residual * residual, axis=0, keepdims=True)
     r_out[...] = residual
 
 
-def close_kernel(r, x, pivots, x_out):
-    x_out[...] = x[...] + r[...] / wide(pivots[...], x.shape[1])
+def close_kernel(r, x, scale, x_out):
+    x_out[...] = x[...] + r[...] * wide(scale[...], x.shape[1])
 
 
 def pairings():
@@ -259,16 +268,20 @@
     )
     opened = message = across(opened)
     inner = along(inner)
-    diag, coupling, near, pivots, side, x, v, sums = call(
+    half = pltpu.VMEM((rows // 2, columns), F32)
+    all_terms = pltpu.VMEM((3 * rows, columns), BF16)
+    coupling_shape = pltpu.VMEM((rows, 3 * width), BF16)
+    diag, outward, inward, scale, side, x, terms, v, sums = call(
         setup_kernel,
         [
             pltpu.VMEM((rows, 3 * rows), BF16),
-            pltpu.VMEM((rows, 6 * width), BF16),
-            pltpu.VMEM((width, 3 * width), BF16),
+            coupling_shape,
+            coupling_shape,
             pltpu.VMEM((rows, lanes), F32),
             panel,
             panel,
-            panel,
+            all_terms,
+            half,
             sums_shape,
         ],
         diag_blocks, lower, upper, right_sides,
@@ -279,33 +292,42 @@
             pltpu.VMEM((width, rows), F32),
             pltpu.SemaphoreType.DMA((4,)),
         ],
-        flops=6 * rows * rows * columns,
-    )
-    mine = []
-    for sweep in range(1, SWEEPS - 1):
-        sent = call(send_kernel, rim, inner, x, v, near, pivots, flops=6 * width * width * columns)
-        ahead = across(sent)
-        kept = call(keep_kernel, rim, x)
-        rim_values = call(
+        flops=3 * rows * rows * columns,
+    )
+    correction = []
+    for sweep in range(1, SWEEPS):
+        if sweep < SWEEPS - 1:
+            sent = call(send_kernel, rim, inner, x, v, inward, scale, flops=6 * width * width * columns)
+            ahead = across(sent)
+        u = call(
+            fill_kernel,
+            panel,
+            inner, terms, v, side, diag, inward,
+            flops=3 * rows * (rows + 2 * width) * columns,
+        )
+        if sweep == SWEEPS - 1:
+            break
+        halo, rim_values = call(
             functools.partial(rim_kernel, first=sweep == 1),
-            rim,
-            *mine, message, opened, inner, x, v, coupling, pivots,
-            flops=18 * width * width * columns,
+            [pltpu.VMEM((3 * width, columns), BF16), rim],
+            *correction, message, x, u, outward, scale,
+            flops=6 * width * width * columns,
         )
-        x, v, sums = call(
-            functools.partial(sweep_kernel, sweep=sweep, first=sweep == 1),
-            [panel, panel, sums_shape],
-            *mine, message, opened, inner, x, v, side, diag, coupling, pivots, sums,
-            flops=6 * rows * (rows + 2 * width) * columns,
+        inner = along(rim_values)
+        x, terms, v, kept, sums = call(
+            functools.partial(sweep_kernel, sweep=sweep),
+            [panel, all_terms, half, rim, sums_shape],
+            halo, opened, x, terms, u, side, diag, outward, scale, sums,
+            flops=3 * rows * (rows + 2 * width) * columns,
         )
-        mine, message, inner = [kept], ahead, along(rim_values)
+        correction, message = [kept], ahead
     r, sums = call(
         functools.partial(last_kernel, sweep=SWEEPS - 1),
         [panel, sums_shape],
-        *mine, message, opened, inner, v, coupling, sums,
-        flops=12 * rows * width * columns,
-    )
-    solution = call(close_kernel, jax.ShapeDtypeStruct((rows, columns), F32), r, x, pivots, flops=10 * rows * columns)
+        *correction, message, u, outward, sums,
+        flops=6 * rows * width * columns,
+    )
+    solution = call(close_kernel, jax.ShapeDtypeStruct((rows, columns), F32), r, x, scale, flops=10 * rows * columns)
     return solution, jnp.sqrt(row_sum(sums))
 
 

time: 52.6 us -> 60.6 us (1.15)
  starting transfers between devices: 20.5 us -> 26.6 us
  waiting for transfers between devices: 12.1 us -> 13.7 us
    ppermute x7, starting transfers between devices: 1.8 us -> 5.05 us  [along(): return lax.ppermute(inner, 'row', pairings()[0])]
    ppermute x7, starting transfers between devices: 10.6 us -> 12.4 us  [across(): return lax.ppermute(outer, ('grp', 'row'), pairings()[1])]
    ppermute x7, waiting for transfers between devices: 7.82 us -> 9.59 us  [across(): return lax.ppermute(outer, ('grp', 'row'), pairings()[1])]
    ppermute x4, starting transfers between devices: 8.14 us -> 9.14 us  [row_sum(): x = x + lax.ppermute(x, 'row', [(i, i ^ flip) for i in range(size)])]
    pallas_call x28 -> x29, Pallas kernels: 18.4 us -> 18.7 us  [call(): pl.pallas_call(kernel, out_shape=outs, in_specs=[HBM_BLOCK if i in hbm el...]
  transfers between devices with their start and end apart: 18 -> 18, of which waited for: 10 -> 10; matrix products, arithmetic and copies ran while one was open for 0% -> 0% of each run, Pallas kernels for 29% -> 27%
where the time goes in v3:
time: 60.6 us; the launch traced here: 60.4 us
  starting transfers between devices  26.6 us (44%)
  Pallas kernels  18.7 us (31%)
  waiting for transfers between devices  13.7 us (23%)
  between operations  0.85 us (1%)
  other arithmetic  0.63 us (1%)
    pallas_call x29, Pallas kernels, call(): pl.pallas_call(kernel, out_shape=outs, in_specs=[HBM_BLOCK if i in hbm el...  18.7 us
    ppermute x7, starting transfers between devices, across(): return lax.ppermute(outer, ('grp', 'row'), pairings()[1])  12.4 us
    ppermute x7, waiting for transfers between devices, across(): return lax.ppermute(outer, ('grp', 'row'), pairings()[1])  9.59 us
    ppermute x4, starting transfers between devices, row_sum(): x = x + lax.ppermute(x, 'row', [(i, i ^ flip) for i in range(size)])  9.14 us
    ppermute x7, starting transfers between devices, along(): return lax.ppermute(inner, 'row', pairings()[0])  5.05 us
    ppermute x4, waiting for transfers between devices, row_sum(): x = x + lax.ppermute(x, 'row', [(i, i ^ flip) for i in range(size)])  4.08 us
  transfers between devices with their start and end apart: 18, of which 10 were waited for; matrix products, arithmetic and copies ran while one was open for 0% of the time, Pallas kernels for 27%

profile of v3, /device:TPU:0, one launch (start us, length us, event | category | flops | bytes accessed | tf_op | source)
XLA Modules:
  0.0 60.4 jit_solution(16011531423421414927)
XLA Ops:
  0.6 1.2 %shard_map.59 = (f32[64,640]{1,0:T(8,128)S(1)}, f32[64,512]{1,0:T(8,128)S(1)}) custom-call(f32[512,512]{1,0:T(8,128)} %diag.3, f32[64,512]{1,0:T(8,128)} %bitcast.2, f32[64,512]{1,0:T(8,128)} %bitcast.4, f32[512,512]{1,0:T(8,128)} %sides.3), custom_call_target="tpu_custom_call" | custom-call | tf_op jit(solution)/shard_map/pallas_call | solution.py:22
  2.4 2.6 %collective-permute-start = (f32[64,640]{1,0:T(8,128)S(1)}, f32[64,640]{1,0:T(8,128)S(1)}, u32[]{:S(2)}, u32[]{:S(2)}) collective-permute-start(f32[64,640]{1,0:T(8,128)S(1)} %get-tuple-element.57), channel_id=1, source_target_pairs={{0,16},{1,2},{2,1},{3,4},{4,3},{5,6},{6,5},{7,8},{8,7},{9,10},{10,... | collective-permute-start | bytes 491528 | tf_op jit(solution)/shard_map/ppermute | solution.py:230
  5.0 2.8 %shard_map.60 = (bf16[512,1536]{1,0:T(8,128)(2,1)S(1)}, bf16[512,192]{1,0:T(8,128)(2,1)S(1)}, bf16[512,192]{1,0:T(8,128)(2,1)S(1)}, f32[512,128]{1,0:T(8,128)S(1...) custom-call(f32[512,512]{1,0:T(8,128)} %diag.3, ...), custom_call_target="tpu_custom_call" | custom-call | flops 402653184 | tf_op jit(solution)/shard_map/pallas_call | solution.py:22
  9.0 1.9 %collective-permute-start.2 = (f32[64,512]{1,0:T(8,128)S(1)}, f32[64,512]{1,0:T(8,128)S(1)}, u32[]{:S(2)}, u32[]{:S(2)}) collective-permute-start(f32[64,512]{1,0:T(8,128)S(1)} %shard_map.64), channel_id=1, source_target_pairs={{0,16},{1,2},{2,1},{3,4},{4,3},{5,6},{6,5},{7,8},{8,7},{9,10},{10,... | collective-permute-start | bytes 393224 | tf_op jit(solution)/shard_map/ppermute | solution.py:230
  10.9 1.1 %shard_map.63 = (f32[512,512]{1,0:T(8,128)S(1)}, bf16[1536,512]{1,0:T(8,128)(2,1)S(1)}, f32[256,512]{1,0:T(8,128)S(1)}, f32[64,512]{1,0:T(8,128)S(1)}, f32[8,512]{1,0:T(8,128)S(1)}) custom-call(bf16[192,512]{1,0:T(8,128)(2,1)S(1)} %get-tuple-element.67.halo, f32[64,640]{1,0:T(8,128)S(1)} %collective-permute-done.refs_0_.opened, ...), custom_call_target="tpu_custom_call" | custom-call | flops 503316480 | tf_op jit(solution)/shard_map/pallas_call | solution.py:22
  12.7 1.3 %collective-permute-done.2.refs_1_ = f32[64,512]{1,0:T(8,128)S(1)} collective-permute-done((f32[64,512]{1,0:T(8,128)S(1)}, f32[64,512]{1,0:T(8,128)S(1)}, u32[]{:S(2)}, u32[]{:S(2)}) %collective-permute-start.2) | collective-permute-done | bytes 131104 | tf_op jit(solution)/shard_map/ppermute | solution.py:230
  15.1 1.6 %collective-permute-start.4 = (f32[64,512]{1,0:T(8,128)S(1)}, f32[64,512]{1,0:T(8,128)S(1)}, u32[]{:S(2)}, u32[]{:S(2)}) collective-permute-start(f32[64,512]{1,0:T(8,128)S(1)} %shard_map.68), channel_id=1, source_target_pairs={{0,16},{1,2},{2,1},{3,4},{4,3},{5,6},{6,5},{7,8},{8,7},{9,10},{10,... | collective-permute-start | bytes 393224 | tf_op jit(solution)/shard_map/ppermute | solution.py:230
  18.5 1.7 %collective-permute-done.4.refs_1_ = f32[64,512]{1,0:T(8,128)S(1)} collective-permute-done((f32[64,512]{1,0:T(8,128)S(1)}, f32[64,512]{1,0:T(8,128)S(1)}, u32[]{:S(2)}, u32[]{:S(2)}) %collective-permute-start.4) | collective-permute-done | bytes 131104 | tf_op jit(solution)/shard_map/ppermute | solution.py:230
  21.4 1.6 %collective-permute-start.6 = (f32[64,512]{1,0:T(8,128)S(1)}, f32[64,512]{1,0:T(8,128)S(1)}, u32[]{:S(2)}, u32[]{:S(2)}) collective-permute-start(f32[64,512]{1,0:T(8,128)S(1)} %shard_map.72), channel_id=1, source_target_pairs={{0,16},{1,2},{2,1},{3,4},{4,3},{5,6},{6,5},{7,8},{8,7},{9,10},{10,... | collective-permute-start | bytes 393224 | tf_op jit(solution)/shard_map/ppermute | solution.py:230
  24.7 1.7 %collective-permute-done.6.refs_1_ = f32[64,512]{1,0:T(8,128)S(1)} collective-permute-done((f32[64,512]{1,0:T(8,128)S(1)}, f32[64,512]{1,0:T(8,128)S(1)}, u32[]{:S(2)}, u32[]{:S(2)}) %collective-permute-start.6) | collective-permute-done | bytes 131104 | tf_op jit(solution)/shard_map/ppermute | solution.py:230
  27.6 1.6 %collective-permute-start.8 = (f32[64,512]{1,0:T(8,128)S(1)}, f32[64,512]{1,0:T(8,128)S(1)}, u32[]{:S(2)}, u32[]{:S(2)}) collective-permute-start(f32[64,512]{1,0:T(8,128)S(1)} %shard_map.76), channel_id=1, source_target_pairs={{0,16},{1,2},{2,1},{3,4},{4,3},{5,6},{6,5},{7,8},{8,7},{9,10},{10,... | collective-permute-start | bytes 393224 | tf_op jit(solution)/shard_map/ppermute | solution.py:230
  29.2 1.1 %shard_map.75 = (f32[512,512]{1,0:T(8,128)S(1)}, bf16[1536,512]{1,0:T(8,128)(2,1)S(1)}, f32[256,512]{1,0:T(8,128)S(1)}, f32[64,512]{1,0:T(8,128)S(1)}, f32[8,512]{1,0:T(8,128)S(1)}) custom-call(bf16[192,512]{1,0:T(8,128)(2,1)S(1)} %get-tuple-element.88.halo, f32[64,640]{1,0:T(8,128)S(1)} %collective-permute-done.refs_0_.opened, ...), custom_call_target="tpu_custom_call" | custom-call | flops 503316480 | tf_op jit(solution)/shard_map/pallas_call | solution.py:22
  31.0 1.6 %collective-permute-done.8.refs_1_ = f32[64,512]{1,0:T(8,128)S(1)} collective-permute-done((f32[64,512]{1,0:T(8,128)S(1)}, f32[64,512]{1,0:T(8,128)S(1)}, u32[]{:S(2)}, u32[]{:S(2)}) %collective-permute-start.8) | collective-permute-done | bytes 131104 | tf_op jit(solution)/shard_map/ppermute | solution.py:230
  33.9 1.6 %collective-permute-start.10 = (f32[64,512]{1,0:T(8,128)S(1)}, f32[64,512]{1,0:T(8,128)S(1)}, u32[]{:S(2)}, u32[]{:S(2)}) collective-permute-start(f32[64,512]{1,0:T(8,128)S(1)} %shard_map.80), channel_id=1, source_target_pairs={{0,16},{1,2},{2,1},{3,4},{4,3},{5,6},{6,5},{7,8},{8,7},{9,10},{10,... | collective-permute-start | bytes 393224 | tf_op jit(solution)/shard_map/ppermute | solution.py:230
  37.3 1.7 %collective-permute-done.10.refs_1_ = f32[64,512]{1,0:T(8,128)S(1)} collective-permute-done((f32[64,512]{1,0:T(8,128)S(1)}, f32[64,512]{1,0:T(8,128)S(1)}, u32[]{:S(2)}, u32[]{:S(2)}) %collective-permute-start.10) | collective-permute-done | bytes 131104 | tf_op jit(solution)/shard_map/ppermute | solution.py:230
  40.2 1.6 %collective-permute-start.12 = (f32[64,512]{1,0:T(8,128)S(1)}, f32[64,512]{1,0:T(8,128)S(1)}, u32[]{:S(2)}, u32[]{:S(2)}) collective-permute-start(f32[64,512]{1,0:T(8,128)S(1)} %shard_map.84), channel_id=1, source_target_pairs={{0,16},{1,2},{2,1},{3,4},{4,3},{5,6},{6,5},{7,8},{8,7},{9,10},{10,... | collective-permute-start | bytes 393224 | tf_op jit(solution)/shard_map/ppermute | solution.py:230
  41.7 1.1 %shard_map.83 = (f32[512,512]{1,0:T(8,128)S(1)}, bf16[1536,512]{1,0:T(8,128)(2,1)S(1)}, f32[256,512]{1,0:T(8,128)S(1)}, f32[64,512]{1,0:T(8,128)S(1)}, f32[8,512]{1,0:T(8,128)S(1)}) custom-call(bf16[192,512]{1,0:T(8,128)(2,1)S(1)} %get-tuple-element.102.halo, f32[64,640]{1,0:T(8,128)S(1)} %collective-permute-done.refs_0_.opened, ...), custom_call_target="tpu_custom_call" | custom-call | flops 503316480 | tf_op jit(solution)/shard_map/pallas_call | solution.py:22
  43.5 1.6 %collective-permute-done.12.message = f32[64,512]{1,0:T(8,128)S(1)} collective-permute-done((f32[64,512]{1,0:T(8,128)S(1)}, f32[64,512]{1,0:T(8,128)S(1)}, u32[]{:S(2)}, u32[]{:S(2)}) %collective-permute-start.12) | collective-permute-done | bytes 131104 | tf_op jit(solution)/shard_map/ppermute | solution.py:230
  47.2 3.1 %collective-permute-start.15 = (f32[8,512]{1,0:T(8,128)S(1)}, f32[8,512]{1,0:T(8,128)S(1)}, u32[]{:S(2)}, u32[]{:S(2)}) collective-permute-start(f32[8,512]{1,0:T(8,128)S(1)} %add.12), channel_id=1, source_target_pairs={{0,3},{1,2},{2,1},{3,0},{4,7},{5,6},{6,5},{7,4},{8,11},{9,10},{10,... | collective-permute-start | bytes 49160 | tf_op jit(solution)/shard_map/ppermute | solution.py:243
  50.4 1.4 %collective-permute-done.15 = f32[8,512]{1,0:T(8,128)S(1)} collective-permute-done((f32[8,512]{1,0:T(8,128)S(1)}, f32[8,512]{1,0:T(8,128)S(1)}, u32[]{:S(2)}, u32[]{:S(2)}) %collective-permute-start.15) | collective-permute-done | bytes 16416 | tf_op jit(solution)/shard_map/ppermute | solution.py:243
  51.8 2.4 %collective-permute-start.16 = (f32[8,512]{1,0:T(8,128)S(1)}, f32[8,512]{1,0:T(8,128)S(1)}, u32[]{:S(2)}, u32[]{:S(2)}) collective-permute-start(f32[8,512]{1,0:T(8,128)S(1)} %add.13), channel_id=1, source_target_pairs={{0,5},{1,4},{2,7},{3,6},{4,1},{5,0},{6,3},{7,2},{8,13},{9,12},{10,... | collective-permute-start | bytes 49160 | tf_op jit(solution)/shard_map/ppermute | solution.py:243
  54.2 1.4 %collective-permute-done.16 = f32[8,512]{1,0:T(8,128)S(1)} collective-permute-done((f32[8,512]{1,0:T(8,128)S(1)}, f32[8,512]{1,0:T(8,128)S(1)}, u32[]{:S(2)}, u32[]{:S(2)}) %collective-permute-start.16) | collective-permute-done | bytes 16416 | tf_op jit(solution)/shard_map/ppermute | solution.py:243
  55.7 2.7 %collective-permute-start.17 = (f32[8,512]{1,0:T(8,128)S(1)}, f32[8,512]{1,0:T(8,128)S(1)}, u32[]{:S(2)}, u32[]{:S(2)}) collective-permute-start(f32[8,512]{1,0:T(8,128)S(1)} %add.14), channel_id=1, source_target_pairs={{0,9},{1,8},{2,11},{3,10},{4,13},{5,12},{6,15},{7,14},{8,1},{9,0},... | collective-permute-start | bytes 49160 | tf_op jit(solution)/shard_map/ppermute | solution.py:243
  58.4 1.1 %shard_map.87 = f32[512,512]{1,0:T(8,128)} custom-call(f32[512,512]{1,0:T(8,128)S(1)} %get-tuple-element.109.r, f32[512,512]{1,0:T(8,128)S(1)} %get-tuple-element.110.x, f32[512,128]{1,0:T(8,128)S(1)} %get-tuple-element.66.refs_4_.scale.refs_5_), custom_call_target="tpu_custom_call" | custom-call | flops 2621440 | tf_op jit(solution)/shard_map/pallas_call | solution.py:22
  (45 shorter events, 18.2 us)
Async XLA Ops:
  1.8 5.9 %collective-permute-start.1 = (f32[64,512]{1,0:T(8,128)S(1)}, f32[64,512]{1,0:T(8,128)S(1)}, u32[]{:S(2)}, u32[]{:S(2)}) collective-permute-start(f32[64,512]{1,0:T(8,128)S(1)} %get-tuple-element.59), channel_id=1, source_target_pairs={{0,1},{1,0},{2,3},{3,2},{4,5},{5,4},{6,7},{7,6},{8,9},{9,8},{10,11... | collective-permute-start | bytes 393224 | tf_op jit(solution)/shard_map/ppermute | solution.py:234
  2.4 6.1 %collective-permute-start = (f32[64,640]{1,0:T(8,128)S(1)}, f32[64,640]{1,0:T(8,128)S(1)}, u32[]{:S(2)}, u32[]{:S(2)}) collective-permute-start(f32[64,640]{1,0:T(8,128)S(1)} %get-tuple-element.57), channel_id=1, source_target_pairs={{0,16},{1,2},{2,1},{3,4},{4,3},{5,6},{6,5},{7,8},{8,7},{9,10},{10,... | collective-permute-start | bytes 491528 | tf_op jit(solution)/shard_map/ppermute | solution.py:230
  8.7 3.3 %collective-permute-start.3 = (f32[64,512]{1,0:T(8,128)S(1)}, f32[64,512]{1,0:T(8,128)S(1)}, u32[]{:S(2)}, u32[]{:S(2)}) collective-permute-start(f32[64,512]{1,0:T(8,128)S(1)} %get-tuple-element.71), channel_id=1, source_target_pairs={{0,1},{1,0},{2,3},{3,2},{4,5},{5,4},{6,7},{7,6},{8,9},{9,8},{10,11... | collective-permute-start | bytes 393224 | tf_op jit(solution)/shard_map/ppermute | solution.py:234
  9.0 5.0 %collective-permute-start.2 = (f32[64,512]{1,0:T(8,128)S(1)}, f32[64,512]{1,0:T(8,128)S(1)}, u32[]{:S(2)}, u32[]{:S(2)}) collective-permute-start(f32[64,512]{1,0:T(8,128)S(1)} %shard_map.64), channel_id=1, source_target_pairs={{0,16},{1,2},{2,1},{3,4},{4,3},{5,6},{6,5},{7,8},{8,7},{9,10},{10,... | collective-permute-start | bytes 393224 | tf_op jit(solution)/shard_map/ppermute | solution.py:230
  14.2 3.6 %collective-permute-start.5 = (f32[64,512]{1,0:T(8,128)S(1)}, f32[64,512]{1,0:T(8,128)S(1)}, u32[]{:S(2)}, u32[]{:S(2)}) collective-permute-start(f32[64,512]{1,0:T(8,128)S(1)} %get-tuple-element.78), channel_id=1, source_target_pairs={{0,1},{1,0},{2,3},{3,2},{4,5},{5,4},{6,7},{7,6},{8,9},{9,8},{10,11... | collective-permute-start | bytes 393224 | tf_op jit(solution)/shard_map/ppermute | solution.py:234
  15.1 5.0 %collective-permute-start.4 = (f32[64,512]{1,0:T(8,128)S(1)}, f32[64,512]{1,0:T(8,128)S(1)}, u32[]{:S(2)}, u32[]{:S(2)}) collective-permute-start(f32[64,512]{1,0:T(8,128)S(1)} %shard_map.68), channel_id=1, source_target_pairs={{0,16},{1,2},{2,1},{3,4},{4,3},{5,6},{6,5},{7,8},{8,7},{9,10},{10,... | collective-permute-start | bytes 393224 | tf_op jit(solution)/shard_map/ppermute | solution.py:230
  20.3 3.7 %collective-permute-start.7 = (f32[64,512]{1,0:T(8,128)S(1)}, f32[64,512]{1,0:T(8,128)S(1)}, u32[]{:S(2)}, u32[]{:S(2)}) collective-permute-start(f32[64,512]{1,0:T(8,128)S(1)} %get-tuple-element.85), channel_id=1, source_target_pairs={{0,1},{1,0},{2,3},{3,2},{4,5},{5,4},{6,7},{7,6},{8,9},{9,8},{10,11... | collective-permute-start | bytes 393224 | tf_op jit(solution)/shard_map/ppermute | solution.py:234
  21.4 5.0 %collective-permute-start.6 = (f32[64,512]{1,0:T(8,128)S(1)}, f32[64,512]{1,0:T(8,128)S(1)}, u32[]{:S(2)}, u32[]{:S(2)}) collective-permute-start(f32[64,512]{1,0:T(8,128)S(1)} %shard_map.72), channel_id=1, source_target_pairs={{0,16},{1,2},{2,1},{3,4},{4,3},{5,6},{6,5},{7,8},{8,7},{9,10},{10,... | collective-permute-start | bytes 393224 | tf_op jit(solution)/shard_map/ppermute | solution.py:230
  26.6 3.7 %collective-permute-start.9 = (f32[64,512]{1,0:T(8,128)S(1)}, f32[64,512]{1,0:T(8,128)S(1)}, u32[]{:S(2)}, u32[]{:S(2)}) collective-permute-start(f32[64,512]{1,0:T(8,128)S(1)} %get-tuple-element.92), channel_id=1, source_target_pairs={{0,1},{1,0},{2,3},{3,2},{4,5},{5,4},{6,7},{7,6},{8,9},{9,8},{10,11... | collective-permute-start | bytes 393224 | tf_op jit(solution)/shard_map/ppermute | solution.py:234
  27.6 5.0 %collective-permute-start.8 = (f32[64,512]{1,0:T(8,128)S(1)}, f32[64,512]{1,0:T(8,128)S(1)}, u32[]{:S(2)}, u32[]{:S(2)}) collective-permute-start(f32[64,512]{1,0:T(8,128)S(1)} %shard_map.76), channel_id=1, source_target_pairs={{0,16},{1,2},{2,1},{3,4},{4,3},{5,6},{6,5},{7,8},{8,7},{9,10},{10,... | collective-permute-start | bytes 393224 | tf_op jit(solution)/shard_map/ppermute | solution.py:230
  32.8 3.7 %collective-permute-start.11 = (f32[64,512]{1,0:T(8,128)S(1)}, f32[64,512]{1,0:T(8,128)S(1)}, u32[]{:S(2)}, u32[]{:S(2)}) collective-permute-start(f32[64,512]{1,0:T(8,128)S(1)} %get-tuple-element.99), channel_id=1, source_target_pairs={{0,1},{1,0},{2,3},{3,2},{4,5},{5,4},{6,7},{7,6},{8,9},{9,8},{10,11... | collective-permute-start | bytes 393224 | tf_op jit(solution)/shard_map/ppermute | solution.py:234
  33.9 5.0 %collective-permute-start.10 = (f32[64,512]{1,0:T(8,128)S(1)}, f32[64,512]{1,0:T(8,128)S(1)}, u32[]{:S(2)}, u32[]{:S(2)}) collective-permute-start(f32[64,512]{1,0:T(8,128)S(1)} %shard_map.80), channel_id=1, source_target_pairs={{0,16},{1,2},{2,1},{3,4},{4,3},{5,6},{6,5},{7,8},{8,7},{9,10},{10,... | collective-permute-start | bytes 393224 | tf_op jit(solution)/shard_map/ppermute | solution.py:230
  39.1 3.7 %collective-permute-start.13 = (f32[64,512]{1,0:T(8,128)S(1)}, f32[64,512]{1,0:T(8,128)S(1)}, u32[]{:S(2)}, u32[]{:S(2)}) collective-permute-start(f32[64,512]{1,0:T(8,128)S(1)} %get-tuple-element.105), channel_id=1, source_target_pairs={{0,1},{1,0},{2,3},{3,2},{4,5},{5,4},{6,7},{7,6},{8,9},{9,8},{10,11... | collective-permute-start | bytes 393224 | tf_op jit(solution)/shard_map/ppermute | solution.py:234
  40.2 5.0 %collective-permute-start.12 = (f32[64,512]{1,0:T(8,128)S(1)}, f32[64,512]{1,0:T(8,128)S(1)}, u32[]{:S(2)}, u32[]{:S(2)}) collective-permute-start(f32[64,512]{1,0:T(8,128)S(1)} %shard_map.84), channel_id=1, source_target_pairs={{0,16},{1,2},{2,1},{3,4},{4,3},{5,6},{6,5},{7,8},{8,7},{9,10},{10,... | collective-permute-start | bytes 393224 | tf_op jit(solution)/shard_map/ppermute | solution.py:230
  45.5 1.7 %collective-permute-start.14 = (f32[8,512]{1,0:T(8,128)S(1)}, f32[8,512]{1,0:T(8,128)S(1)}, u32[]{:S(2)}, u32[]{:S(2)}) collective-permute-start(f32[8,512]{1,0:T(8,128)S(1)} %get-tuple-element.111), channel_id=1, source_target_pairs={{0,1},{1,0},{2,3},{3,2},{4,5},{5,4},{6,7},{7,6},{8,9},{9,8},{10,11... | collective-permute-start | bytes 49160 | tf_op jit(solution)/shard_map/ppermute | solution.py:243
  47.2 4.6 %collective-permute-start.15 = (f32[8,512]{1,0:T(8,128)S(1)}, f32[8,512]{1,0:T(8,128)S(1)}, u32[]{:S(2)}, u32[]{:S(2)}) collective-permute-start(f32[8,512]{1,0:T(8,128)S(1)} %add.12), channel_id=1, source_target_pairs={{0,3},{1,2},{2,1},{3,0},{4,7},{5,6},{6,5},{7,4},{8,11},{9,10},{10,... | collective-permute-start | bytes 49160 | tf_op jit(solution)/shard_map/ppermute | solution.py:243
  51.8 3.8 %collective-permute-start.16 = (f32[8,512]{1,0:T(8,128)S(1)}, f32[8,512]{1,0:T(8,128)S(1)}, u32[]{:S(2)}, u32[]{:S(2)}) collective-permute-start(f32[8,512]{1,0:T(8,128)S(1)} %add.13), channel_id=1, source_target_pairs={{0,5},{1,4},{2,7},{3,6},{4,1},{5,0},{6,3},{7,2},{8,13},{9,12},{10,... | collective-permute-start | bytes 49160 | tf_op jit(solution)/shard_map/ppermute | solution.py:243
  55.7 4.2 %collective-permute-start.17 = (f32[8,512]{1,0:T(8,128)S(1)}, f32[8,512]{1,0:T(8,128)S(1)}, u32[]{:S(2)}, u32[]{:S(2)}) collective-permute-start(f32[8,512]{1,0:T(8,128)S(1)} %add.14), channel_id=1, source_target_pairs={{0,9},{1,8},{2,11},{3,10},{4,13},{5,12},{6,15},{7,14},{8,1},{9,0},... | collective-permute-start | bytes 49160 | tf_op jit(solution)/shard_map/ppermute | solution.py:243

commit v4 on v3

v4 whole, which is shorter than its diff:
```python
import functools

import jax
import jax.numpy as jnp
from jax import lax
from jax.experimental import pallas as pl
from jax.experimental.pallas import tpu as pltpu
from jax.sharding import PartitionSpec as P


SWEEPS = 8
F32 = jnp.float32
BF16 = jnp.bfloat16
VMEM_GRANT = 24 * 2**20
HBM_BLOCK = pl.BlockSpec(memory_space=pltpu.HBM)
VMEM_BLOCK = pl.BlockSpec(memory_space=pltpu.VMEM)


def call(kernel, outs, *args, hbm=(), free=(), scratch=(), flops=0):
    args = [a if i in free else pltpu.with_memory_space_constraint(a, pltpu.HBM if i in hbm else pltpu.VMEM) for i, a in enumerate(args)]
    many = isinstance(outs, list)
    return pl.pallas_call(
        kernel,
        out_shape=outs,
        in_specs=[HBM_BLOCK if i in hbm else VMEM_BLOCK for i in range(len(args))],
        out_specs=[VMEM_BLOCK] * len(outs) if many else VMEM_BLOCK,
        scratch_shapes=scratch,
        compiler_params=pltpu.CompilerParams(vmem_limit_bytes=VMEM_GRANT),
        cost_estimate=pl.CostEstimate(flops=flops, transcendentals=0, bytes_accessed=0),
    )(*args)


def halves(x):
    high = x.astype(BF16)
    return high, (x - high.astype(F32)).astype(BF16)


def left_terms(x):
    high, low = halves(x)
    return jnp.concatenate([high, low, high], axis=1)


def right_terms(x):
    high, low = halves(x)
    return jnp.concatenate([high, high, low], axis=0)


def both(x, axis):
    return jnp.concatenate(halves(x), axis=axis)


def product(left, right):
    return jnp.dot(left, right, preferred_element_type=F32)


def place():
    index, size = lax.axis_index("row"), lax.axis_size("row")
    return index % 2, jnp.logical_or(index == 0, index == size - 1)


def rims(rows, width):
    odd, _ = place()
    top = rows - width
    return pl.multiple_of(odd * top, width), pl.multiple_of((1 - odd) * top, width)


def diagonal(block, offset):
    row = lax.broadcasted_iota(jnp.int32, block.shape, 0) + offset
    column = lax.broadcasted_iota(jnp.int32, block.shape, 1)
    return jnp.sum(jnp.where(row == column, block, 0.0), axis=1, keepdims=True)


def facing(outer):
    _, end = place()
    return jnp.where(end, jnp.zeros_like(outer), outer)


def copies(pairs, sems):
    moves = [pltpu.make_async_copy(source, target, sems.at[i]) for i, (source, target) in enumerate(pairs)]
    for move in moves:
        move.start()
    return moves


def open_kernel(diag, sides, lower, upper, outer_out, inner_out, corners, strips, sems):
    odd, _ = place()
    rows = sides.shape[0]
    width, lanes = corners.shape[1:]
    top = rows - width
    moves = copies(
        [
            (diag.at[pl.ds(0, width), pl.ds(0, lanes)], corners.at[0]),
            (diag.at[pl.ds(top, width), pl.ds(rows - lanes, lanes)], corners.at[1]),
            (sides.at[pl.ds(0, width)], strips.at[0]),
            (sides.at[pl.ds(top, width)], strips.at[1]),
        ],
        sems,
    )
    for move in moves:
        move.wait()
    first = strips[0] / diagonal(corners[0], 0)
    last = strips[1] / diagonal(corners[1], lanes - width)
    outer_out[...] = facing(jnp.where(odd == 1, last, first))
    inner_out[...] = jnp.where(odd == 1, first, last)


def setup_kernel(block, low, up, sides, diag_out, outer_out, inner_out, told_out, scale_out, x_out, terms_out, v_out, sums_out):
    odd, _ = place()
    width, rows = low.shape
    side = sides[...]
    sums_out[0:1, :] = jnp.sum(side * side, axis=0, keepdims=True)
    scale = 1.0 / diagonal(block[...], 0)
    scale_out[...] = jnp.broadcast_to(scale, scale_out.shape)
    x = side * scale
    x_out[...] = x
    terms_out[...] = both(x, 0)
    diag_out[...] = both(block[...], 1)
    far, _ = spans(rows)
    v_out[...] = applied(sides, diag_out, terms_out, far)
    low, up = low[...], up[...]
    outer = jnp.where(odd == 1, up, low).T
    outer_out[...] = left_terms(outer)
    told = jnp.where(odd == 1, outer[rows - width :], outer[:width])
    told = told * jnp.where(odd == 1, scale[rows - width :], scale[:width])
    told_out[...] = facing(packed(told))
    inner_out[...] = left_terms(jnp.where(odd == 1, low, up).T)


def packed(square):
    return jnp.concatenate([square[i : i + 8] for i in range(0, square.shape[0], 8)], axis=1)


def unpacked(strip, width):
    return jnp.concatenate([strip[:, i : i + width] for i in range(0, width * width // 8, width)], axis=0)


def spans(rows):
    odd, _ = place()
    half = rows // 2
    return pl.multiple_of(odd * half, half), pl.multiple_of((1 - odd) * half, half)


def applied(side, diag, terms, start):
    rows = side.shape[0]
    some = pl.ds(start, rows // 2)
    high, low = diag[some, :rows], diag[some, rows:]
    images = product(high, terms[rows:, :]) + product(low, terms[:rows, :]) + product(high, terms[:rows, :])
    return side[some, :] - images


def wide(pivots, columns):
    return jnp.concatenate([pivots] * (columns // pivots.shape[1]), axis=1)


def send_kernel(*refs):
    *told, inner, x, v, coupling, scale, outer_out = refs
    odd, _ = place()
    rows, columns = x.shape
    width = inner.shape[0]
    far, _ = rims(rows, width)
    rim = pl.ds(far, width)
    inside = pl.ds(pl.multiple_of(odd * (v.shape[0] - width), width), width)
    residual = v[inside, :] - product(coupling[rim, :], right_terms(inner[...]))
    outer_out[:width, :] = facing(x[rim, :] + residual * wide(scale[rim, :], columns))
    if told:
        outer_out[width:, :] = told[0][...]


def fill_kernel(inner, terms, v, side, diag, coupling, u_out):
    far, near = spans(side.shape[0])
    half = v.shape[0]
    halo = right_terms(inner[...])
    u_out[pl.ds(far, half), :] = v[...] - product(coupling[pl.ds(far, half), :], halo)
    u_out[pl.ds(near, half), :] = applied(side, diag, terms, near) - product(coupling[pl.ds(near, half), :], halo)


def rim_kernel(*refs, sweep):
    told_out = None
    if sweep == 2:
        *refs, told_out = refs
    *known, message, x, u, coupling, scale, halo_out, inner_out = refs
    rows, columns = x.shape
    width = inner_out.shape[0]
    _, near = rims(rows, width)
    rim = pl.ds(near, width)
    outer = message[:width, :]
    if sweep == 2:
        told = left_terms(unpacked(message[width:, :], width))
        told_out[...] = told
        outer = outer - product(told, known[0][...])
    elif sweep > 2:
        outer = outer - known[0][...]
    halo = right_terms(outer)
    halo_out[...] = halo
    residual = u[rim, :] - product(coupling[rim, :], halo)
    inner_out[...] = x[rim, :] + residual * wide(scale[rim, :], columns)


def sweep_kernel(*refs, sweep):
    *told, halo, x, terms, u, side, diag, coupling, scale, sums, x_out, terms_out, v_out, known_out, sums_out = refs
    rows, columns = x.shape
    width = halo.shape[0] // 3
    far, _ = rims(rows, width)
    mine = jnp.concatenate([terms[pl.ds(far + part * rows, width), :] for part in (0, 0, 1)], axis=0)
    known_out[...] = product(told[0][...], mine) if told else mine
    sums_out[...] = sums[...]
    residual = u[...] - product(coupling[...], halo[...])
    sums_out[sweep : sweep + 1, :] = jnp.sum(residual * residual, axis=0, keepdims=True)
    new = x[...] + residual * wide(scale[...], columns)
    x_out[...] = new
    terms_out[...] = both(new, 0)
    start, _ = spans(rows)
    v_out[...] = applied(side, diag, terms_out, start)


def last_kernel(known, message, u, coupling, sums, r_out, sums_out, *, sweep):
    sums_out[...] = sums[...]
    residual = u[...] - product(coupling[...], right_terms(message[...] - known[...]))
    sums_out[sweep : sweep + 1, :] = jnp.sum(residual * residual, axis=0, keepdims=True)
    r_out[...] = residual


def close_kernel(r, x, scale, x_out):
    x_out[...] = x[...] + r[...] * wide(scale[...], x.shape[1])


def pairings():
    size, groups = lax.axis_size("row"), lax.axis_size("grp")
    within = [(i, i ^ 1) for i in range(size)]
    between = []
    for g in range(groups):
        for i in range(size):
            j = i + 1 if i % 2 else i - 1
            if 0 <= j < size:
                target = g * size + j
            elif groups % 2 == 0:
                target = (g ^ 1) * size + i
            else:
                target = g * size + size - 1 - i
            between.append((g * size + i, target))
    return within, between


def across(outer):
    return lax.ppermute(outer, ("grp", "row"), pairings()[1])


def along(inner):
    return lax.ppermute(inner, "row", pairings()[0])


def row_sum(x):
    size = lax.axis_size("row")
    assert size & (size - 1) == 0
    step = 1
    while step < size:
        flips = [1] if step == 1 else [step + 1, 2 * step + 1, 3 * step] if 2 * step < size else [step + 1]
        x = functools.reduce(jnp.add, [x] + [lax.ppermute(x, "row", [(i, i ^ f) for i in range(size)]) for f in flips])
        step *= 1 + len(flips)
    return x


def program(diag_blocks, lower_coupling, upper_coupling, right_sides):
    rows, columns = right_sides.shape
    width = lower_coupling.shape[1]
    rim = pltpu.VMEM((width, columns), F32)
    panel = pltpu.VMEM((rows, columns), F32)
    sums_shape = pltpu.VMEM((SWEEPS, columns), F32)
    lanes = 128
    lower, upper = lower_coupling.T, upper_coupling.T
    outer, inner = call(
        open_kernel,
        [rim, rim],
        diag_blocks, right_sides, lower, upper,
        hbm=(0, 1, 2, 3),
        scratch=[
            pltpu.VMEM((2, width, lanes), F32),
            pltpu.VMEM((2, width, columns), F32),
            pltpu.SemaphoreType.DMA((4,)),
        ],
    )
    message = across(outer)
    inner = along(inner)
    half = pltpu.VMEM((rows // 2, columns), F32)
    all_terms = pltpu.VMEM((2 * rows, columns), BF16)
    coupling_shape = pltpu.VMEM((rows, 3 * width), BF16)
    diag, outward, inward, told, scale, x, terms, v, sums = call(
        setup_kernel,
        [
            pltpu.VMEM((rows, 2 * rows), BF16),
            coupling_shape,
            coupling_shape,
            pltpu.VMEM((8, width * width // 8), F32),
            pltpu.VMEM((rows, lanes), F32),
            panel,
            all_terms,
            half,
            sums_shape,
        ],
        diag_blocks, lower, upper, right_sides,
        free=(0, 1, 2, 3),
        flops=3 * rows * rows * columns,
    )
    known, heard = [], []
    halo_shape = pltpu.VMEM((3 * width, columns), BF16)
    for sweep in range(1, SWEEPS):
        if sweep < SWEEPS - 1:
            tell = [told] if sweep == 1 else []
            sent = call(
                send_kernel,
                pltpu.VMEM((width + 8 * len(tell), columns), F32),
                *tell, inner, x, v, inward, scale,
                flops=6 * width * width * columns,
            )
            ahead = across(sent)
        u = call(
            fill_kernel,
            panel,
            inner, terms, v, right_sides, diag, inward,
            free=(3,),
            flops=3 * rows * (rows + 2 * width) * columns,
        )
        if sweep == SWEEPS - 1:
            break
        halo, rim_values, *news = call(
            functools.partial(rim_kernel, sweep=sweep),
            [halo_shape, rim] + ([pltpu.VMEM((width, 3 * width), BF16)] if sweep == 2 else []),
            *known, message, x, u, outward, scale,
            flops=6 * width * width * columns,
        )
        inner = along(rim_values)
        heard = heard or news
        x, terms, v, kept, sums = call(
            functools.partial(sweep_kernel, sweep=sweep),
            [panel, all_terms, half, rim if heard else halo_shape, sums_shape],
            *heard, halo, x, terms, u, right_sides, diag, outward, scale, sums,
            free=(len(heard) + 4,),
            flops=3 * rows * (rows + 2 * width) * columns,
        )
        known, message = [kept], ahead
    r, sums = call(
        functools.partial(last_kernel, sweep=SWEEPS - 1),
        [panel, sums_shape],
        *known, message, u, outward, sums,
        flops=6 * rows * width * columns,
    )
    solution = call(close_kernel, jax.ShapeDtypeStruct((rows, columns), F32), r, x, scale, flops=10 * rows * columns)
    return solution, jnp.sqrt(row_sum(sums))


def solution(mesh):
    return jax.shard_map(
        program,
        mesh=mesh,
        in_specs=(P("row", None), P("row", None), P("row", None), P("row", "grp")),
        out_specs=(P("row", "grp"), P(None, "grp")),
        check_vma=False,
    )
```

time: 60.6 us -> 59.4 us (0.980)
  Pallas kernels: 18.7 us -> 16.9 us
  waiting for transfers between devices: 13.7 us -> 14.8 us
    pallas_call x29, Pallas kernels: 18.7 us -> 16.9 us  [call(): pl.pallas_call(kernel, out_shape=outs, in_specs=[HBM_BLOCK if i in hbm el...]
    ppermute x7, waiting for transfers between devices: 9.59 us -> 11.2 us  [across(): return lax.ppermute(outer, ('grp', 'row'), pairings()[1])]
    ppermute x4 -> x5, starting transfers between devices: 9.14 us -> 8.52 us  [row_sum(): lax.ppermute(x, 'row', [(i, i ^ f) for i in range(size)])]
    ppermute x4 -> x5, waiting for transfers between devices: 4.08 us -> 3.55 us  [row_sum(): lax.ppermute(x, 'row', [(i, i ^ f) for i in range(size)])]
  transfers between devices with their start and end apart: 18 -> 19, of which waited for: 10 -> 12; matrix products, arithmetic and copies ran while one was open for 0% -> 0% of each run, Pallas kernels for 27% -> 24%
where the time goes in v4:
time: 59.4 us; the launch traced here: 59.2 us
  starting transfers between devices  26.1 us (44%)
  Pallas kernels  16.9 us (28%)
  waiting for transfers between devices  14.8 us (25%)
  between operations  0.88 us (1%)
  other arithmetic  0.63 us (1%)
    pallas_call x29, Pallas kernels, call(): pl.pallas_call(kernel, out_shape=outs, in_specs=[HBM_BLOCK if i in hbm el...  16.9 us
    ppermute x7, starting transfers between devices, across(): return lax.ppermute(outer, ('grp', 'row'), pairings()[1])  12.6 us
    ppermute x7, waiting for transfers between devices, across(): return lax.ppermute(outer, ('grp', 'row'), pairings()[1])  11.2 us
    ppermute x5, starting transfers between devices, row_sum(): lax.ppermute(x, 'row', [(i, i ^ f) for i in range(size)])  8.52 us
    ppermute x7, starting transfers between devices, along(): return lax.ppermute(inner, 'row', pairings()[0])  4.97 us
    ppermute x5, waiting for transfers between devices, row_sum(): lax.ppermute(x, 'row', [(i, i ^ f) for i in range(size)])  3.55 us
  transfers between devices with their start and end apart: 19, of which 12 were waited for; matrix products, arithmetic and copies ran while one was open for 0% of the time, Pallas kernels for 24%

profile of v4, /device:TPU:0, one launch (start us, length us, event | category | flops | bytes accessed | tf_op | source)
XLA Modules:
  0.0 59.2 jit_solution(7107225645082333903)
XLA Ops:
  0.7 1.3 %shard_map.59 = (f32[64,512]{1,0:T(8,128)S(1)}, f32[64,512]{1,0:T(8,128)S(1)}) custom-call(f32[512,512]{1,0:T(8,128)} %block.1, f32[512,512]{1,0:T(8,128)} %side.13, f32[64,512]{1,0:T(8,128)} %bitcast.2, f32[64,512]{1,0:T(8,128)} %bitcast.4), custom_call_target="tpu_custom_call" | custom-call | tf_op jit(solution)/shard_map/pallas_call | solution.py:22
  2.5 2.6 %collective-permute-start = (f32[64,512]{1,0:T(8,128)S(1)}, f32[64,512]{1,0:T(8,128)S(1)}, u32[]{:S(2)}, u32[]{:S(2)}) collective-permute-start(f32[64,512]{1,0:T(8,128)S(1)} %get-tuple-element.58), channel_id=1, source_target_pairs={{0,16},{1,2},{2,1},{3,4},{4,3},{5,6},{6,5},{7,8},{8,7},{9,10},{10,... | collective-permute-start | bytes 393224 | tf_op jit(solution)/shard_map/ppermute | solution.py:245
  5.1 1.0 %shard_map.60 = (bf16[512,1024]{1,0:T(8,128)(2,1)S(1)}, bf16[512,192]{1,0:T(8,128)(2,1)S(1)}, bf16[512,192]{1,0:T(8,128)(2,1)S(1)}, f32[8,512]{1,0:T(8,128)S(1)}...) custom-call(f32[512,512]{1,0:T(8,128)S(1)} %copy-done.1, ...), custom_call_target="tpu_custom_call" | custom-call | flops 402653184 | tf_op jit(solution)/shard_map/pallas_call | solution.py:22
  6.9 1.2 %collective-permute-done.refs_0_ = f32[64,512]{1,0:T(8,128)S(1)} collective-permute-done((f32[64,512]{1,0:T(8,128)S(1)}, f32[64,512]{1,0:T(8,128)S(1)}, u32[]{:S(2)}, u32[]{:S(2)}) %collective-permute-start) | collective-permute-done | bytes 131104 | tf_op jit(solution)/shard_map/ppermute | solution.py:245
  8.5 2.1 %collective-permute-start.2 = (f32[72,512]{1,0:T(8,128)S(1)}, f32[72,512]{1,0:T(8,128)S(1)}, u32[]{:S(2)}, u32[]{:S(2)}) collective-permute-start(f32[72,512]{1,0:T(8,128)S(1)} %shard_map.64), channel_id=1, source_target_pairs={{0,16},{1,2},{2,1},{3,4},{4,3},{5,6},{6,5},{7,8},{8,7},{9,10},{10,... | collective-permute-start | bytes 442376 | tf_op jit(solution)/shard_map/ppermute | solution.py:245
  12.4 1.4 %collective-permute-done.2.refs_1_ = f32[72,512]{1,0:T(8,128)S(1)} collective-permute-done((f32[72,512]{1,0:T(8,128)S(1)}, f32[72,512]{1,0:T(8,128)S(1)}, u32[]{:S(2)}, u32[]{:S(2)}) %collective-permute-start.2) | collective-permute-done | bytes 147488 | tf_op jit(solution)/shard_map/ppermute | solution.py:245
  14.2 1.3 %collective-permute-start.5 = (f32[64,512]{1,0:T(8,128)S(1)}, f32[64,512]{1,0:T(8,128)S(1)}, u32[]{:S(2)}, u32[]{:S(2)}) collective-permute-start(f32[64,512]{1,0:T(8,128)S(1)} %get-tuple-element.80), channel_id=1, source_target_pairs={{0,1},{1,0},{2,3},{3,2},{4,5},{5,4},{6,7},{7,6},{8,9},{9,8},{10,11... | collective-permute-start | bytes 393224 | tf_op jit(solution)/shard_map/ppermute | solution.py:249
  15.7 1.6 %collective-permute-start.4 = (f32[64,512]{1,0:T(8,128)S(1)}, f32[64,512]{1,0:T(8,128)S(1)}, u32[]{:S(2)}, u32[]{:S(2)}) collective-permute-start(f32[64,512]{1,0:T(8,128)S(1)} %shard_map.68), channel_id=1, source_target_pairs={{0,16},{1,2},{2,1},{3,4},{4,3},{5,6},{6,5},{7,8},{8,7},{9,10},{10,... | collective-permute-start | bytes 393224 | tf_op jit(solution)/shard_map/ppermute | solution.py:245
  17.3 1.0 %shard_map.67 = (f32[512,512]{1,0:T(8,128)S(1)}, bf16[1024,512]{1,0:T(8,128)(2,1)S(1)}, f32[256,512]{1,0:T(8,128)S(1)}, f32[64,512]{1,0:T(8,128)S(1)}, f32[8,512]{1,0:T(8,128)S(1)}) custom-call(bf16[64,192]{1,0:T(8,128)(2,1)S(1)} %get-tuple-element.75.refs_0_, bf16[192,512]{1,0:T(8,128)(2,1)S(1)} %get-tuple-element.76.refs_1_, ...), custom_call_target="tpu_custom_call" | custom-call | flops 503316480 | tf_op jit(solution)/shard_map/pallas_call | solution.py:22
  19.0 1.7 %collective-permute-done.4.refs_1_ = f32[64,512]{1,0:T(8,128)S(1)} collective-permute-done((f32[64,512]{1,0:T(8,128)S(1)}, f32[64,512]{1,0:T(8,128)S(1)}, u32[]{:S(2)}, u32[]{:S(2)}) %collective-permute-start.4) | collective-permute-done | bytes 131104 | tf_op jit(solution)/shard_map/ppermute | solution.py:245
  21.3 1.6 %collective-permute-start.6 = (f32[64,512]{1,0:T(8,128)S(1)}, f32[64,512]{1,0:T(8,128)S(1)}, u32[]{:S(2)}, u32[]{:S(2)}) collective-permute-start(f32[64,512]{1,0:T(8,128)S(1)} %shard_map.72), channel_id=1, source_target_pairs={{0,16},{1,2},{2,1},{3,4},{4,3},{5,6},{6,5},{7,8},{8,7},{9,10},{10,... | collective-permute-start | bytes 393224 | tf_op jit(solution)/shard_map/ppermute | solution.py:245
  24.6 1.7 %collective-permute-done.6.refs_1_ = f32[64,512]{1,0:T(8,128)S(1)} collective-permute-done((f32[64,512]{1,0:T(8,128)S(1)}, f32[64,512]{1,0:T(8,128)S(1)}, u32[]{:S(2)}, u32[]{:S(2)}) %collective-permute-start.6) | collective-permute-done | bytes 131104 | tf_op jit(solution)/shard_map/ppermute | solution.py:245
  27.6 1.6 %collective-permute-start.8 = (f32[64,512]{1,0:T(8,128)S(1)}, f32[64,512]{1,0:T(8,128)S(1)}, u32[]{:S(2)}, u32[]{:S(2)}) collective-permute-start(f32[64,512]{1,0:T(8,128)S(1)} %shard_map.76), channel_id=1, source_target_pairs={{0,16},{1,2},{2,1},{3,4},{4,3},{5,6},{6,5},{7,8},{8,7},{9,10},{10,... | collective-permute-start | bytes 393224 | tf_op jit(solution)/shard_map/ppermute | solution.py:245
  29.2 1.0 %shard_map.75 = (f32[512,512]{1,0:T(8,128)S(1)}, bf16[1024,512]{1,0:T(8,128)(2,1)S(1)}, f32[256,512]{1,0:T(8,128)S(1)}, f32[64,512]{1,0:T(8,128)S(1)}, f32[8,512]{1,0:T(8,128)S(1)}) custom-call(bf16[64,192]{1,0:T(8,128)(2,1)S(1)} %get-tuple-element.75.refs_0_, bf16[192,512]{1,0:T(8,128)(2,1)S(1)} %get-tuple-element.90.refs_1_, ...), custom_call_target="tpu_custom_call" | custom-call | flops 503316480 | tf_op jit(solution)/shard_map/pallas_call | solution.py:22
  30.9 1.7 %collective-permute-done.8.refs_1_ = f32[64,512]{1,0:T(8,128)S(1)} collective-permute-done((f32[64,512]{1,0:T(8,128)S(1)}, f32[64,512]{1,0:T(8,128)S(1)}, u32[]{:S(2)}, u32[]{:S(2)}) %collective-permute-start.8) | collective-permute-done | bytes 131104 | tf_op jit(solution)/shard_map/ppermute | solution.py:245
  33.9 1.6 %collective-permute-start.10 = (f32[64,512]{1,0:T(8,128)S(1)}, f32[64,512]{1,0:T(8,128)S(1)}, u32[]{:S(2)}, u32[]{:S(2)}) collective-permute-start(f32[64,512]{1,0:T(8,128)S(1)} %shard_map.80), channel_id=1, source_target_pairs={{0,16},{1,2},{2,1},{3,4},{4,3},{5,6},{6,5},{7,8},{8,7},{9,10},{10,... | collective-permute-start | bytes 393224 | tf_op jit(solution)/shard_map/ppermute | solution.py:245
  35.4 1.0 %shard_map.79 = (f32[512,512]{1,0:T(8,128)S(1)}, bf16[1024,512]{1,0:T(8,128)(2,1)S(1)}, f32[256,512]{1,0:T(8,128)S(1)}, f32[64,512]{1,0:T(8,128)S(1)}, f32[8,512]{1,0:T(8,128)S(1)}) custom-call(bf16[64,192]{1,0:T(8,128)(2,1)S(1)} %get-tuple-element.75.refs_0_, bf16[192,512]{1,0:T(8,128)(2,1)S(1)} %get-tuple-element.97.refs_1_, ...), custom_call_target="tpu_custom_call" | custom-call | flops 503316480 | tf_op jit(solution)/shard_map/pallas_call | solution.py:22
  37.2 1.7 %collective-permute-done.10.refs_1_ = f32[64,512]{1,0:T(8,128)S(1)} collective-permute-done((f32[64,512]{1,0:T(8,128)S(1)}, f32[64,512]{1,0:T(8,128)S(1)}, u32[]{:S(2)}, u32[]{:S(2)}) %collective-permute-start.10) | collective-permute-done | bytes 131104 | tf_op jit(solution)/shard_map/ppermute | solution.py:245
  40.1 1.6 %collective-permute-start.12 = (f32[64,512]{1,0:T(8,128)S(1)}, f32[64,512]{1,0:T(8,128)S(1)}, u32[]{:S(2)}, u32[]{:S(2)}) collective-permute-start(f32[64,512]{1,0:T(8,128)S(1)} %shard_map.84), channel_id=1, source_target_pairs={{0,16},{1,2},{2,1},{3,4},{4,3},{5,6},{6,5},{7,8},{8,7},{9,10},{10,... | collective-permute-start | bytes 393224 | tf_op jit(solution)/shard_map/ppermute | solution.py:245
  43.4 1.7 %collective-permute-done.12.message = f32[64,512]{1,0:T(8,128)S(1)} collective-permute-done((f32[64,512]{1,0:T(8,128)S(1)}, f32[64,512]{1,0:T(8,128)S(1)}, u32[]{:S(2)}, u32[]{:S(2)}) %collective-permute-start.12) | collective-permute-done | bytes 131104 | tf_op jit(solution)/shard_map/ppermute | solution.py:245
  47.2 4.0 %collective-permute-start.17 = (f32[8,512]{1,0:T(8,128)S(1)}, f32[8,512]{1,0:T(8,128)S(1)}, u32[]{:S(2)}, u32[]{:S(2)}) collective-permute-start(f32[8,512]{1,0:T(8,128)S(1)} %add.15), channel_id=1, source_target_pairs={{0,6},{1,7},{2,4},{3,5},{4,2},{5,3},{6,0},{7,1},{8,14},{9,15},{10,... | collective-permute-start | bytes 49160 | tf_op jit(solution)/shard_map/ppermute | solution.py:258
  53.0 1.4 %collective-permute-done.16 = f32[8,512]{1,0:T(8,128)S(1)} collective-permute-done((f32[8,512]{1,0:T(8,128)S(1)}, f32[8,512]{1,0:T(8,128)S(1)}, u32[]{:S(2)}, u32[]{:S(2)}) %collective-permute-start.16) | collective-permute-done | bytes 16416 | tf_op jit(solution)/shard_map/ppermute | solution.py:258
  54.5 2.6 %collective-permute-start.18 = (f32[8,512]{1,0:T(8,128)S(1)}, f32[8,512]{1,0:T(8,128)S(1)}, u32[]{:S(2)}, u32[]{:S(2)}) collective-permute-start(f32[8,512]{1,0:T(8,128)S(1)} %add_add_fusion), channel_id=1, source_target_pairs={{0,9},{1,8},{2,11},{3,10},{4,13},{5,12},{6,15},{7,14},{8,1},{9,0},... | collective-permute-start | bytes 49160 | tf_op jit(solution)/shard_map/ppermute | solution.py:258
  57.2 1.1 %shard_map.87 = f32[512,512]{1,0:T(8,128)} custom-call(f32[512,512]{1,0:T(8,128)S(1)} %get-tuple-element.111.r, f32[512,512]{1,0:T(8,128)S(1)} %get-tuple-element.112.x, f32[512,128]{1,0:T(8,128)S(1)} %get-tuple-element.66.refs_4_.refs_7_.refs_5_.refs_8_.scale), custom_call_target="tpu_custom_call" | custom-call | flops 2621440 | tf_op jit(solution)/shard_map/pallas_call | solution.py:22
  (54 shorter events, 18.7 us)
Async XLA Ops:
  0.6 4.5 %copy-start = (f32[512,512]{1,0:T(8,128)S(1)}, f32[512,512]{1,0:T(8,128)}, u32[]{:S(2)}) copy-start(f32[512,512]{1,0:T(8,128)} %side.13) | copy-start | bytes 3145732
  0.6 4.5 %copy-start.1 = (f32[512,512]{1,0:T(8,128)S(1)}, f32[512,512]{1,0:T(8,128)}, u32[]{:S(2)}) copy-start(f32[512,512]{1,0:T(8,128)} %block.1) | copy-start | bytes 3145732
  0.7 4.5 %copy-start.2 = (f32[512,64]{0,1:T(8,128)S(1)}, f32[512,64]{0,1:T(8,128)}, u32[]{:S(2)}) copy-start(f32[512,64]{0,1:T(8,128)} %param.5) | copy-start | bytes 393220
  0.7 4.5 %copy-start.3 = (f32[512,64]{0,1:T(8,128)S(1)}, f32[512,64]{0,1:T(8,128)}, u32[]{:S(2)}) copy-start(f32[512,64]{0,1:T(8,128)} %param.6) | copy-start | bytes 393220
  2.0 4.2 %collective-permute-start.1 = (f32[64,512]{1,0:T(8,128)S(1)}, f32[64,512]{1,0:T(8,128)S(1)}, u32[]{:S(2)}, u32[]{:S(2)}) collective-permute-start(f32[64,512]{1,0:T(8,128)S(1)} %get-tuple-element.60), channel_id=1, source_target_pairs={{0,1},{1,0},{2,3},{3,2},{4,5},{5,4},{6,7},{7,6},{8,9},{9,8},{10,11... | collective-permute-start | bytes 393224 | tf_op jit(solution)/shard_map/ppermute | solution.py:249
  2.5 5.5 %collective-permute-start = (f32[64,512]{1,0:T(8,128)S(1)}, f32[64,512]{1,0:T(8,128)S(1)}, u32[]{:S(2)}, u32[]{:S(2)}) collective-permute-start(f32[64,512]{1,0:T(8,128)S(1)} %get-tuple-element.58), channel_id=1, source_target_pairs={{0,16},{1,2},{2,1},{3,4},{4,3},{5,6},{6,5},{7,8},{8,7},{9,10},{10,... | collective-permute-start | bytes 393224 | tf_op jit(solution)/shard_map/ppermute | solution.py:245
  8.2 3.4 %collective-permute-start.3 = (f32[64,512]{1,0:T(8,128)S(1)}, f32[64,512]{1,0:T(8,128)S(1)}, u32[]{:S(2)}, u32[]{:S(2)}) collective-permute-start(f32[64,512]{1,0:T(8,128)S(1)} %get-tuple-element.72), channel_id=1, source_target_pairs={{0,1},{1,0},{2,3},{3,2},{4,5},{5,4},{6,7},{7,6},{8,9},{9,8},{10,11... | collective-permute-start | bytes 393224 | tf_op jit(solution)/shard_map/ppermute | solution.py:249
  8.5 5.2 %collective-permute-start.2 = (f32[72,512]{1,0:T(8,128)S(1)}, f32[72,512]{1,0:T(8,128)S(1)}, u32[]{:S(2)}, u32[]{:S(2)}) collective-permute-start(f32[72,512]{1,0:T(8,128)S(1)} %shard_map.64), channel_id=1, source_target_pairs={{0,16},{1,2},{2,1},{3,4},{4,3},{5,6},{6,5},{7,8},{8,7},{9,10},{10,... | collective-permute-start | bytes 442376 | tf_op jit(solution)/shard_map/ppermute | solution.py:245
  14.2 4.1 %collective-permute-start.5 = (f32[64,512]{1,0:T(8,128)S(1)}, f32[64,512]{1,0:T(8,128)S(1)}, u32[]{:S(2)}, u32[]{:S(2)}) collective-permute-start(f32[64,512]{1,0:T(8,128)S(1)} %get-tuple-element.80), channel_id=1, source_target_pairs={{0,1},{1,0},{2,3},{3,2},{4,5},{5,4},{6,7},{7,6},{8,9},{9,8},{10,11... | collective-permute-start | bytes 393224 | tf_op jit(solution)/shard_map/ppermute | solution.py:249
  15.7 5.0 %collective-permute-start.4 = (f32[64,512]{1,0:T(8,128)S(1)}, f32[64,512]{1,0:T(8,128)S(1)}, u32[]{:S(2)}, u32[]{:S(2)}) collective-permute-start(f32[64,512]{1,0:T(8,128)S(1)} %shard_map.68), channel_id=1, source_target_pairs={{0,16},{1,2},{2,1},{3,4},{4,3},{5,6},{6,5},{7,8},{8,7},{9,10},{10,... | collective-permute-start | bytes 393224 | tf_op jit(solution)/shard_map/ppermute | solution.py:245
  20.9 3.0 %collective-permute-start.7 = (f32[64,512]{1,0:T(8,128)S(1)}, f32[64,512]{1,0:T(8,128)S(1)}, u32[]{:S(2)}, u32[]{:S(2)}) collective-permute-start(f32[64,512]{1,0:T(8,128)S(1)} %get-tuple-element.87), channel_id=1, source_target_pairs={{0,1},{1,0},{2,3},{3,2},{4,5},{5,4},{6,7},{7,6},{8,9},{9,8},{10,11... | collective-permute-start | bytes 393224 | tf_op jit(solution)/shard_map/ppermute | solution.py:249
  21.3 5.0 %collective-permute-start.6 = (f32[64,512]{1,0:T(8,128)S(1)}, f32[64,512]{1,0:T(8,128)S(1)}, u32[]{:S(2)}, u32[]{:S(2)}) collective-permute-start(f32[64,512]{1,0:T(8,128)S(1)} %shard_map.72), channel_id=1, source_target_pairs={{0,16},{1,2},{2,1},{3,4},{4,3},{5,6},{6,5},{7,8},{8,7},{9,10},{10,... | collective-permute-start | bytes 393224 | tf_op jit(solution)/shard_map/ppermute | solution.py:245
  26.5 3.6 %collective-permute-start.9 = (f32[64,512]{1,0:T(8,128)S(1)}, f32[64,512]{1,0:T(8,128)S(1)}, u32[]{:S(2)}, u32[]{:S(2)}) collective-permute-start(f32[64,512]{1,0:T(8,128)S(1)} %get-tuple-element.94), channel_id=1, source_target_pairs={{0,1},{1,0},{2,3},{3,2},{4,5},{5,4},{6,7},{7,6},{8,9},{9,8},{10,11... | collective-permute-start | bytes 393224 | tf_op jit(solution)/shard_map/ppermute | solution.py:249
  27.6 5.0 %collective-permute-start.8 = (f32[64,512]{1,0:T(8,128)S(1)}, f32[64,512]{1,0:T(8,128)S(1)}, u32[]{:S(2)}, u32[]{:S(2)}) collective-permute-start(f32[64,512]{1,0:T(8,128)S(1)} %shard_map.76), channel_id=1, source_target_pairs={{0,16},{1,2},{2,1},{3,4},{4,3},{5,6},{6,5},{7,8},{8,7},{9,10},{10,... | collective-permute-start | bytes 393224 | tf_op jit(solution)/shard_map/ppermute | solution.py:245
  32.8 3.7 %collective-permute-start.11 = (f32[64,512]{1,0:T(8,128)S(1)}, f32[64,512]{1,0:T(8,128)S(1)}, u32[]{:S(2)}, u32[]{:S(2)}) collective-permute-start(f32[64,512]{1,0:T(8,128)S(1)} %get-tuple-element.101), channel_id=1, source_target_pairs={{0,1},{1,0},{2,3},{3,2},{4,5},{5,4},{6,7},{7,6},{8,9},{9,8},{10,11... | collective-permute-start | bytes 393224 | tf_op jit(solution)/shard_map/ppermute | solution.py:249
  33.9 5.0 %collective-permute-start.10 = (f32[64,512]{1,0:T(8,128)S(1)}, f32[64,512]{1,0:T(8,128)S(1)}, u32[]{:S(2)}, u32[]{:S(2)}) collective-permute-start(f32[64,512]{1,0:T(8,128)S(1)} %shard_map.80), channel_id=1, source_target_pairs={{0,16},{1,2},{2,1},{3,4},{4,3},{5,6},{6,5},{7,8},{8,7},{9,10},{10,... | collective-permute-start | bytes 393224 | tf_op jit(solution)/shard_map/ppermute | solution.py:245
  39.1 3.6 %collective-permute-start.13 = (f32[64,512]{1,0:T(8,128)S(1)}, f32[64,512]{1,0:T(8,128)S(1)}, u32[]{:S(2)}, u32[]{:S(2)}) collective-permute-start(f32[64,512]{1,0:T(8,128)S(1)} %get-tuple-element.107), channel_id=1, source_target_pairs={{0,1},{1,0},{2,3},{3,2},{4,5},{5,4},{6,7},{7,6},{8,9},{9,8},{10,11... | collective-permute-start | bytes 393224 | tf_op jit(solution)/shard_map/ppermute | solution.py:249
  40.1 5.0 %collective-permute-start.12 = (f32[64,512]{1,0:T(8,128)S(1)}, f32[64,512]{1,0:T(8,128)S(1)}, u32[]{:S(2)}, u32[]{:S(2)}) collective-permute-start(f32[64,512]{1,0:T(8,128)S(1)} %shard_map.84), channel_id=1, source_target_pairs={{0,16},{1,2},{2,1},{3,4},{4,3},{5,6},{6,5},{7,8},{8,7},{9,10},{10,... | collective-permute-start | bytes 393224 | tf_op jit(solution)/shard_map/ppermute | solution.py:245
  45.5 1.8 %collective-permute-start.14 = (f32[8,512]{1,0:T(8,128)S(1)}, f32[8,512]{1,0:T(8,128)S(1)}, u32[]{:S(2)}, u32[]{:S(2)}) collective-permute-start(f32[8,512]{1,0:T(8,128)S(1)} %get-tuple-element.113), channel_id=1, source_target_pairs={{0,1},{1,0},{2,3},{3,2},{4,5},{5,4},{6,7},{7,6},{8,9},{9,8},{10,11... | collective-permute-start | bytes 49160 | tf_op jit(solution)/shard_map/ppermute | solution.py:258
  47.2 5.7 %collective-permute-start.17 = (f32[8,512]{1,0:T(8,128)S(1)}, f32[8,512]{1,0:T(8,128)S(1)}, u32[]{:S(2)}, u32[]{:S(2)}) collective-permute-start(f32[8,512]{1,0:T(8,128)S(1)} %add.15), channel_id=1, source_target_pairs={{0,6},{1,7},{2,4},{3,5},{4,2},{5,3},{6,0},{7,1},{8,14},{9,15},{10,... | collective-permute-start | bytes 49160 | tf_op jit(solution)/shard_map/ppermute | solution.py:258
  51.2 3.2 %collective-permute-start.16 = (f32[8,512]{1,0:T(8,128)S(1)}, f32[8,512]{1,0:T(8,128)S(1)}, u32[]{:S(2)}, u32[]{:S(2)}) collective-permute-start(f32[8,512]{1,0:T(8,128)S(1)} %add.15), channel_id=1, source_target_pairs={{0,5},{1,4},{2,7},{3,6},{4,1},{5,0},{6,3},{7,2},{8,13},{9,12},{10,... | collective-permute-start | bytes 49160 | tf_op jit(solution)/shard_map/ppermute | solution.py:258
  51.4 3.2 %collective-permute-start.15 = (f32[8,512]{1,0:T(8,128)S(1)}, f32[8,512]{1,0:T(8,128)S(1)}, u32[]{:S(2)}, u32[]{:S(2)}) collective-permute-start(f32[8,512]{1,0:T(8,128)S(1)} %add.15), channel_id=1, source_target_pairs={{0,3},{1,2},{2,1},{3,0},{4,7},{5,6},{6,5},{7,4},{8,11},{9,10},{10,... | collective-permute-start | bytes 49160 | tf_op jit(solution)/shard_map/ppermute | solution.py:258
  54.5 4.1 %collective-permute-start.18 = (f32[8,512]{1,0:T(8,128)S(1)}, f32[8,512]{1,0:T(8,128)S(1)}, u32[]{:S(2)}, u32[]{:S(2)}) collective-permute-start(f32[8,512]{1,0:T(8,128)S(1)} %add_add_fusion), channel_id=1, source_target_pairs={{0,9},{1,8},{2,11},{3,10},{4,13},{5,12},{6,15},{7,14},{8,1},{9,0},... | collective-permute-start | bytes 49160 | tf_op jit(solution)/shard_map/ppermute | solution.py:258

commit v5 on v4

--- a/solution.py
+++ b/solution.py
@@ -82,25 +82,25 @@
     return moves
 
 
-def open_kernel(diag, sides, lower, upper, outer_out, inner_out, corners, strips, sems):
+def open_kernel(diag, sides, lower, upper, outer_out, corner, strip, sems):
     odd, _ = place()
     rows = sides.shape[0]
-    width, lanes = corners.shape[1:]
-    top = rows - width
-    moves = copies(
-        [
-            (diag.at[pl.ds(0, width), pl.ds(0, lanes)], corners.at[0]),
-            (diag.at[pl.ds(top, width), pl.ds(rows - lanes, lanes)], corners.at[1]),
-            (sides.at[pl.ds(0, width)], strips.at[0]),
-            (sides.at[pl.ds(top, width)], strips.at[1]),
-        ],
-        sems,
-    )
+    width, lanes = corner.shape
+    far, _ = rims(rows, width)
+    tile = pl.ds(pl.multiple_of(odd * (rows - lanes), lanes), lanes)
+    moves = copies([(diag.at[pl.ds(far, width), tile], corner), (sides.at[pl.ds(far, width)], strip)], sems)
     for move in moves:
         move.wait()
-    first = strips[0] / diagonal(corners[0], 0)
-    last = strips[1] / diagonal(corners[1], lanes - width)
-    outer_out[...] = facing(jnp.where(odd == 1, last, first))
+    outer_out[...] = facing(strip[...] / diagonal(corner[...], odd * (lanes - width)))
+
+
+def inner_kernel(diag, sides, inner_out):
+    odd, _ = place()
+    rows = sides.shape[0]
+    width, lanes = inner_out.shape[0], 128
+    top = rows - width
+    first = sides[:width, :] / diagonal(diag[:width, :lanes], 0)
+    last = sides[top:, :] / diagonal(diag[top:, rows - lanes :], lanes - width)
     inner_out[...] = jnp.where(odd == 1, first, last)
 
 
@@ -213,15 +213,17 @@
     v_out[...] = applied(side, diag, terms_out, start)
 
 
-def last_kernel(known, message, u, coupling, sums, r_out, sums_out, *, sweep):
+def last_kernel(known, message, u, coupling, sums, halo_out, sums_out, *, sweep):
     sums_out[...] = sums[...]
-    residual = u[...] - product(coupling[...], right_terms(message[...] - known[...]))
+    halo = right_terms(message[...] - known[...])
+    halo_out[...] = halo
+    residual = u[...] - product(coupling[...], halo)
     sums_out[sweep : sweep + 1, :] = jnp.sum(residual * residual, axis=0, keepdims=True)
-    r_out[...] = residual
-
-
-def close_kernel(r, x, scale, x_out):
-    x_out[...] = x[...] + r[...] * wide(scale[...], x.shape[1])
+
+
+def close_kernel(halo, u, coupling, x, scale, x_out):
+    residual = u[...] - product(coupling[...], halo[...])
+    x_out[...] = x[...] + residual * wide(scale[...], x.shape[1])
 
 
 def pairings():
@@ -268,18 +270,19 @@
     sums_shape = pltpu.VMEM((SWEEPS, columns), F32)
     lanes = 128
     lower, upper = lower_coupling.T, upper_coupling.T
-    outer, inner = call(
+    outer = call(
         open_kernel,
-        [rim, rim],
+        rim,
         diag_blocks, right_sides, lower, upper,
         hbm=(0, 1, 2, 3),
         scratch=[
-            pltpu.VMEM((2, width, lanes), F32),
-            pltpu.VMEM((2, width, columns), F32),
-            pltpu.SemaphoreType.DMA((4,)),
+            pltpu.VMEM((width, lanes), F32),
+            pltpu.VMEM((width, columns), F32),
+            pltpu.SemaphoreType.DMA((2,)),
         ],
     )
     message = across(outer)
+    inner = call(inner_kernel, rim, diag_blocks, right_sides, free=(0, 1))
     inner = along(inner)
     half = pltpu.VMEM((rows // 2, columns), F32)
     all_terms = pltpu.VMEM((2 * rows, columns), BF16)
@@ -338,13 +341,13 @@
             flops=3 * rows * (rows + 2 * width) * columns,
         )
         known, message = [kept], ahead
-    r, sums = call(
+    halo, sums = call(
         functools.partial(last_kernel, sweep=SWEEPS - 1),
-        [panel, sums_shape],
+        [halo_shape, sums_shape],
         *known, message, u, outward, sums,
         flops=6 * rows * width * columns,
     )
-    solution = call(close_kernel, jax.ShapeDtypeStruct((rows, columns), F32), r, x, scale, flops=10 * rows * columns)
+    solution = call(close_kernel, jax.ShapeDtypeStruct((rows, columns), F32), halo, u, outward, x, scale, flops=10 * rows * columns)
     return solution, jnp.sqrt(row_sum(sums))
 
 

time: 59.4 us -> 62 us (1.044)
  local copies, waits for them, and re-layouts: 0.02 us -> 2.46 us
    unnamed x8 -> x12, local copies, waits for them, and re-layouts: 0.02 us -> 2.46 us
    pallas_call x29 -> x30, Pallas kernels: 16.9 us -> 17.1 us  [call(): pl.pallas_call(kernel, out_shape=outs, in_specs=[HBM_BLOCK if i in hbm el...]
  transfers between devices with their start and end apart: 19 -> 19, of which waited for: 12 -> 12; matrix products, arithmetic and copies ran while one was open for 0% -> 0% of each run, Pallas kernels for 24% -> 25%
where the time goes in v5:
time: 62 us; the launch traced here: 61.7 us
  starting transfers between devices  26.2 us (42%)
  Pallas kernels  17.1 us (28%)
  waiting for transfers between devices  14.6 us (24%)
  local copies, waits for them, and re-layouts  2.46 us (4%)
  between operations  0.87 us (1%)
  other arithmetic  0.63 us (1%)
    pallas_call x30, Pallas kernels, call(): pl.pallas_call(kernel, out_shape=outs, in_specs=[HBM_BLOCK if i in hbm el...  17.1 us
    ppermute x7, starting transfers between devices, across(): return lax.ppermute(outer, ('grp', 'row'), pairings()[1])  12.6 us
    ppermute x7, waiting for transfers between devices, across(): return lax.ppermute(outer, ('grp', 'row'), pairings()[1])  11.2 us
    ppermute x5, starting transfers between devices, row_sum(): lax.ppermute(x, 'row', [(i, i ^ f) for i in range(size)])  8.53 us
    ppermute x7, starting transfers between devices, along(): return lax.ppermute(inner, 'row', pairings()[0])  4.99 us
    ppermute x5, waiting for transfers between devices, row_sum(): lax.ppermute(x, 'row', [(i, i ^ f) for i in range(size)])  3.37 us
    unnamed x12, local copies, waits for them, and re-layouts  2.46 us
  transfers between devices with their start and end apart: 19, of which 12 were waited for; matrix products, arithmetic and copies ran while one was open for 0% of the time, Pallas kernels for 25%

profile of v5, /device:TPU:0, one launch (start us, length us, event | category | flops | bytes accessed | tf_op | source)
XLA Modules:
  0.0 61.7 jit_solution(7727270742907202740)
XLA Ops:
  0.6 1.2 %copy-done = f32[512,512]{1,0:T(8,128)S(1)} copy-done((f32[512,512]{1,0:T(8,128)S(1)}, f32[512,512]{1,0:T(8,128)}, u32[]{:S(2)}) %copy-start) | copy-done | bytes 1048600
  1.9 1.2 %copy-done.2 = f32[512,512]{1,0:T(8,128)S(1)} copy-done((f32[512,512]{1,0:T(8,128)S(1)}, f32[512,512]{1,0:T(8,128)}, u32[]{:S(2)}) %copy-start.2) | copy-done | bytes 1048600
  3.8 1.2 %shard_map.59 = f32[64,512]{1,0:T(8,128)S(1)} custom-call(f32[512,512]{1,0:T(8,128)} %diag.3, f32[512,512]{1,0:T(8,128)} %side.13, f32[64,512]{1,0:T(8,128)} %bitcast.2, f32[64,512]{1,0:T(8,128)} %bitcast.4), custom_call_target="tpu_custom_call" | custom-call | tf_op jit(solution)/shard_map/pallas_call | solution.py:22
  5.0 2.6 %collective-permute-start = (f32[64,512]{1,0:T(8,128)S(1)}, f32[64,512]{1,0:T(8,128)S(1)}, u32[]{:S(2)}, u32[]{:S(2)}) collective-permute-start(f32[64,512]{1,0:T(8,128)S(1)} %shard_map.59), channel_id=1, source_target_pairs={{0,16},{1,2},{2,1},{3,4},{4,3},{5,6},{6,5},{7,8},{8,7},{9,10},{10,... | collective-permute-start | bytes 393224 | tf_op jit(solution)/shard_map/ppermute | solution.py:247
  7.6 1.0 %shard_map.60 = (bf16[512,1024]{1,0:T(8,128)(2,1)S(1)}, bf16[512,192]{1,0:T(8,128)(2,1)S(1)}, bf16[512,192]{1,0:T(8,128)(2,1)S(1)}, f32[8,512]{1,0:T(8,128)S(1)}...) custom-call(f32[512,512]{1,0:T(8,128)S(1)} %copy-done.3, ...), custom_call_target="tpu_custom_call" | custom-call | flops 402653184 | tf_op jit(solution)/shard_map/pallas_call | solution.py:22
  9.4 1.2 %collective-permute-done.refs_0_ = f32[64,512]{1,0:T(8,128)S(1)} collective-permute-done((f32[64,512]{1,0:T(8,128)S(1)}, f32[64,512]{1,0:T(8,128)S(1)}, u32[]{:S(2)}, u32[]{:S(2)}) %collective-permute-start) | collective-permute-done | bytes 131104 | tf_op jit(solution)/shard_map/ppermute | solution.py:247
  11.0 2.1 %collective-permute-start.2 = (f32[72,512]{1,0:T(8,128)S(1)}, f32[72,512]{1,0:T(8,128)S(1)}, u32[]{:S(2)}, u32[]{:S(2)}) collective-permute-start(f32[72,512]{1,0:T(8,128)S(1)} %shard_map.65), channel_id=1, source_target_pairs={{0,16},{1,2},{2,1},{3,4},{4,3},{5,6},{6,5},{7,8},{8,7},{9,10},{10,... | collective-permute-start | bytes 442376 | tf_op jit(solution)/shard_map/ppermute | solution.py:247
  14.8 1.4 %collective-permute-done.2.refs_1_ = f32[72,512]{1,0:T(8,128)S(1)} collective-permute-done((f32[72,512]{1,0:T(8,128)S(1)}, f32[72,512]{1,0:T(8,128)S(1)}, u32[]{:S(2)}, u32[]{:S(2)}) %collective-permute-start.2) | collective-permute-done | bytes 147488 | tf_op jit(solution)/shard_map/ppermute | solution.py:247
  16.7 1.4 %collective-permute-start.5 = (f32[64,512]{1,0:T(8,128)S(1)}, f32[64,512]{1,0:T(8,128)S(1)}, u32[]{:S(2)}, u32[]{:S(2)}) collective-permute-start(f32[64,512]{1,0:T(8,128)S(1)} %get-tuple-element.76), channel_id=1, source_target_pairs={{0,1},{1,0},{2,3},{3,2},{4,5},{5,4},{6,7},{7,6},{8,9},{9,8},{10,11... | collective-permute-start | bytes 393224 | tf_op jit(solution)/shard_map/ppermute | solution.py:251
  18.2 1.6 %collective-permute-start.4 = (f32[64,512]{1,0:T(8,128)S(1)}, f32[64,512]{1,0:T(8,128)S(1)}, u32[]{:S(2)}, u32[]{:S(2)}) collective-permute-start(f32[64,512]{1,0:T(8,128)S(1)} %shard_map.69), channel_id=1, source_target_pairs={{0,16},{1,2},{2,1},{3,4},{4,3},{5,6},{6,5},{7,8},{8,7},{9,10},{10,... | collective-permute-start | bytes 393224 | tf_op jit(solution)/shard_map/ppermute | solution.py:247
  21.5 1.7 %collective-permute-done.4.refs_1_ = f32[64,512]{1,0:T(8,128)S(1)} collective-permute-done((f32[64,512]{1,0:T(8,128)S(1)}, f32[64,512]{1,0:T(8,128)S(1)}, u32[]{:S(2)}, u32[]{:S(2)}) %collective-permute-start.4) | collective-permute-done | bytes 131104 | tf_op jit(solution)/shard_map/ppermute | solution.py:247
  23.8 1.6 %collective-permute-start.6 = (f32[64,512]{1,0:T(8,128)S(1)}, f32[64,512]{1,0:T(8,128)S(1)}, u32[]{:S(2)}, u32[]{:S(2)}) collective-permute-start(f32[64,512]{1,0:T(8,128)S(1)} %shard_map.73), channel_id=1, source_target_pairs={{0,16},{1,2},{2,1},{3,4},{4,3},{5,6},{6,5},{7,8},{8,7},{9,10},{10,... | collective-permute-start | bytes 393224 | tf_op jit(solution)/shard_map/ppermute | solution.py:247
  27.1 1.7 %collective-permute-done.6.refs_1_ = f32[64,512]{1,0:T(8,128)S(1)} collective-permute-done((f32[64,512]{1,0:T(8,128)S(1)}, f32[64,512]{1,0:T(8,128)S(1)}, u32[]{:S(2)}, u32[]{:S(2)}) %collective-permute-start.6) | collective-permute-done | bytes 131104 | tf_op jit(solution)/shard_map/ppermute | solution.py:247
  30.1 1.6 %collective-permute-start.8 = (f32[64,512]{1,0:T(8,128)S(1)}, f32[64,512]{1,0:T(8,128)S(1)}, u32[]{:S(2)}, u32[]{:S(2)}) collective-permute-start(f32[64,512]{1,0:T(8,128)S(1)} %shard_map.77), channel_id=1, source_target_pairs={{0,16},{1,2},{2,1},{3,4},{4,3},{5,6},{6,5},{7,8},{8,7},{9,10},{10,... | collective-permute-start | bytes 393224 | tf_op jit(solution)/shard_map/ppermute | solution.py:247
  31.7 1.0 %shard_map.76 = (f32[512,512]{1,0:T(8,128)S(1)}, bf16[1024,512]{1,0:T(8,128)(2,1)S(1)}, f32[256,512]{1,0:T(8,128)S(1)}, f32[64,512]{1,0:T(8,128)S(1)}, f32[8,512]{1,0:T(8,128)S(1)}) custom-call(bf16[64,192]{1,0:T(8,128)(2,1)S(1)} %get-tuple-element.71.refs_0_, bf16[192,512]{1,0:T(8,128)(2,1)S(1)} %get-tuple-element.86.refs_1_, ...), custom_call_target="tpu_custom_call" | custom-call | flops 503316480 | tf_op jit(solution)/shard_map/pallas_call | solution.py:22
  33.4 1.7 %collective-permute-done.8.refs_1_ = f32[64,512]{1,0:T(8,128)S(1)} collective-permute-done((f32[64,512]{1,0:T(8,128)S(1)}, f32[64,512]{1,0:T(8,128)S(1)}, u32[]{:S(2)}, u32[]{:S(2)}) %collective-permute-start.8) | collective-permute-done | bytes 131104 | tf_op jit(solution)/shard_map/ppermute | solution.py:247
  36.4 1.6 %collective-permute-start.10 = (f32[64,512]{1,0:T(8,128)S(1)}, f32[64,512]{1,0:T(8,128)S(1)}, u32[]{:S(2)}, u32[]{:S(2)}) collective-permute-start(f32[64,512]{1,0:T(8,128)S(1)} %shard_map.81), channel_id=1, source_target_pairs={{0,16},{1,2},{2,1},{3,4},{4,3},{5,6},{6,5},{7,8},{8,7},{9,10},{10,... | collective-permute-start | bytes 393224 | tf_op jit(solution)/shard_map/ppermute | solution.py:247
  39.7 1.7 %collective-permute-done.10.refs_1_ = f32[64,512]{1,0:T(8,128)S(1)} collective-permute-done((f32[64,512]{1,0:T(8,128)S(1)}, f32[64,512]{1,0:T(8,128)S(1)}, u32[]{:S(2)}, u32[]{:S(2)}) %collective-permute-start.10) | collective-permute-done | bytes 131104 | tf_op jit(solution)/shard_map/ppermute | solution.py:247
  42.6 1.6 %collective-permute-start.12 = (f32[64,512]{1,0:T(8,128)S(1)}, f32[64,512]{1,0:T(8,128)S(1)}, u32[]{:S(2)}, u32[]{:S(2)}) collective-permute-start(f32[64,512]{1,0:T(8,128)S(1)} %shard_map.85), channel_id=1, source_target_pairs={{0,16},{1,2},{2,1},{3,4},{4,3},{5,6},{6,5},{7,8},{8,7},{9,10},{10,... | collective-permute-start | bytes 393224 | tf_op jit(solution)/shard_map/ppermute | solution.py:247
  45.9 1.7 %collective-permute-done.12.message = f32[64,512]{1,0:T(8,128)S(1)} collective-permute-done((f32[64,512]{1,0:T(8,128)S(1)}, f32[64,512]{1,0:T(8,128)S(1)}, u32[]{:S(2)}, u32[]{:S(2)}) %collective-permute-start.12) | collective-permute-done | bytes 131104 | tf_op jit(solution)/shard_map/ppermute | solution.py:247
  49.7 4.0 %collective-permute-start.17 = (f32[8,512]{1,0:T(8,128)S(1)}, f32[8,512]{1,0:T(8,128)S(1)}, u32[]{:S(2)}, u32[]{:S(2)}) collective-permute-start(f32[8,512]{1,0:T(8,128)S(1)} %add.15), channel_id=1, source_target_pairs={{0,6},{1,7},{2,4},{3,5},{4,2},{5,3},{6,0},{7,1},{8,14},{9,15},{10,... | collective-permute-start | bytes 49160 | tf_op jit(solution)/shard_map/ppermute | solution.py:260
  55.5 1.4 %collective-permute-done.16 = f32[8,512]{1,0:T(8,128)S(1)} collective-permute-done((f32[8,512]{1,0:T(8,128)S(1)}, f32[8,512]{1,0:T(8,128)S(1)}, u32[]{:S(2)}, u32[]{:S(2)}) %collective-permute-start.16) | collective-permute-done | bytes 16416 | tf_op jit(solution)/shard_map/ppermute | solution.py:260
  57.0 2.6 %collective-permute-start.18 = (f32[8,512]{1,0:T(8,128)S(1)}, f32[8,512]{1,0:T(8,128)S(1)}, u32[]{:S(2)}, u32[]{:S(2)}) collective-permute-start(f32[8,512]{1,0:T(8,128)S(1)} %add_add_fusion), channel_id=1, source_target_pairs={{0,9},{1,8},{2,11},{3,10},{4,13},{5,12},{6,15},{7,14},{8,1},{9,0},... | collective-permute-start | bytes 49160 | tf_op jit(solution)/shard_map/ppermute | solution.py:260
  59.7 1.3 %shard_map.88 = f32[512,512]{1,0:T(8,128)} custom-call(bf16[192,512]{1,0:T(8,128)(2,1)S(1)} %get-tuple-element.107.halo, f32[512,512]{1,0:T(8,128)S(1)} %shard_map.86.u, bf16[512,192]{1,0:T(8,128)(2,1)S(1)} %get-tuple-element.61.refs_3_.refs_6_.refs_4_.refs_7_.coupling, f32[512,512]{1,0:T(8,128)S(1)} %get-tuple-element.108.x, ...), custom_call_target="tpu_custom_call" | custom-call | flops 2621440 | tf_op jit(solution)/shard_map/pallas_call | solution.py:22
  (59 shorter events, 20.6 us)
Async XLA Ops:
  0.6 1.2 %copy-start = (f32[512,512]{1,0:T(8,128)S(1)}, f32[512,512]{1,0:T(8,128)}, u32[]{:S(2)}) copy-start(f32[512,512]{1,0:T(8,128)} %side.13) | copy-start | bytes 3145732
  3.2 5.5 %collective-permute-start.1 = (f32[64,512]{1,0:T(8,128)S(1)}, f32[64,512]{1,0:T(8,128)S(1)}, u32[]{:S(2)}, u32[]{:S(2)}) collective-permute-start(f32[64,512]{1,0:T(8,128)S(1)} %shard_map.61), channel_id=1, source_target_pairs={{0,1},{1,0},{2,3},{3,2},{4,5},{5,4},{6,7},{7,6},{8,9},{9,8},{10,11... | collective-permute-start | bytes 393224 | tf_op jit(solution)/shard_map/ppermute | solution.py:251
  3.7 3.8 %copy-start.1 = (f32[512,512]{1,0:T(8,128)S(1)}, f32[512,512]{1,0:T(8,128)}, u32[]{:S(2)}) copy-start(f32[512,512]{1,0:T(8,128)} %side.13) | copy-start | bytes 3145732
  3.8 3.8 %copy-start.3 = (f32[512,512]{1,0:T(8,128)S(1)}, f32[512,512]{1,0:T(8,128)}, u32[]{:S(2)}) copy-start(f32[512,512]{1,0:T(8,128)} %diag.3) | copy-start | bytes 3145732
  3.8 3.8 %copy-start.4 = (f32[512,64]{0,1:T(8,128)S(1)}, f32[512,64]{0,1:T(8,128)}, u32[]{:S(2)}) copy-start(f32[512,64]{0,1:T(8,128)} %param.5) | copy-start | bytes 393220
  3.8 3.8 %copy-start.5 = (f32[512,64]{0,1:T(8,128)S(1)}, f32[512,64]{0,1:T(8,128)}, u32[]{:S(2)}) copy-start(f32[512,64]{0,1:T(8,128)} %param.6) | copy-start | bytes 393220
  5.0 5.6 %collective-permute-start = (f32[64,512]{1,0:T(8,128)S(1)}, f32[64,512]{1,0:T(8,128)S(1)}, u32[]{:S(2)}, u32[]{:S(2)}) collective-permute-start(f32[64,512]{1,0:T(8,128)S(1)} %shard_map.59), channel_id=1, source_target_pairs={{0,16},{1,2},{2,1},{3,4},{4,3},{5,6},{6,5},{7,8},{8,7},{9,10},{10,... | collective-permute-start | bytes 393224 | tf_op jit(solution)/shard_map/ppermute | solution.py:247
  10.7 3.4 %collective-permute-start.3 = (f32[64,512]{1,0:T(8,128)S(1)}, f32[64,512]{1,0:T(8,128)S(1)}, u32[]{:S(2)}, u32[]{:S(2)}) collective-permute-start(f32[64,512]{1,0:T(8,128)S(1)} %get-tuple-element.68), channel_id=1, source_target_pairs={{0,1},{1,0},{2,3},{3,2},{4,5},{5,4},{6,7},{7,6},{8,9},{9,8},{10,11... | collective-permute-start | bytes 393224 | tf_op jit(solution)/shard_map/ppermute | solution.py:251
  11.0 5.2 %collective-permute-start.2 = (f32[72,512]{1,0:T(8,128)S(1)}, f32[72,512]{1,0:T(8,128)S(1)}, u32[]{:S(2)}, u32[]{:S(2)}) collective-permute-start(f32[72,512]{1,0:T(8,128)S(1)} %shard_map.65), channel_id=1, source_target_pairs={{0,16},{1,2},{2,1},{3,4},{4,3},{5,6},{6,5},{7,8},{8,7},{9,10},{10,... | collective-permute-start | bytes 442376 | tf_op jit(solution)/shard_map/ppermute | solution.py:247
  16.7 4.1 %collective-permute-start.5 = (f32[64,512]{1,0:T(8,128)S(1)}, f32[64,512]{1,0:T(8,128)S(1)}, u32[]{:S(2)}, u32[]{:S(2)}) collective-permute-start(f32[64,512]{1,0:T(8,128)S(1)} %get-tuple-element.76), channel_id=1, source_target_pairs={{0,1},{1,0},{2,3},{3,2},{4,5},{5,4},{6,7},{7,6},{8,9},{9,8},{10,11... | collective-permute-start | bytes 393224 | tf_op jit(solution)/shard_map/ppermute | solution.py:251
  18.2 5.0 %collective-permute-start.4 = (f32[64,512]{1,0:T(8,128)S(1)}, f32[64,512]{1,0:T(8,128)S(1)}, u32[]{:S(2)}, u32[]{:S(2)}) collective-permute-start(f32[64,512]{1,0:T(8,128)S(1)} %shard_map.69), channel_id=1, source_target_pairs={{0,16},{1,2},{2,1},{3,4},{4,3},{5,6},{6,5},{7,8},{8,7},{9,10},{10,... | collective-permute-start | bytes 393224 | tf_op jit(solution)/shard_map/ppermute | solution.py:247
  23.4 3.0 %collective-permute-start.7 = (f32[64,512]{1,0:T(8,128)S(1)}, f32[64,512]{1,0:T(8,128)S(1)}, u32[]{:S(2)}, u32[]{:S(2)}) collective-permute-start(f32[64,512]{1,0:T(8,128)S(1)} %get-tuple-element.83), channel_id=1, source_target_pairs={{0,1},{1,0},{2,3},{3,2},{4,5},{5,4},{6,7},{7,6},{8,9},{9,8},{10,11... | collective-permute-start | bytes 393224 | tf_op jit(solution)/shard_map/ppermute | solution.py:251
  23.8 5.0 %collective-permute-start.6 = (f32[64,512]{1,0:T(8,128)S(1)}, f32[64,512]{1,0:T(8,128)S(1)}, u32[]{:S(2)}, u32[]{:S(2)}) collective-permute-start(f32[64,512]{1,0:T(8,128)S(1)} %shard_map.73), channel_id=1, source_target_pairs={{0,16},{1,2},{2,1},{3,4},{4,3},{5,6},{6,5},{7,8},{8,7},{9,10},{10,... | collective-permute-start | bytes 393224 | tf_op jit(solution)/shard_map/ppermute | solution.py:247
  29.0 3.6 %collective-permute-start.9 = (f32[64,512]{1,0:T(8,128)S(1)}, f32[64,512]{1,0:T(8,128)S(1)}, u32[]{:S(2)}, u32[]{:S(2)}) collective-permute-start(f32[64,512]{1,0:T(8,128)S(1)} %get-tuple-element.90), channel_id=1, source_target_pairs={{0,1},{1,0},{2,3},{3,2},{4,5},{5,4},{6,7},{7,6},{8,9},{9,8},{10,11... | collective-permute-start | bytes 393224 | tf_op jit(solution)/shard_map/ppermute | solution.py:251
  30.1 5.0 %collective-permute-start.8 = (f32[64,512]{1,0:T(8,128)S(1)}, f32[64,512]{1,0:T(8,128)S(1)}, u32[]{:S(2)}, u32[]{:S(2)}) collective-permute-start(f32[64,512]{1,0:T(8,128)S(1)} %shard_map.77), channel_id=1, source_target_pairs={{0,16},{1,2},{2,1},{3,4},{4,3},{5,6},{6,5},{7,8},{8,7},{9,10},{10,... | collective-permute-start | bytes 393224 | tf_op jit(solution)/shard_map/ppermute | solution.py:247
  35.3 3.7 %collective-permute-start.11 = (f32[64,512]{1,0:T(8,128)S(1)}, f32[64,512]{1,0:T(8,128)S(1)}, u32[]{:S(2)}, u32[]{:S(2)}) collective-permute-start(f32[64,512]{1,0:T(8,128)S(1)} %get-tuple-element.97), channel_id=1, source_target_pairs={{0,1},{1,0},{2,3},{3,2},{4,5},{5,4},{6,7},{7,6},{8,9},{9,8},{10,11... | collective-permute-start | bytes 393224 | tf_op jit(solution)/shard_map/ppermute | solution.py:251
  36.4 5.0 %collective-permute-start.10 = (f32[64,512]{1,0:T(8,128)S(1)}, f32[64,512]{1,0:T(8,128)S(1)}, u32[]{:S(2)}, u32[]{:S(2)}) collective-permute-start(f32[64,512]{1,0:T(8,128)S(1)} %shard_map.81), channel_id=1, source_target_pairs={{0,16},{1,2},{2,1},{3,4},{4,3},{5,6},{6,5},{7,8},{8,7},{9,10},{10,... | collective-permute-start | bytes 393224 | tf_op jit(solution)/shard_map/ppermute | solution.py:247
  41.6 3.6 %collective-permute-start.13 = (f32[64,512]{1,0:T(8,128)S(1)}, f32[64,512]{1,0:T(8,128)S(1)}, u32[]{:S(2)}, u32[]{:S(2)}) collective-permute-start(f32[64,512]{1,0:T(8,128)S(1)} %get-tuple-element.103), channel_id=1, source_target_pairs={{0,1},{1,0},{2,3},{3,2},{4,5},{5,4},{6,7},{7,6},{8,9},{9,8},{10,11... | collective-permute-start | bytes 393224 | tf_op jit(solution)/shard_map/ppermute | solution.py:251
  42.6 5.0 %collective-permute-start.12 = (f32[64,512]{1,0:T(8,128)S(1)}, f32[64,512]{1,0:T(8,128)S(1)}, u32[]{:S(2)}, u32[]{:S(2)}) collective-permute-start(f32[64,512]{1,0:T(8,128)S(1)} %shard_map.85), channel_id=1, source_target_pairs={{0,16},{1,2},{2,1},{3,4},{4,3},{5,6},{6,5},{7,8},{8,7},{9,10},{10,... | collective-permute-start | bytes 393224 | tf_op jit(solution)/shard_map/ppermute | solution.py:247
  48.0 1.8 %collective-permute-start.14 = (f32[8,512]{1,0:T(8,128)S(1)}, f32[8,512]{1,0:T(8,128)S(1)}, u32[]{:S(2)}, u32[]{:S(2)}) collective-permute-start(f32[8,512]{1,0:T(8,128)S(1)} %get-tuple-element.109), channel_id=1, source_target_pairs={{0,1},{1,0},{2,3},{3,2},{4,5},{5,4},{6,7},{7,6},{8,9},{9,8},{10,11... | collective-permute-start | bytes 49160 | tf_op jit(solution)/shard_map/ppermute | solution.py:260
  49.7 5.7 %collective-permute-start.17 = (f32[8,512]{1,0:T(8,128)S(1)}, f32[8,512]{1,0:T(8,128)S(1)}, u32[]{:S(2)}, u32[]{:S(2)}) collective-permute-start(f32[8,512]{1,0:T(8,128)S(1)} %add.15), channel_id=1, source_target_pairs={{0,6},{1,7},{2,4},{3,5},{4,2},{5,3},{6,0},{7,1},{8,14},{9,15},{10,... | collective-permute-start | bytes 49160 | tf_op jit(solution)/shard_map/ppermute | solution.py:260
  53.7 3.2 %collective-permute-start.16 = (f32[8,512]{1,0:T(8,128)S(1)}, f32[8,512]{1,0:T(8,128)S(1)}, u32[]{:S(2)}, u32[]{:S(2)}) collective-permute-start(f32[8,512]{1,0:T(8,128)S(1)} %add.15), channel_id=1, source_target_pairs={{0,5},{1,4},{2,7},{3,6},{4,1},{5,0},{6,3},{7,2},{8,13},{9,12},{10,... | collective-permute-start | bytes 49160 | tf_op jit(solution)/shard_map/ppermute | solution.py:260
  53.9 3.2 %collective-permute-start.15 = (f32[8,512]{1,0:T(8,128)S(1)}, f32[8,512]{1,0:T(8,128)S(1)}, u32[]{:S(2)}, u32[]{:S(2)}) collective-permute-start(f32[8,512]{1,0:T(8,128)S(1)} %add.15), channel_id=1, source_target_pairs={{0,3},{1,2},{2,1},{3,0},{4,7},{5,6},{6,5},{7,4},{8,11},{9,10},{10,... | collective-permute-start | bytes 49160 | tf_op jit(solution)/shard_map/ppermute | solution.py:260
  57.0 4.1 %collective-permute-start.18 = (f32[8,512]{1,0:T(8,128)S(1)}, f32[8,512]{1,0:T(8,128)S(1)}, u32[]{:S(2)}, u32[]{:S(2)}) collective-permute-start(f32[8,512]{1,0:T(8,128)S(1)} %add_add_fusion), channel_id=1, source_target_pairs={{0,9},{1,8},{2,11},{3,10},{4,13},{5,12},{6,15},{7,14},{8,1},{9,0},... | collective-permute-start | bytes 49160 | tf_op jit(solution)/shard_map/ppermute | solution.py:260
  (1 other events, 1.2 us)

commit v6 on v5

--- a/solution.py
+++ b/solution.py
@@ -114,9 +114,11 @@
     x = side * scale
     x_out[...] = x
     terms_out[...] = both(x, 0)
-    diag_out[...] = both(block[...], 1)
-    far, _ = spans(rows)
-    v_out[...] = applied(sides, diag_out, terms_out, far)
+    early, late = spans(rows)
+    cut = 2 * early.size
+    diag_out[:cut, :] = both(block[early, :], 0)
+    diag_out[cut:, :] = both(block[late, :], 0)
+    v_out[...] = applied(sides, diag_out, terms_out, early, 0)
     low, up = low[...], up[...]
     outer = jnp.where(odd == 1, up, low).T
     outer_out[...] = left_terms(outer)
@@ -134,18 +136,23 @@
     return jnp.concatenate([strip[:, i : i + width] for i in range(0, width * width // 8, width)], axis=0)
 
 
+def early_rows(rows):
+    return rows * 9 // 16
+
+
 def spans(rows):
     odd, _ = place()
-    half = rows // 2
-    return pl.multiple_of(odd * half, half), pl.multiple_of((1 - odd) * half, half)
-
-
-def applied(side, diag, terms, start):
-    rows = side.shape[0]
-    some = pl.ds(start, rows // 2)
-    high, low = diag[some, :rows], diag[some, rows:]
-    images = product(high, terms[rows:, :]) + product(low, terms[:rows, :]) + product(high, terms[:rows, :])
-    return side[some, :] - images
+    early = early_rows(rows)
+    late = rows - early
+    tile = 32
+    return pl.ds(pl.multiple_of(odd * late, tile), early), pl.ds(pl.multiple_of((1 - odd) * early, tile), late)
+
+
+def applied(side, diag, terms, span, first):
+    rows, some = side.shape[0], span.size
+    images = product(diag[first : first + 2 * some, :], terms[:rows, :])
+    images = images[:some] + images[some:] + product(diag[first : first + some, :], terms[rows:, :])
+    return side[span, :] - images
 
 
 def wide(pivots, columns):
@@ -167,11 +174,10 @@
 
 
 def fill_kernel(inner, terms, v, side, diag, coupling, u_out):
-    far, near = spans(side.shape[0])
-    half = v.shape[0]
+    early, late = spans(side.shape[0])
     halo = right_terms(inner[...])
-    u_out[pl.ds(far, half), :] = v[...] - product(coupling[pl.ds(far, half), :], halo)
-    u_out[pl.ds(near, half), :] = applied(side, diag, terms, near) - product(coupling[pl.ds(near, half), :], halo)
+    u_out[early, :] = v[...] - product(coupling[early, :], halo)
+    u_out[late, :] = applied(side, diag, terms, late, 2 * early.size) - product(coupling[late, :], halo)
 
 
 def rim_kernel(*refs, sweep):
@@ -209,8 +215,8 @@
     new = x[...] + residual * wide(scale[...], columns)
     x_out[...] = new
     terms_out[...] = both(new, 0)
-    start, _ = spans(rows)
-    v_out[...] = applied(side, diag, terms_out, start)
+    early, _ = spans(rows)
+    v_out[...] = applied(side, diag, terms_out, early, 0)
 
 
 def last_kernel(known, message, u, coupling, sums, halo_out, sums_out, *, sweep):
@@ -284,13 +290,13 @@
     message = across(outer)
     inner = call(inner_kernel, rim, diag_blocks, right_sides, free=(0, 1))
     inner = along(inner)
-    half = pltpu.VMEM((rows // 2, columns), F32)
+    half = pltpu.VMEM((early_rows(rows), columns), F32)
     all_terms = pltpu.VMEM((2 * rows, columns), BF16)
     coupling_shape = pltpu.VMEM((rows, 3 * width), BF16)
     diag, outward, inward, told, scale, x, terms, v, sums = call(
         setup_kernel,
         [
-            pltpu.VMEM((rows, 2 * rows), BF16),
+            pltpu.VMEM((2 * rows, rows), BF16),
             coupling_shape,
             coupling_shape,
             pltpu.VMEM((8, width * width // 8), F32),

time: 62 us -> 62 us (level)
  transfers between devices with their start and end apart: 19 -> 19, of which waited for: 12 -> 12; matrix products, arithmetic and copies ran while one was open for 0% -> 0% of each run, Pallas kernels for 25% -> 24%
where the time goes in v6:
time: 62 us; the launch traced here: 61.7 us
  starting transfers between devices  26.2 us (42%)
  Pallas kernels  16.6 us (27%)
  waiting for transfers between devices  15.1 us (24%)
  local copies, waits for them, and re-layouts  2.46 us (4%)
  between operations  0.86 us (1%)
  other arithmetic  0.63 us (1%)
    pallas_call x30, Pallas kernels, call(): pl.pallas_call(kernel, out_shape=outs, in_specs=[HBM_BLOCK if i in hbm el...  16.6 us
    ppermute x7, starting transfers between devices, across(): return lax.ppermute(outer, ('grp', 'row'), pairings()[1])  12.6 us
    ppermute x7, waiting for transfers between devices, across(): return lax.ppermute(outer, ('grp', 'row'), pairings()[1])  11.7 us
    ppermute x5, starting transfers between devices, row_sum(): lax.ppermute(x, 'row', [(i, i ^ f) for i in range(size)])  8.53 us
    ppermute x7, starting transfers between devices, along(): return lax.ppermute(inner, 'row', pairings()[0])  4.99 us
    ppermute x5, waiting for transfers between devices, row_sum(): lax.ppermute(x, 'row', [(i, i ^ f) for i in range(size)])  3.37 us
    unnamed x12, local copies, waits for them, and re-layouts  2.46 us
  transfers between devices with their start and end apart: 19, of which 12 were waited for; matrix products, arithmetic and copies ran while one was open for 0% of the time, Pallas kernels for 24%

profile of v6, /device:TPU:0, one launch (start us, length us, event | category | flops | bytes accessed | tf_op | source)
XLA Modules:
  0.0 61.7 jit_solution(5094197549946757210)
XLA Ops:
  0.6 1.2 %copy-done = f32[512,512]{1,0:T(8,128)S(1)} copy-done((f32[512,512]{1,0:T(8,128)S(1)}, f32[512,512]{1,0:T(8,128)}, u32[]{:S(2)}) %copy-start) | copy-done | bytes 1048600
  1.9 1.2 %copy-done.2 = f32[512,512]{1,0:T(8,128)S(1)} copy-done((f32[512,512]{1,0:T(8,128)S(1)}, f32[512,512]{1,0:T(8,128)}, u32[]{:S(2)}) %copy-start.2) | copy-done | bytes 1048600
  3.8 1.2 %shard_map.59 = f32[64,512]{1,0:T(8,128)S(1)} custom-call(f32[512,512]{1,0:T(8,128)} %diag.3, f32[512,512]{1,0:T(8,128)} %side.13, f32[64,512]{1,0:T(8,128)} %bitcast.2, f32[64,512]{1,0:T(8,128)} %bitcast.4), custom_call_target="tpu_custom_call" | custom-call | tf_op jit(solution)/shard_map/pallas_call | solution.py:22
  5.0 2.6 %collective-permute-start = (f32[64,512]{1,0:T(8,128)S(1)}, f32[64,512]{1,0:T(8,128)S(1)}, u32[]{:S(2)}, u32[]{:S(2)}) collective-permute-start(f32[64,512]{1,0:T(8,128)S(1)} %shard_map.59), channel_id=1, source_target_pairs={{0,16},{1,2},{2,1},{3,4},{4,3},{5,6},{6,5},{7,8},{8,7},{9,10},{10,... | collective-permute-start | bytes 393224 | tf_op jit(solution)/shard_map/ppermute | solution.py:253
  7.6 1.0 %shard_map.60 = (bf16[1024,512]{1,0:T(8,128)(2,1)S(1)}, bf16[512,192]{1,0:T(8,128)(2,1)S(1)}, bf16[512,192]{1,0:T(8,128)(2,1)S(1)}, f32[8,512]{1,0:T(8,128)S(1)}...) custom-call(f32[512,512]{1,0:T(8,128)S(1)} %copy-done.3, ...), custom_call_target="tpu_custom_call" | custom-call | flops 402653184 | tf_op jit(solution)/shard_map/pallas_call | solution.py:22
  9.3 1.3 %collective-permute-done.refs_0_ = f32[64,512]{1,0:T(8,128)S(1)} collective-permute-done((f32[64,512]{1,0:T(8,128)S(1)}, f32[64,512]{1,0:T(8,128)S(1)}, u32[]{:S(2)}, u32[]{:S(2)}) %collective-permute-start) | collective-permute-done | bytes 131104 | tf_op jit(solution)/shard_map/ppermute | solution.py:253
  11.0 2.1 %collective-permute-start.2 = (f32[72,512]{1,0:T(8,128)S(1)}, f32[72,512]{1,0:T(8,128)S(1)}, u32[]{:S(2)}, u32[]{:S(2)}) collective-permute-start(f32[72,512]{1,0:T(8,128)S(1)} %shard_map.65), channel_id=1, source_target_pairs={{0,16},{1,2},{2,1},{3,4},{4,3},{5,6},{6,5},{7,8},{8,7},{9,10},{10,... | collective-permute-start | bytes 442376 | tf_op jit(solution)/shard_map/ppermute | solution.py:253
  14.8 1.5 %collective-permute-done.2.refs_1_ = f32[72,512]{1,0:T(8,128)S(1)} collective-permute-done((f32[72,512]{1,0:T(8,128)S(1)}, f32[72,512]{1,0:T(8,128)S(1)}, u32[]{:S(2)}, u32[]{:S(2)}) %collective-permute-start.2) | collective-permute-done | bytes 147488 | tf_op jit(solution)/shard_map/ppermute | solution.py:253
  16.7 1.4 %collective-permute-start.5 = (f32[64,512]{1,0:T(8,128)S(1)}, f32[64,512]{1,0:T(8,128)S(1)}, u32[]{:S(2)}, u32[]{:S(2)}) collective-permute-start(f32[64,512]{1,0:T(8,128)S(1)} %get-tuple-element.76), channel_id=1, source_target_pairs={{0,1},{1,0},{2,3},{3,2},{4,5},{5,4},{6,7},{7,6},{8,9},{9,8},{10,11... | collective-permute-start | bytes 393224 | tf_op jit(solution)/shard_map/ppermute | solution.py:257
  18.2 1.6 %collective-permute-start.4 = (f32[64,512]{1,0:T(8,128)S(1)}, f32[64,512]{1,0:T(8,128)S(1)}, u32[]{:S(2)}, u32[]{:S(2)}) collective-permute-start(f32[64,512]{1,0:T(8,128)S(1)} %shard_map.69), channel_id=1, source_target_pairs={{0,16},{1,2},{2,1},{3,4},{4,3},{5,6},{6,5},{7,8},{8,7},{9,10},{10,... | collective-permute-start | bytes 393224 | tf_op jit(solution)/shard_map/ppermute | solution.py:253
  19.8 1.0 %shard_map.68 = (f32[512,512]{1,0:T(8,128)S(1)}, bf16[1024,512]{1,0:T(8,128)(2,1)S(1)}, f32[288,512]{1,0:T(8,128)S(1)}, f32[64,512]{1,0:T(8,128)S(1)}, f32[8,512]{1,0:T(8,128)S(1)}) custom-call(bf16[64,192]{1,0:T(8,128)(2,1)S(1)} %get-tuple-element.71.refs_0_, bf16[192,512]{1,0:T(8,128)(2,1)S(1)} %get-tuple-element.72.refs_1_, ...), custom_call_target="tpu_custom_call" | custom-call | flops 503316480 | tf_op jit(solution)/shard_map/pallas_call | solution.py:22
  21.5 1.8 %collective-permute-done.4.refs_1_ = f32[64,512]{1,0:T(8,128)S(1)} collective-permute-done((f32[64,512]{1,0:T(8,128)S(1)}, f32[64,512]{1,0:T(8,128)S(1)}, u32[]{:S(2)}, u32[]{:S(2)}) %collective-permute-start.4) | collective-permute-done | bytes 131104 | tf_op jit(solution)/shard_map/ppermute | solution.py:253
  23.8 1.6 %collective-permute-start.6 = (f32[64,512]{1,0:T(8,128)S(1)}, f32[64,512]{1,0:T(8,128)S(1)}, u32[]{:S(2)}, u32[]{:S(2)}) collective-permute-start(f32[64,512]{1,0:T(8,128)S(1)} %shard_map.73), channel_id=1, source_target_pairs={{0,16},{1,2},{2,1},{3,4},{4,3},{5,6},{6,5},{7,8},{8,7},{9,10},{10,... | collective-permute-start | bytes 393224 | tf_op jit(solution)/shard_map/ppermute | solution.py:253
  27.1 1.8 %collective-permute-done.6.refs_1_ = f32[64,512]{1,0:T(8,128)S(1)} collective-permute-done((f32[64,512]{1,0:T(8,128)S(1)}, f32[64,512]{1,0:T(8,128)S(1)}, u32[]{:S(2)}, u32[]{:S(2)}) %collective-permute-start.6) | collective-permute-done | bytes 131104 | tf_op jit(solution)/shard_map/ppermute | solution.py:253
  30.1 1.6 %collective-permute-start.8 = (f32[64,512]{1,0:T(8,128)S(1)}, f32[64,512]{1,0:T(8,128)S(1)}, u32[]{:S(2)}, u32[]{:S(2)}) collective-permute-start(f32[64,512]{1,0:T(8,128)S(1)} %shard_map.77), channel_id=1, source_target_pairs={{0,16},{1,2},{2,1},{3,4},{4,3},{5,6},{6,5},{7,8},{8,7},{9,10},{10,... | collective-permute-start | bytes 393224 | tf_op jit(solution)/shard_map/ppermute | solution.py:253
  33.3 1.8 %collective-permute-done.8.refs_1_ = f32[64,512]{1,0:T(8,128)S(1)} collective-permute-done((f32[64,512]{1,0:T(8,128)S(1)}, f32[64,512]{1,0:T(8,128)S(1)}, u32[]{:S(2)}, u32[]{:S(2)}) %collective-permute-start.8) | collective-permute-done | bytes 131104 | tf_op jit(solution)/shard_map/ppermute | solution.py:253
  36.4 1.6 %collective-permute-start.10 = (f32[64,512]{1,0:T(8,128)S(1)}, f32[64,512]{1,0:T(8,128)S(1)}, u32[]{:S(2)}, u32[]{:S(2)}) collective-permute-start(f32[64,512]{1,0:T(8,128)S(1)} %shard_map.81), channel_id=1, source_target_pairs={{0,16},{1,2},{2,1},{3,4},{4,3},{5,6},{6,5},{7,8},{8,7},{9,10},{10,... | collective-permute-start | bytes 393224 | tf_op jit(solution)/shard_map/ppermute | solution.py:253
  39.6 1.8 %collective-permute-done.10.refs_1_ = f32[64,512]{1,0:T(8,128)S(1)} collective-permute-done((f32[64,512]{1,0:T(8,128)S(1)}, f32[64,512]{1,0:T(8,128)S(1)}, u32[]{:S(2)}, u32[]{:S(2)}) %collective-permute-start.10) | collective-permute-done | bytes 131104 | tf_op jit(solution)/shard_map/ppermute | solution.py:253
  42.6 1.6 %collective-permute-start.12 = (f32[64,512]{1,0:T(8,128)S(1)}, f32[64,512]{1,0:T(8,128)S(1)}, u32[]{:S(2)}, u32[]{:S(2)}) collective-permute-start(f32[64,512]{1,0:T(8,128)S(1)} %shard_map.85), channel_id=1, source_target_pairs={{0,16},{1,2},{2,1},{3,4},{4,3},{5,6},{6,5},{7,8},{8,7},{9,10},{10,... | collective-permute-start | bytes 393224 | tf_op jit(solution)/shard_map/ppermute | solution.py:253
  45.9 1.8 %collective-permute-done.12.message = f32[64,512]{1,0:T(8,128)S(1)} collective-permute-done((f32[64,512]{1,0:T(8,128)S(1)}, f32[64,512]{1,0:T(8,128)S(1)}, u32[]{:S(2)}, u32[]{:S(2)}) %collective-permute-start.12) | collective-permute-done | bytes 131104 | tf_op jit(solution)/shard_map/ppermute | solution.py:253
  49.7 4.0 %collective-permute-start.17 = (f32[8,512]{1,0:T(8,128)S(1)}, f32[8,512]{1,0:T(8,128)S(1)}, u32[]{:S(2)}, u32[]{:S(2)}) collective-permute-start(f32[8,512]{1,0:T(8,128)S(1)} %add.15), channel_id=1, source_target_pairs={{0,6},{1,7},{2,4},{3,5},{4,2},{5,3},{6,0},{7,1},{8,14},{9,15},{10,... | collective-permute-start | bytes 49160 | tf_op jit(solution)/shard_map/ppermute | solution.py:266
  55.5 1.4 %collective-permute-done.16 = f32[8,512]{1,0:T(8,128)S(1)} collective-permute-done((f32[8,512]{1,0:T(8,128)S(1)}, f32[8,512]{1,0:T(8,128)S(1)}, u32[]{:S(2)}, u32[]{:S(2)}) %collective-permute-start.16) | collective-permute-done | bytes 16416 | tf_op jit(solution)/shard_map/ppermute | solution.py:266
  57.0 2.6 %collective-permute-start.18 = (f32[8,512]{1,0:T(8,128)S(1)}, f32[8,512]{1,0:T(8,128)S(1)}, u32[]{:S(2)}, u32[]{:S(2)}) collective-permute-start(f32[8,512]{1,0:T(8,128)S(1)} %add_add_fusion), channel_id=1, source_target_pairs={{0,9},{1,8},{2,11},{3,10},{4,13},{5,12},{6,15},{7,14},{8,1},{9,0},... | collective-permute-start | bytes 49160 | tf_op jit(solution)/shard_map/ppermute | solution.py:266
  59.7 1.3 %shard_map.88 = f32[512,512]{1,0:T(8,128)} custom-call(bf16[192,512]{1,0:T(8,128)(2,1)S(1)} %get-tuple-element.107.halo, f32[512,512]{1,0:T(8,128)S(1)} %shard_map.86.u, bf16[512,192]{1,0:T(8,128)(2,1)S(1)} %get-tuple-element.61.refs_3_.refs_6_.refs_4_.refs_7_.coupling, f32[512,512]{1,0:T(8,128)S(1)} %get-tuple-element.108.x, ...), custom_call_target="tpu_custom_call" | custom-call | flops 2621440 | tf_op jit(solution)/shard_map/pallas_call | solution.py:22
  (59 shorter events, 20.2 us)
Async XLA Ops:
  0.6 1.2 %copy-start = (f32[512,512]{1,0:T(8,128)S(1)}, f32[512,512]{1,0:T(8,128)}, u32[]{:S(2)}) copy-start(f32[512,512]{1,0:T(8,128)} %side.13) | copy-start | bytes 3145732
  3.2 5.4 %collective-permute-start.1 = (f32[64,512]{1,0:T(8,128)S(1)}, f32[64,512]{1,0:T(8,128)S(1)}, u32[]{:S(2)}, u32[]{:S(2)}) collective-permute-start(f32[64,512]{1,0:T(8,128)S(1)} %shard_map.61), channel_id=1, source_target_pairs={{0,1},{1,0},{2,3},{3,2},{4,5},{5,4},{6,7},{7,6},{8,9},{9,8},{10,11... | collective-permute-start | bytes 393224 | tf_op jit(solution)/shard_map/ppermute | solution.py:257
  3.7 3.8 %copy-start.1 = (f32[512,512]{1,0:T(8,128)S(1)}, f32[512,512]{1,0:T(8,128)}, u32[]{:S(2)}) copy-start(f32[512,512]{1,0:T(8,128)} %side.13) | copy-start | bytes 3145732
  3.8 3.8 %copy-start.3 = (f32[512,512]{1,0:T(8,128)S(1)}, f32[512,512]{1,0:T(8,128)}, u32[]{:S(2)}) copy-start(f32[512,512]{1,0:T(8,128)} %diag.3) | copy-start | bytes 3145732
  3.8 3.8 %copy-start.4 = (f32[512,64]{0,1:T(8,128)S(1)}, f32[512,64]{0,1:T(8,128)}, u32[]{:S(2)}) copy-start(f32[512,64]{0,1:T(8,128)} %param.5) | copy-start | bytes 393220
  3.8 3.8 %copy-start.5 = (f32[512,64]{0,1:T(8,128)S(1)}, f32[512,64]{0,1:T(8,128)}, u32[]{:S(2)}) copy-start(f32[512,64]{0,1:T(8,128)} %param.6) | copy-start | bytes 393220
  5.0 5.6 %collective-permute-start = (f32[64,512]{1,0:T(8,128)S(1)}, f32[64,512]{1,0:T(8,128)S(1)}, u32[]{:S(2)}, u32[]{:S(2)}) collective-permute-start(f32[64,512]{1,0:T(8,128)S(1)} %shard_map.59), channel_id=1, source_target_pairs={{0,16},{1,2},{2,1},{3,4},{4,3},{5,6},{6,5},{7,8},{8,7},{9,10},{10,... | collective-permute-start | bytes 393224 | tf_op jit(solution)/shard_map/ppermute | solution.py:253
  10.7 3.4 %collective-permute-start.3 = (f32[64,512]{1,0:T(8,128)S(1)}, f32[64,512]{1,0:T(8,128)S(1)}, u32[]{:S(2)}, u32[]{:S(2)}) collective-permute-start(f32[64,512]{1,0:T(8,128)S(1)} %get-tuple-element.68), channel_id=1, source_target_pairs={{0,1},{1,0},{2,3},{3,2},{4,5},{5,4},{6,7},{7,6},{8,9},{9,8},{10,11... | collective-permute-start | bytes 393224 | tf_op jit(solution)/shard_map/ppermute | solution.py:257
  11.0 5.2 %collective-permute-start.2 = (f32[72,512]{1,0:T(8,128)S(1)}, f32[72,512]{1,0:T(8,128)S(1)}, u32[]{:S(2)}, u32[]{:S(2)}) collective-permute-start(f32[72,512]{1,0:T(8,128)S(1)} %shard_map.65), channel_id=1, source_target_pairs={{0,16},{1,2},{2,1},{3,4},{4,3},{5,6},{6,5},{7,8},{8,7},{9,10},{10,... | collective-permute-start | bytes 442376 | tf_op jit(solution)/shard_map/ppermute | solution.py:253
  16.7 4.1 %collective-permute-start.5 = (f32[64,512]{1,0:T(8,128)S(1)}, f32[64,512]{1,0:T(8,128)S(1)}, u32[]{:S(2)}, u32[]{:S(2)}) collective-permute-start(f32[64,512]{1,0:T(8,128)S(1)} %get-tuple-element.76), channel_id=1, source_target_pairs={{0,1},{1,0},{2,3},{3,2},{4,5},{5,4},{6,7},{7,6},{8,9},{9,8},{10,11... | collective-permute-start | bytes 393224 | tf_op jit(solution)/shard_map/ppermute | solution.py:257
  18.2 5.0 %collective-permute-start.4 = (f32[64,512]{1,0:T(8,128)S(1)}, f32[64,512]{1,0:T(8,128)S(1)}, u32[]{:S(2)}, u32[]{:S(2)}) collective-permute-start(f32[64,512]{1,0:T(8,128)S(1)} %shard_map.69), channel_id=1, source_target_pairs={{0,16},{1,2},{2,1},{3,4},{4,3},{5,6},{6,5},{7,8},{8,7},{9,10},{10,... | collective-permute-start | bytes 393224 | tf_op jit(solution)/shard_map/ppermute | solution.py:253
  23.4 3.0 %collective-permute-start.7 = (f32[64,512]{1,0:T(8,128)S(1)}, f32[64,512]{1,0:T(8,128)S(1)}, u32[]{:S(2)}, u32[]{:S(2)}) collective-permute-start(f32[64,512]{1,0:T(8,128)S(1)} %get-tuple-element.83), channel_id=1, source_target_pairs={{0,1},{1,0},{2,3},{3,2},{4,5},{5,4},{6,7},{7,6},{8,9},{9,8},{10,11... | collective-permute-start | bytes 393224 | tf_op jit(solution)/shard_map/ppermute | solution.py:257
  23.8 5.0 %collective-permute-start.6 = (f32[64,512]{1,0:T(8,128)S(1)}, f32[64,512]{1,0:T(8,128)S(1)}, u32[]{:S(2)}, u32[]{:S(2)}) collective-permute-start(f32[64,512]{1,0:T(8,128)S(1)} %shard_map.73), channel_id=1, source_target_pairs={{0,16},{1,2},{2,1},{3,4},{4,3},{5,6},{6,5},{7,8},{8,7},{9,10},{10,... | collective-permute-start | bytes 393224 | tf_op jit(solution)/shard_map/ppermute | solution.py:253
  29.0 3.6 %collective-permute-start.9 = (f32[64,512]{1,0:T(8,128)S(1)}, f32[64,512]{1,0:T(8,128)S(1)}, u32[]{:S(2)}, u32[]{:S(2)}) collective-permute-start(f32[64,512]{1,0:T(8,128)S(1)} %get-tuple-element.90), channel_id=1, source_target_pairs={{0,1},{1,0},{2,3},{3,2},{4,5},{5,4},{6,7},{7,6},{8,9},{9,8},{10,11... | collective-permute-start | bytes 393224 | tf_op jit(solution)/shard_map/ppermute | solution.py:257
  30.1 5.0 %collective-permute-start.8 = (f32[64,512]{1,0:T(8,128)S(1)}, f32[64,512]{1,0:T(8,128)S(1)}, u32[]{:S(2)}, u32[]{:S(2)}) collective-permute-start(f32[64,512]{1,0:T(8,128)S(1)} %shard_map.77), channel_id=1, source_target_pairs={{0,16},{1,2},{2,1},{3,4},{4,3},{5,6},{6,5},{7,8},{8,7},{9,10},{10,... | collective-permute-start | bytes 393224 | tf_op jit(solution)/shard_map/ppermute | solution.py:253
  35.3 3.7 %collective-permute-start.11 = (f32[64,512]{1,0:T(8,128)S(1)}, f32[64,512]{1,0:T(8,128)S(1)}, u32[]{:S(2)}, u32[]{:S(2)}) collective-permute-start(f32[64,512]{1,0:T(8,128)S(1)} %get-tuple-element.97), channel_id=1, source_target_pairs={{0,1},{1,0},{2,3},{3,2},{4,5},{5,4},{6,7},{7,6},{8,9},{9,8},{10,11... | collective-permute-start | bytes 393224 | tf_op jit(solution)/shard_map/ppermute | solution.py:257
  36.4 5.0 %collective-permute-start.10 = (f32[64,512]{1,0:T(8,128)S(1)}, f32[64,512]{1,0:T(8,128)S(1)}, u32[]{:S(2)}, u32[]{:S(2)}) collective-permute-start(f32[64,512]{1,0:T(8,128)S(1)} %shard_map.81), channel_id=1, source_target_pairs={{0,16},{1,2},{2,1},{3,4},{4,3},{5,6},{6,5},{7,8},{8,7},{9,10},{10,... | collective-permute-start | bytes 393224 | tf_op jit(solution)/shard_map/ppermute | solution.py:253
  41.6 3.6 %collective-permute-start.13 = (f32[64,512]{1,0:T(8,128)S(1)}, f32[64,512]{1,0:T(8,128)S(1)}, u32[]{:S(2)}, u32[]{:S(2)}) collective-permute-start(f32[64,512]{1,0:T(8,128)S(1)} %get-tuple-element.103), channel_id=1, source_target_pairs={{0,1},{1,0},{2,3},{3,2},{4,5},{5,4},{6,7},{7,6},{8,9},{9,8},{10,11... | collective-permute-start | bytes 393224 | tf_op jit(solution)/shard_map/ppermute | solution.py:257
  42.6 5.0 %collective-permute-start.12 = (f32[64,512]{1,0:T(8,128)S(1)}, f32[64,512]{1,0:T(8,128)S(1)}, u32[]{:S(2)}, u32[]{:S(2)}) collective-permute-start(f32[64,512]{1,0:T(8,128)S(1)} %shard_map.85), channel_id=1, source_target_pairs={{0,16},{1,2},{2,1},{3,4},{4,3},{5,6},{6,5},{7,8},{8,7},{9,10},{10,... | collective-permute-start | bytes 393224 | tf_op jit(solution)/shard_map/ppermute | solution.py:253
  48.0 1.8 %collective-permute-start.14 = (f32[8,512]{1,0:T(8,128)S(1)}, f32[8,512]{1,0:T(8,128)S(1)}, u32[]{:S(2)}, u32[]{:S(2)}) collective-permute-start(f32[8,512]{1,0:T(8,128)S(1)} %get-tuple-element.109), channel_id=1, source_target_pairs={{0,1},{1,0},{2,3},{3,2},{4,5},{5,4},{6,7},{7,6},{8,9},{9,8},{10,11... | collective-permute-start | bytes 49160 | tf_op jit(solution)/shard_map/ppermute | solution.py:266
  49.7 5.7 %collective-permute-start.17 = (f32[8,512]{1,0:T(8,128)S(1)}, f32[8,512]{1,0:T(8,128)S(1)}, u32[]{:S(2)}, u32[]{:S(2)}) collective-permute-start(f32[8,512]{1,0:T(8,128)S(1)} %add.15), channel_id=1, source_target_pairs={{0,6},{1,7},{2,4},{3,5},{4,2},{5,3},{6,0},{7,1},{8,14},{9,15},{10,... | collective-permute-start | bytes 49160 | tf_op jit(solution)/shard_map/ppermute | solution.py:266
  53.7 3.2 %collective-permute-start.16 = (f32[8,512]{1,0:T(8,128)S(1)}, f32[8,512]{1,0:T(8,128)S(1)}, u32[]{:S(2)}, u32[]{:S(2)}) collective-permute-start(f32[8,512]{1,0:T(8,128)S(1)} %add.15), channel_id=1, source_target_pairs={{0,5},{1,4},{2,7},{3,6},{4,1},{5,0},{6,3},{7,2},{8,13},{9,12},{10,... | collective-permute-start | bytes 49160 | tf_op jit(solution)/shard_map/ppermute | solution.py:266
  53.9 3.2 %collective-permute-start.15 = (f32[8,512]{1,0:T(8,128)S(1)}, f32[8,512]{1,0:T(8,128)S(1)}, u32[]{:S(2)}, u32[]{:S(2)}) collective-permute-start(f32[8,512]{1,0:T(8,128)S(1)} %add.15), channel_id=1, source_target_pairs={{0,3},{1,2},{2,1},{3,0},{4,7},{5,6},{6,5},{7,4},{8,11},{9,10},{10,... | collective-permute-start | bytes 49160 | tf_op jit(solution)/shard_map/ppermute | solution.py:266
  57.0 4.1 %collective-permute-start.18 = (f32[8,512]{1,0:T(8,128)S(1)}, f32[8,512]{1,0:T(8,128)S(1)}, u32[]{:S(2)}, u32[]{:S(2)}) collective-permute-start(f32[8,512]{1,0:T(8,128)S(1)} %add_add_fusion), channel_id=1, source_target_pairs={{0,9},{1,8},{2,11},{3,10},{4,13},{5,12},{6,15},{7,14},{8,1},{9,0},... | collective-permute-start | bytes 49160 | tf_op jit(solution)/shard_map/ppermute | solution.py:266
  (1 other events, 1.2 us)
